TPU v7x, 32 devices: a whole 2x2x4 slice. The times are simulated.
32 devices in a mesh: gz: 2 (over core), dp: 16 (over z, y, x).
Axes of the slice: x: 2, y: 2, z: 4, core: 2. Of those that a mesh axis runs over, the one named last changes fastest.
Arguments:
- inputs: bfloat16 [16, 32, 16, 8, 128], P('dp', None, 'gz'), may hold values from -6 to 6
- kernel_one: bfloat16 [32, 32, 3, 3, 3], replicated, may hold values from -0.21875 to 0.21875
- kernel_two: bfloat16 [32, 32, 3, 3, 3], replicated, may hold values from -0.21875 to 0.21875
- cotangent: bfloat16 [16, 32, 16, 8, 128], P('dp', None, 'gz'), may hold values from -12 to 12
Outputs:
- input_grad: bfloat16 [16, 32, 16, 8, 128], P('dp', None, 'gz')
- kernel_one_grad: float32 [32, 32, 3, 3, 3], replicated
- kernel_two_grad: float32 [32, 32, 3, 3, 3], replicated
All inputs are finite; a program needn't handle non-finite values.
Results may differ from a plain program's by a relative error of at most 0.006.
Values may be sent and summed in bfloat16 or wider, within the bound.
No kernel may reach another device: no remote copies, remote signals or barrier semaphores. Data moves between devices by JAX's collectives and lax.ppermute only.
A program may use at most 64 MiB of HBM per device.

v0:
```python
import math

import jax
import jax.numpy as jnp
from jax import lax
from jax.sharding import PartitionSpec as P


def extended(value, sides, width):
    for axis, dim in sides:
        count, length = (lax.axis_size(axis), value.shape[dim])
        up = [(i, (i + 1) % count) for i in range(count - 1)]
        down = [(j, i) for i, j in up]
        last = lax.slice_in_dim(value, length - width, length, axis=dim)
        initial = lax.slice_in_dim(value, 0, width, axis=dim)
        before = lax.ppermute(last, axis, up)
        after = lax.ppermute(initial, axis, down)
        value = jnp.concatenate([before, value, after], axis=dim)
    return value


def column_stack(field):
    padded = jnp.pad(field, ((0, 0), (0, 0), (1, 1), (1, 1)))
    width = field.shape[3]
    return jnp.stack([padded[..., col_off : col_off + width] for col_off in range(3)])


def convolve_valid(field, kernel):
    stacked = column_stack(field)
    planes = field.shape[1] - 2
    height = field.shape[2]
    total = None
    for plane_off in range(3):
        for row_off in range(3):
            weights = jnp.moveaxis(kernel[:, :, plane_off, row_off, :], 2, 1)
            window = stacked[:, :, plane_off : plane_off + planes, row_off : row_off + height, :]
            piece = jnp.einsum(
                "oki,kizyx->ozyx", weights, window, preferred_element_type=jnp.float32
            )
            total = piece if total is None else total + piece
    return total


def convolve_all(fields, kernel):
    return jax.vmap(convolve_valid, in_axes=(0, None))(fields, kernel)


def flipped(kernel):
    return jnp.swapaxes(jnp.flip(kernel, (2, 3, 4)), 0, 1)


def kernel_terms(banded, grad):
    stacked = column_stack(banded)
    planes = grad.shape[1]
    height = grad.shape[2]
    outer = []
    for plane_off in range(3):
        inner = []
        for row_off in range(3):
            window = stacked[:, :, plane_off : plane_off + planes, row_off : row_off + height, :]
            inner.append(
                jnp.einsum("ozyx,kizyx->oik", grad, window, preferred_element_type=jnp.float32)
            )
        outer.append(jnp.stack(inner, 2))
    return jnp.stack(outer, 2)


def terms_all(banded, grad):
    return jnp.sum(jax.vmap(kernel_terms)(banded, grad), axis=0)


def dsilu(value):
    sigmoid_val = jax.nn.sigmoid(value)
    return sigmoid_val * (1.0 + value * (1.0 - sigmoid_val))


def local(inputs, kernel_one, kernel_two, cotangent):
    slab_depth = inputs.shape[2]
    source_band = extended(inputs, (("gz", 2),), 1)
    pre_one = convolve_all(source_band, kernel_one)
    hidden = jax.nn.silu(pre_one).astype(jnp.bfloat16)
    hidden_band = extended(hidden, (("gz", 2),), 1)
    pre_two = convolve_all(hidden_band, kernel_two)
    grad_two = (cotangent.astype(jnp.float32) * dsilu(pre_two)).astype(jnp.bfloat16)
    grad_two_band = extended(grad_two, (("gz", 2),), 1)
    hidden_grad = convolve_all(grad_two_band, flipped(kernel_two))
    grad_one = (hidden_grad * dsilu(pre_one)).astype(jnp.bfloat16)
    grad_one_band = extended(grad_one, (("gz", 2),), 1)
    input_grad = convolve_all(grad_one_band, flipped(kernel_one)).astype(jnp.bfloat16)
    term_two = terms_all(hidden_band, grad_two)
    term_one = terms_all(source_band, grad_one)
    total_one, total_two = lax.psum((term_one, term_two), ("gz", "dp"))
    count = (
        lax.axis_size("dp")
        * inputs.shape[0]
        * lax.axis_size("gz")
        * slab_depth
        * inputs.shape[3]
        * inputs.shape[4]
    )
    factor = 1.0 / math.sqrt(count)
    return (input_grad, total_one * factor, total_two * factor)


def solution(mesh):
    return jax.shard_map(
        local,
        mesh=mesh,
        in_specs=(P("dp", None, "gz", None, None), P(), P(), P("dp", None, "gz", None, None)),
        out_specs=(P("dp", None, "gz", None, None), P(), P()),
        check_vma=False,
    )
```

profile of v0, /device:TPU:0, one launch (start us, length us, event | category | flops | bytes accessed | tf_op | source)
XLA Modules:
  0.0 216.6 jit_solution(1600772438256316609)
XLA Ops:
  7.2 1.4 copy.8
  8.7 2.4 %collective-permute-start = (bf16[1,32,1,8,128]{4,1,3,2,0:T(8,128)(2,1)S(1)}, bf16[1,32,1,8,128]{4,1,3,2,0:T(8,128)(2,1)S(1)}, u32[]{:S(2)}, u32[]{:S(2)}) collective-permute-start(bf16[1,32,1,8,128]{4,1,3,2,0:T(8,128)(2,1)S(1)} %get-tuple-element.62), channel_id=1, source_target_pairs={{0,16},{1,17},{2,18},{3,19},{4,20},{5,21},{6,22},{7,23},{8,24},{9,... | collective-permute-start | bytes 196616 | tf_op jit(solution)/shard_map/ppermute | solution.py:16
  11.1 1.3 collective-permute-start.1
  12.4 1.1 copy.22
  14.2 0.9 fusion.26
  19.9 0.8 fusion.107
  21.1 2.5 %collective-permute-start.2 = (bf16[1,32,1,8,128]{4,1,3,2,0:T(8,128)(2,1)S(1)}, bf16[1,32,1,8,128]{4,1,3,2,0:T(8,128)(2,1)S(1)}, u32[]{:S(2)}, u32[]{:S(2)}) collective-permute-start(bf16[1,32,1,8,128]{4,1,3,2,0:T(8,128)(2,1)S(1)} %get-tuple-element.60), channel_id=1, source_target_pairs={{0,16},{1,17},{2,18},{3,19},{4,20},{5,21},{6,22},{7,23},{8,24},{9,... | collective-permute-start | bytes 196616 | tf_op jit(solution)/shard_map/ppermute | solution.py:16
  23.6 1.5 collective-permute-start.3
  25.1 4.3 %slice_bitcast_fusion.35 = (bf16[3,32,8,8,128]{4,1,0,3,2:T(8,128)(2,1)}, bf16[3,32,8,8,128]{4,1,0,3,2:T(8,128)(2,1)S(1)}, bf16[3,32,8,8,128]{4,1,0,3,2:T(8,128)(...) fusion(bf16[3,1,32,10,10,128]{5,2,0,4,3,1:T(8,128)(2,1)S(1)} %p, ...), kind=kLoop, calls=%fused_computation.72 | loop fusion | bytes 28311552 | tf_op jit(solution)/shard_map/reshape
  29.4 0.9 fusion.24
  31.3 3.5 %slice_bitcast_fusion.26 = (bf16[3,32,8,8,128]{4,1,3,2,0:T(8,128)(2,1)S(1)}, bf16[3,32,8,8,128]{4,1,3,2,0:T(8,128)(2,1)S(1)}, bf16[3,32,8,8,128]{4,1,3,2,0:T(8,1...) fusion(bf16[3,1,32,10,10,128]{5,2,4,3,1,0:T(8,128)(2,1)S(1)} %p, ...), kind=kLoop, calls=%fused_computation.63 | loop fusion | bytes 28311552 | tf_op jit(solution)/shard_map/reshape.21
  39.2 1.3 fusion.137
  45.4 3.0 %collective-permute-start.4 = (bf16[1,32,1,8,128]{4,1,3,2,0:T(8,128)(2,1)S(1)}, bf16[1,32,1,8,128]{4,1,3,2,0:T(8,128)(2,1)S(1)}, u32[]{:S(2)}, u32[]{:S(2)}) collective-permute-start(bf16[1,32,1,8,128]{4,1,3,2,0:T(8,128)(2,1)S(1)} %get-tuple-element.58), channel_id=1, source_target_pairs={{0,16},{1,17},{2,18},{3,19},{4,20},{5,21},{6,22},{7,23},{8,24},{9,... | collective-permute-start | bytes 196616 | tf_op jit(solution)/shard_map/ppermute | solution.py:16
  48.4 1.5 collective-permute-start.5
  50.0 0.8 maximum_bitcast_fusion.1
  50.8 0.8 collective-permute-done.5
  51.6 0.9 fusion.22
  53.4 3.5 %slice_bitcast_fusion.17 = (bf16[3,32,8,8,128]{4,1,3,2,0:T(8,128)(2,1)S(1)}, bf16[3,32,8,8,128]{4,1,3,2,0:T(8,128)(2,1)S(1)}, bf16[3,32,8,8,128]{4,1,3,2,0:T(8,1...) fusion(bf16[3,1,32,10,10,128]{5,2,4,3,1,0:T(8,128)(2,1)S(1)} %p, ...), kind=kLoop, calls=%fused_computation.54 | loop fusion | bytes 28311552 | tf_op jit(solution)/shard_map/reshape.39
  60.6 1.3 fusion.136
  62.6 0.8 copy-done.3
  64.7 0.7 copy-done.1
  68.9 2.3 %collective-permute-start.6 = (bf16[1,32,1,8,128]{4,1,3,2,0:T(8,128)(2,1)S(1)}, bf16[1,32,1,8,128]{4,1,3,2,0:T(8,128)(2,1)S(1)}, u32[]{:S(2)}, u32[]{:S(2)}) collective-permute-start(bf16[1,32,1,8,128]{4,1,3,2,0:T(8,128)(2,1)S(1)} %get-tuple-element.56), channel_id=1, source_target_pairs={{0,16},{1,17},{2,18},{3,19},{4,20},{5,21},{6,22},{7,23},{8,24},{9,... | collective-permute-start | bytes 196616 | tf_op jit(solution)/shard_map/ppermute | solution.py:16
  71.2 1.6 collective-permute-start.7
  72.8 0.8 maximum_bitcast_fusion
  74.4 0.9 select_maximum_fusion
  76.2 3.5 %slice_bitcast_fusion.8 = (bf16[3,32,8,8,128]{4,1,3,2,0:T(8,128)(2,1)S(1)}, bf16[3,32,8,8,128]{4,1,3,2,0:T(8,128)(2,1)S(1)}, bf16[3,32,8,8,128]{4,1,3,2,0:T(8,12...) fusion(bf16[3,1,32,10,10,128]{5,2,4,3,1,0:T(8,128)(2,1)S(1)} %p, ...), kind=kLoop, calls=%fused_computation.45 | loop fusion | bytes 28311552 | tf_op jit(solution)/shard_map/reshape.57
  83.5 1.2 fusion.153
  84.6 1.0 copy.78
  85.6 121.0 %all-reduce.7.cloned.1.call-done = (f32[32,32,3,3,3]{0,1,4,3,2:T(8,128)}, f32[32,32,3,3,3]{0,1,4,3,2:T(8,128)}) async-done(((f32[32,32,3,3,3]{0,1,4,3,2:T(8,128)}, f32[32,32,3,3,3]{0,1,4,3,2:T(8,128)}), (f32[32,32,3,3,3]{0,1,4,3,2:T(8,128)}, f32[32,32,3,3,3]{0,1,4,3,2:T(8,128)})) %all-reduce.7.cloned.1.call-update) | async-done | bytes 221200 | tf_op jit(solution)/shard_map/psum | solution.py:92
  206.7 1.1 broadcast_multiply_fusion.1
  207.8 0.9 copy.79
  208.8 0.9 copy.80
  (99 shorter events, 31.2 us)
Async XLA Ops:
  7.2 6.3 %copy-start.5 = (bf16[32,32,3,3,3]{1,0,4,3,2:T(8,128)(2,1)S(1)}, bf16[32,32,3,3,3]{1,0,4,3,2:T(8,128)(2,1)}, u32[]{:S(2)}) copy-start(bf16[32,32,3,3,3]{1,0,4,3,2:T(8,128)(2,1)} %param.5) | copy-start | bytes 165892
  7.2 199.5 %all-reduce.7.cloned.1.call-start = ((), (), s32[]{:S(2)}) async-start(), calls=%async_computation | async-start | bytes 1769472 | tf_op jit(solution)/shard_map/psum | solution.py:92
  8.7 5.0 %collective-permute-start = (bf16[1,32,1,8,128]{4,1,3,2,0:T(8,128)(2,1)S(1)}, bf16[1,32,1,8,128]{4,1,3,2,0:T(8,128)(2,1)S(1)}, u32[]{:S(2)}, u32[]{:S(2)}) collective-permute-start(bf16[1,32,1,8,128]{4,1,3,2,0:T(8,128)(2,1)S(1)} %get-tuple-element.62), channel_id=1, source_target_pairs={{0,16},{1,17},{2,18},{3,19},{4,20},{5,21},{6,22},{7,23},{8,24},{9,... | collective-permute-start | bytes 196616 | tf_op jit(solution)/shard_map/ppermute | solution.py:16
  11.1 3.1 %collective-permute-start.1 = (bf16[1,32,1,8,128]{4,1,3,2,0:T(8,128)(2,1)S(1)}, bf16[1,32,1,8,128]{4,1,3,2,0:T(8,128)(2,1)S(1)}, u32[]{:S(2)}, u32[]{:S(2)}) collective-permute-start(bf16[1,32,1,8,128]{4,1,3,2,0:T(8,128)(2,1)S(1)} %get-tuple-element.63), channel_id=1, source_target_pairs={{16,0},{17,1},{18,2},{19,3},{20,4},{21,5},{22,6},{23,7},{24,8},{25... | collective-permute-start | bytes 196616 | tf_op jit(solution)/shard_map/ppermute | solution.py:17
  21.1 8.4 %collective-permute-start.2 = (bf16[1,32,1,8,128]{4,1,3,2,0:T(8,128)(2,1)S(1)}, bf16[1,32,1,8,128]{4,1,3,2,0:T(8,128)(2,1)S(1)}, u32[]{:S(2)}, u32[]{:S(2)}) collective-permute-start(bf16[1,32,1,8,128]{4,1,3,2,0:T(8,128)(2,1)S(1)} %get-tuple-element.60), channel_id=1, source_target_pairs={{0,16},{1,17},{2,18},{3,19},{4,20},{5,21},{6,22},{7,23},{8,24},{9,... | collective-permute-start | bytes 196616 | tf_op jit(solution)/shard_map/ppermute | solution.py:16
  23.6 5.8 %collective-permute-start.3 = (bf16[1,32,1,8,128]{4,1,3,2,0:T(8,128)(2,1)S(1)}, bf16[1,32,1,8,128]{4,1,3,2,0:T(8,128)(2,1)S(1)}, u32[]{:S(2)}, u32[]{:S(2)}) collective-permute-start(bf16[1,32,1,8,128]{4,1,3,2,0:T(8,128)(2,1)S(1)} %get-tuple-element.61), channel_id=1, source_target_pairs={{16,0},{17,1},{18,2},{19,3},{20,4},{21,5},{22,6},{23,7},{24,8},{25... | collective-permute-start | bytes 196616 | tf_op jit(solution)/shard_map/ppermute | solution.py:17
  31.3 3.6 %copy-start.6 = (bf16[32,32,3,3,3]{1,0,4,3,2:T(8,128)(2,1)S(1)}, bf16[32,32,3,3,3]{1,0,4,3,2:T(8,128)(2,1)}, u32[]{:S(2)}) copy-start(bf16[32,32,3,3,3]{1,0,4,3,2:T(8,128)(2,1)} %param.6) | copy-start | bytes 165892
  38.1 1.0 copy-start.7
  45.4 5.4 %collective-permute-start.4 = (bf16[1,32,1,8,128]{4,1,3,2,0:T(8,128)(2,1)S(1)}, bf16[1,32,1,8,128]{4,1,3,2,0:T(8,128)(2,1)S(1)}, u32[]{:S(2)}, u32[]{:S(2)}) collective-permute-start(bf16[1,32,1,8,128]{4,1,3,2,0:T(8,128)(2,1)S(1)} %get-tuple-element.58), channel_id=1, source_target_pairs={{0,16},{1,17},{2,18},{3,19},{4,20},{5,21},{6,22},{7,23},{8,24},{9,... | collective-permute-start | bytes 196616 | tf_op jit(solution)/shard_map/ppermute | solution.py:16
  48.4 3.1 %collective-permute-start.5 = (bf16[1,32,1,8,128]{4,1,3,2,0:T(8,128)(2,1)S(1)}, bf16[1,32,1,8,128]{4,1,3,2,0:T(8,128)(2,1)S(1)}, u32[]{:S(2)}, u32[]{:S(2)}) collective-permute-start(bf16[1,32,1,8,128]{4,1,3,2,0:T(8,128)(2,1)S(1)} %get-tuple-element.59), channel_id=1, source_target_pairs={{16,0},{17,1},{18,2},{19,3},{20,4},{21,5},{22,6},{23,7},{24,8},{25... | collective-permute-start | bytes 196616 | tf_op jit(solution)/shard_map/ppermute | solution.py:17
  60.6 1.4 copy-start.4
  62.0 1.4 copy-start.3
  62.6 1.5 copy-start.2
  63.9 1.5 copy-start.1
  64.7 1.5 copy-start
  68.9 4.7 %collective-permute-start.6 = (bf16[1,32,1,8,128]{4,1,3,2,0:T(8,128)(2,1)S(1)}, bf16[1,32,1,8,128]{4,1,3,2,0:T(8,128)(2,1)S(1)}, u32[]{:S(2)}, u32[]{:S(2)}) collective-permute-start(bf16[1,32,1,8,128]{4,1,3,2,0:T(8,128)(2,1)S(1)} %get-tuple-element.56), channel_id=1, source_target_pairs={{0,16},{1,17},{2,18},{3,19},{4,20},{5,21},{6,22},{7,23},{8,24},{9,... | collective-permute-start | bytes 196616 | tf_op jit(solution)/shard_map/ppermute | solution.py:16
  71.2 3.1 %collective-permute-start.7 = (bf16[1,32,1,8,128]{4,1,3,2,0:T(8,128)(2,1)S(1)}, bf16[1,32,1,8,128]{4,1,3,2,0:T(8,128)(2,1)S(1)}, u32[]{:S(2)}, u32[]{:S(2)}) collective-permute-start(bf16[1,32,1,8,128]{4,1,3,2,0:T(8,128)(2,1)S(1)} %get-tuple-element.57), channel_id=1, source_target_pairs={{16,0},{17,1},{18,2},{19,3},{20,4},{21,5},{22,6},{23,7},{24,8},{25... | collective-permute-start | bytes 196616 | tf_op jit(solution)/shard_map/ppermute | solution.py:17
  206.7 2.1 copy-start.8
Sparse Core Ops, SparseCore 0:
  73.8 132.8 all-reduce.6
where the time goes:
time: 217 us
  waiting for transfers between devices  123 us (57%)
  local copies, waits for them, and re-layouts  25.8 us (12%)
  matrix products  25.3 us (12%)
  starting transfers between devices  16.1 us (7%)
  between operations  14.6 us (7%)
  other arithmetic  11.7 us (5%)
    psum x1, waiting for transfers between devices, local(): total_one, total_two = lax.psum((term_one, term_two), ('gz', 'dp'))  121 us
    dot_general x36, matrix products, convolve_valid(): jnp.einsum('oki,kizyx->ozyx', weights, window, preferred_element_type=jnp...  15.7 us
    another operation x3, local copies, waits for them, and re-layouts  10.6 us
    ppermute x4, starting transfers between devices, extended(): before = lax.ppermute(last, axis, up)  10.2 us
    dot_general x18, matrix products, kernel_terms(): jnp.einsum('ozyx,kizyx->oik', grad, window, preferred_element_type=jnp.fl...  9.6 us
    unnamed x24, local copies, waits for them, and re-layouts  8.24 us
    ppermute x4, starting transfers between devices, extended(): after = lax.ppermute(initial, axis, down)  5.83 us
  transfers between devices with their start and end apart: 9, of which 4 were waited for; matrix products, arithmetic and copies ran while one was open for 9% of the time, Pallas kernels for 0%

commit v1 on v0

v1 whole, which is shorter than its diff:
```python
import functools
import math

import jax
import jax.numpy as jnp
from jax import lax
from jax.experimental import pallas as pl
from jax.experimental.pallas import tpu as pltpu
from jax.sharding import PartitionSpec as P

F32, BF16 = jnp.float32, jnp.bfloat16
NT = (((1,), (1,)), ((), ()))
REACH = 4


def params(mib):
    return pltpu.CompilerParams(vmem_limit_bytes=mib * 2**20)


def cost(flops, size):
    return pl.CostEstimate(flops=int(flops), bytes_accessed=int(size), transcendentals=0)


def prep_kernel(mirrored, one_ref, two_ref, *refs):
    flip = lax.axis_index("gz") == 1 if mirrored else False
    outs, wide = refs[:4], refs[4]
    chan = one_ref.shape[-1]
    full = outs[0].shape[1]
    height = full // chan
    lane = lax.broadcasted_iota(jnp.int32, (chan, full), 1)
    row = lax.broadcasted_iota(jnp.int32, (chan, full), 0)
    repeat = jnp.where(lax.rem(lane, chan) == row, 1.0, 0.0).astype(BF16)
    block = lane // chan
    for index, ref in enumerate((one_ref, two_ref)):
        forward, backward = outs[2 * index], outs[2 * index + 1]
        flat = ref[...].reshape(27 * chan, chan)
        spread = jnp.dot(flat, repeat, preferred_element_type=F32)
        wide[...] = spread.reshape(3, 9 * chan, full)
        for dz in range(3):
            source = jnp.where(flip, 2 - dz, dz) if mirrored else dz
            for dx in range(3):
                taps = [
                    wide[source, (dy * 3 + dx) * chan : (dy * 3 + dx + 1) * chan, :]
                    for dy in range(3)
                ]
                strips = []
                for y in range(height):
                    strip = jnp.zeros((chan, full), F32)
                    for dy in range(3):
                        strip = jnp.where(block == y + dy - 1, taps[dy], strip)
                    strips.append(strip.astype(BF16))
                tile = jnp.concatenate(strips, axis=0)
                forward[dz, :, dx * full : (dx + 1) * full] = tile
                backward[2 - dz, :, (2 - dx) * full : (3 - dx) * full] = tile.T


class Field:
    def __init__(self, ref, base, full, width):
        self.ref, self.base, self.full, self.width = ref, base, full, width

    def lanes(self, first, count):
        start = (first + self.base) * self.width
        return slice(start, start + count * self.width)

    def put(self, plane, value):
        full, width = self.full, self.width
        lane = lax.broadcasted_iota(jnp.int32, (full, width), 1)
        before = jnp.where(lane == 0, 0.0, pltpu.roll(value, 1, 1))
        after = jnp.where(lane == width - 1, 0.0, pltpu.roll(value, width - 1, 1))
        for dx, item in enumerate((before, value, after)):
            self.ref[dx * full : (dx + 1) * full, self.lanes(plane, 1)] = item.astype(BF16)

    def blank(self, plane):
        self.ref[:, self.lanes(plane, 1)] = jnp.zeros((3 * self.full, self.width), BF16)

    def convolve(self, band, first, count):
        total = None
        for dz in range(3):
            piece = jnp.dot(
                band[dz], self.ref[:, self.lanes(first + dz - 1, count)], preferred_element_type=F32
            )
            total = piece if total is None else total + piece
        return total


def spans(low, high):
    return [(at, min(2, high - at)) for at in range(low, high, 2)]


def sigmoid(value):
    return 0.5 * jnp.tanh(0.5 * value) + 0.5


def gradient(field, own, grad_ref, out_ref, planes, chan, flip):
    full, width = field.full, field.width
    height = full // chan
    whole = own + 2
    total = jnp.zeros(out_ref.shape, F32)
    lanes = field.lanes(-1, whole)
    for y in range(height):
        parts = []
        for dz in range(3):
            if flip is None:
                start = (2 - dz) * width
            else:
                start = pl.multiple_of(jnp.where(flip, dz, 2 - dz) * width, width)
            parts.append(grad_ref[y * chan : (y + 1) * chan, pl.ds(start, whole * width)])
        right = jnp.concatenate(parts, axis=0)
        low, high = max(y - 1, 0), min(y + 2, height)
        left = jnp.concatenate(
            [
                field.ref[dx * full + low * chan : dx * full + high * chan, lanes]
                for dx in range(3)
            ],
            axis=0,
        )
        piece = lax.dot_general(left, right, NT, preferred_element_type=F32)
        rows = (high - low) * chan
        if high - low < 3:
            blank = jnp.zeros(((3 - high + low) * chan, piece.shape[1]), F32)
            cut = [piece[dx * rows : (dx + 1) * rows] for dx in range(3)]
            order = [[blank, c] if y == 0 else [c, blank] for c in cut]
            piece = jnp.concatenate([p for pair in order for p in pair], axis=0)
        total = total + piece
    out_ref[...] = total


def main_kernel(count, sizes, *refs):
    chan, own, height, width, low_side, high_side = sizes
    full = chan * height
    mirrored = count == 2
    halos = low_side + high_side
    data_ref, cot_ref = refs[:2]
    halo_refs = refs[2 : 2 + halos]
    band_one, band_two, back_two = refs[2 + halos : 5 + halos]
    grad_field_ref, term_one, term_two = refs[5 + halos : 8 + halos]
    x_ref, h_ref, g_ref, own_ref, slope_ref, turn_ref = refs[8 + halos :]
    position = lax.axis_index("gz")
    flip = position == 1 if mirrored else None

    def reach(depth):
        return (-depth * low_side, own + depth * high_side)

    def field(ref, depth):
        item = Field(ref, depth if low_side else 1, full, width)
        if not low_side:
            item.blank(-1)
        if not high_side:
            item.blank(own)
        return item

    def turned(slot, value):
        turn_ref[slot] = value.astype(F32).reshape(full, width)
        return jnp.concatenate(
            [turn_ref[slot, pl.ds(y, chan, stride=height), :] for y in range(height)], axis=0
        )

    def plane_of(ref, plane, skip, depth):
        if 0 <= plane < own:
            at = jnp.where(flip, own - 1 - plane, plane) if mirrored else plane
            return ref[:, at]
        if plane < 0:
            return halo_refs[0][:, skip + depth + plane]
        at = plane - own
        if mirrored:
            at = jnp.where(flip, depth - 1 - at, at)
        return halo_refs[-1][:, skip + at]

    def kept(plane, value):
        if count == 2:
            return value
        if plane < 0:
            return jnp.where(position > 0, value, 0.0)
        if plane >= own:
            return jnp.where(position < count - 1, value, 0.0)
        return value

    data = field(x_ref, REACH)
    for plane in range(*reach(REACH)):
        data.put(plane, turned(plane % 2, plane_of(data_ref, plane, 0, REACH)))

    hidden = field(h_ref, REACH - 1)
    slope_low, slope_high = reach(1)
    for first, number in spans(*reach(REACH - 1)):
        pre = data.convolve(band_one, first, number)
        for step in range(number):
            plane = first + step
            value = pre[:, step * width : (step + 1) * width]
            gate = sigmoid(value)
            hidden.put(plane, kept(plane, value * gate))
            if slope_low <= plane < slope_high:
                at = (plane - slope_low) * width
                slope_ref[:, at : at + width] = gate * (1.0 + value * (1.0 - gate))

    own_ref[:, : 2 * width] = jnp.zeros((full, 2 * width), BF16)
    own_ref[:, (own + 2) * width :] = jnp.zeros((full, 2 * width), BF16)

    upper = field(g_ref, REACH - 2)
    for first, number in spans(*reach(REACH - 2)):
        pre = hidden.convolve(band_two, first, number)
        for step in range(number):
            plane = first + step
            value = pre[:, step * width : (step + 1) * width]
            gate = sigmoid(value)
            seed = turned(plane % 2, plane_of(cot_ref, plane, REACH, REACH - 2))
            grad = seed * (gate * (1.0 + value * (1.0 - gate)))
            upper.put(plane, grad)
            if 0 <= plane < own:
                own_ref[:, (plane + 2) * width : (plane + 3) * width] = grad.astype(BF16)
    gradient(hidden, own, own_ref, term_two, None, chan, flip)

    lower = field(grad_field_ref, REACH - 3)
    for first, number in spans(*reach(REACH - 3)):
        back = upper.convolve(back_two, first, number)
        for step in range(number):
            plane = first + step
            at = (plane - slope_low) * width
            grad = back[:, step * width : (step + 1) * width] * slope_ref[:, at : at + width]
            grad = kept(plane, grad)
            lower.put(plane, grad)
            if 0 <= plane < own:
                own_ref[:, (plane + 2) * width : (plane + 3) * width] = grad.astype(BF16)
    gradient(data, own, own_ref, term_one, None, chan, flip)


def last_kernel(count, sizes, grad_field_ref, back_one, out_ref, turn_ref):
    chan, own, height, width, _, _ = sizes
    full = chan * height
    mirrored = count == 2
    flip = lax.axis_index("gz") == 1 if mirrored else None
    lower = Field(grad_field_ref, 1, full, width)
    for first, number in spans(0, own):
        out = lower.convolve(back_one, first, number)
        for step in range(number):
            plane = first + step
            value = out[:, step * width : (step + 1) * width]
            slot = plane % 2
            for y in range(height):
                turn_ref[slot, pl.ds(y, chan, stride=height), :] = value[y * chan : (y + 1) * chan]
            at = jnp.where(flip, own - 1 - plane, plane) if mirrored else plane
            out_ref[:, at] = turn_ref[slot].reshape(chan, height, width).astype(BF16)


def unpack_kernel(factor, one_ref, two_ref, out_one, out_two):
    chan = out_one.shape[-1]
    for ref, out in ((one_ref, out_one), (two_ref, out_two)):
        value = ref[...].T * factor
        for dz in range(3):
            for dy in range(3):
                for dx in range(3):
                    at = (dx * 3 + dy) * chan
                    out[dz, dy, dx] = value[dz * chan : (dz + 1) * chan, at : at + chan]


def doubled(value, axis):
    count = lax.axis_size(axis)
    if count & (count - 1):
        return lax.psum(value, axis)
    step = 1
    while step < count:
        value = value + lax.ppermute(value, axis, [(i, i ^ step) for i in range(count)])
        step *= 2
    return value


def reduced(one, two):
    if lax.axis_size("gz") == 2:
        swap = [(0, 1), (1, 0)]
        first = lax.axis_index("gz") == 0
        mine = jnp.where(first, two, one)
        mine = mine + lax.ppermute(jnp.where(first, one, two), "gz", swap)
        mine = doubled(mine, "dp")
        other = lax.ppermute(mine, "gz", swap)
        return jnp.where(first, other, mine), jnp.where(first, mine, other)
    both = doubled(doubled(jnp.stack([one, two]), "gz"), "dp")
    return both[0], both[1]


def halo_of(data, cot, count):
    own = data.shape[1]

    def ends(low):
        parts = []
        for value, depth in ((data, REACH), (cot, REACH - 2)):
            start = jnp.where(low, 0, own - depth) if count == 2 else (0 if low else own - depth)
            parts.append(lax.dynamic_slice_in_dim(value, start, depth, axis=1))
        return jnp.concatenate(parts, axis=1)

    if count == 1:
        return []
    if count == 2:
        return [lax.ppermute(ends(lax.axis_index("gz") == 1), "gz", [(0, 1), (1, 0)])]
    up = [(i, i + 1) for i in range(count - 1)]
    down = [(j, i) for i, j in up]
    return [lax.ppermute(ends(False), "gz", up), lax.ppermute(ends(True), "gz", down)]


def local(inputs, kernel_one, kernel_two, cotangent):
    count = lax.axis_size("gz")
    batch, chan, own, height, width = inputs.shape
    full = chan * height
    low_side, high_side = (1, 1) if count > 2 else (0, 1 if count == 2 else 0)
    sizes = (chan, own, height, width, low_side, high_side)
    sides = low_side + high_side
    taps = [jnp.transpose(k, (2, 3, 4, 0, 1)) for k in (kernel_one, kernel_two)]
    bands = pl.pallas_call(
        functools.partial(prep_kernel, count == 2),
        out_shape=[jax.ShapeDtypeStruct((3, full, 3 * full), BF16)] * 4,
        scratch_shapes=[pltpu.VMEM((3, 9 * chan, full), F32)],
        compiler_params=params(16),
        cost_estimate=cost(2e9, 5e6),
        name="prep",
    )(*taps)

    def slots(depth):
        return own + sum(depth if side else 1 for side in (low_side, high_side))

    def stack(depth):
        return (3 * full, slots(depth) * width)

    outs, ones, twos = [], [], []
    for sample in range(batch):
        data, cot = inputs[sample], cotangent[sample]
        halos = halo_of(data, cot, count)
        term = jax.ShapeDtypeStruct((9 * chan, 3 * chan), F32)
        grad_field, term_one, term_two = pl.pallas_call(
            functools.partial(main_kernel, count, sizes),
            out_shape=[jax.ShapeDtypeStruct(stack(REACH - 3), BF16), term, term],
            scratch_shapes=[
                pltpu.VMEM(stack(REACH), BF16),
                pltpu.VMEM(stack(REACH - 1), BF16),
                pltpu.VMEM(stack(REACH - 2), BF16),
                pltpu.VMEM((full, (own + 4) * width), BF16),
                pltpu.VMEM((full, (own + sides) * width), F32),
                pltpu.VMEM((2, full, width), F32),
            ],
            compiler_params=params(32),
            cost_estimate=cost(8e9, 8e6),
            name="main",
        )(data, cot, *halos, bands[0], bands[2], bands[3])
        out = pl.pallas_call(
            functools.partial(last_kernel, count, sizes),
            out_shape=jax.ShapeDtypeStruct((chan, own, height, width), BF16),
            scratch_shapes=[pltpu.VMEM((2, full, width), F32)],
            compiler_params=params(16),
            cost_estimate=cost(2e9, 3e6),
            name="last",
        )(grad_field, bands[1])
        outs.append(out)
        ones.append(term_one)
        twos.append(term_two)
    one, two = reduced(sum(ones[1:], ones[0]), sum(twos[1:], twos[0]))
    cells = lax.axis_size("dp") * batch * count * own * height * width
    grads = pl.pallas_call(
        functools.partial(unpack_kernel, 1.0 / math.sqrt(cells)),
        out_shape=[jax.ShapeDtypeStruct((3, 3, 3, chan, chan), F32)] * 2,
        compiler_params=params(8),
        name="unpack",
    )(one, two)
    one, two = [jnp.transpose(g, (3, 4, 0, 1, 2)) for g in grads]
    return jnp.stack(outs), one, two


def solution(mesh):
    return jax.shard_map(
        local,
        mesh=mesh,
        in_specs=(P("dp", None, "gz", None, None), P(), P(), P("dp", None, "gz", None, None)),
        out_specs=(P("dp", None, "gz", None, None), P(), P()),
        check_vma=False,
    )
```

time: 217 us -> 46.7 us (0.22)
  waiting for transfers between devices: 123 us -> 17 us
  matrix products: 25.3 us -> 0 us
  local copies, waits for them, and re-layouts: 25.8 us -> 1.98 us
  Pallas kernels: 0 us -> 16 us
  between operations: 14.6 us -> 0.74 us
  other arithmetic: 11.7 us -> 0.17 us
  starting transfers between devices: 16.1 us -> 10.7 us
    psum x1 -> x0, waiting for transfers between devices: 121 us -> none  [local(): total_one, total_two = lax.psum((term_one, term_two), ('gz', 'dp'))]
    dot_general x54 -> x0, matrix products: 25.3 us -> none  [the longest x36 15.7 us: convolve_valid(): jnp.einsum('oki,kizyx->ozyx', weights, window, preferred_element_type=jnp...]
    pallas_call x0 -> x4, Pallas kernels: none -> 16 us  [the longest x1 11.2 us: local(): pl.pallas_call(functools.partial(main_kernel, count, sizes), out_shape=[j...]
    ppermute x8 -> x7, waiting for transfers between devices: 2 us -> 17 us  [the longest x4 15.9 us: doubled(): lax.ppermute(value, axis, [(i, i ^ step) for i in range(count)])]
    another operation x7 -> x0, local copies, waits for them, and re-layouts: 13.1 us -> none
    unnamed x24 -> x8, local copies, waits for them, and re-layouts: 8.24 us -> 0.02 us
    ppermute x8 -> x7, starting transfers between devices: 16 us -> 10.7 us  [the longest x4 9.63 us: doubled(): lax.ppermute(value, axis, [(i, i ^ step) for i in range(count)])]
    reshape x1 -> x0, local copies, waits for them, and re-layouts: 4.33 us -> none
  transfers between devices with their start and end apart: 9 -> 7, of which waited for: 4 -> 6; matrix products, arithmetic and copies ran while one was open for 9% -> 0% of each run, Pallas kernels for 0% -> 8%
where the time goes in v1:
time: 46.7 us; the launch traced here: 46.5 us
  waiting for transfers between devices  17 us (36%)
  Pallas kernels  16 us (34%)
  starting transfers between devices  10.7 us (23%)
  local copies, waits for them, and re-layouts  1.98 us (4%)
  between operations  0.74 us (2%)
    ppermute x4, waiting for transfers between devices, doubled(): lax.ppermute(value, axis, [(i, i ^ step) for i in range(count)])  15.9 us
    pallas_call x1, Pallas kernels, local(): pl.pallas_call(functools.partial(main_kernel, count, sizes), out_shape=[j...  11.2 us
    ppermute x4, starting transfers between devices, doubled(): lax.ppermute(value, axis, [(i, i ^ step) for i in range(count)])  9.63 us
    pallas_call x1, Pallas kernels, local(): pl.pallas_call(functools.partial(last_kernel, count, sizes), out_shape=ja...  2.36 us
    dynamic_slice x2, local copies, waits for them, and re-layouts, ends(): parts.append(lax.dynamic_slice_in_dim(value, start, depth, axis=1))  1.96 us
    pallas_call x1, Pallas kernels, local(): pl.pallas_call(functools.partial(prep_kernel, count == 2), out_shape=[jax...  1.27 us
    pallas_call x1, Pallas kernels, local(): pl.pallas_call(functools.partial(unpack_kernel, 1.0 / math.sqrt(cells)),...  1.17 us
    ppermute x1, waiting for transfers between devices, reduced(): mine = mine + lax.ppermute(jnp.where(first, one, two), 'gz', swap)  1.01 us
  transfers between devices with their start and end apart: 7, of which 6 were waited for; matrix products, arithmetic and copies ran while one was open for 0% of the time, Pallas kernels for 8%

profile of v1, /device:TPU:0, one launch (start us, length us, event | category | flops | bytes accessed | tf_op | source)
XLA Modules:
  0.0 46.5 jit_solution(9110312748748236015)
XLA Ops:
  0.6 0.0 copy-start.3
  0.6 0.0 copy-start.2
  0.7 1.0 %dynamic-slice_bitcast_fusion.1 = bf16[32,2,8,128]{3,2,1,0:T(8,128)(2,1)S(1)} fusion(bf16[1,32,8,8,128]{4,3,2,1,0:T(8,128)(2,1)} %param.7, s32[]{:T(128)S(6)} %select_n.30), kind=kLoop, calls=%fused_computation.3 | loop fusion | bytes 262148 | tf_op jit(solution)/shard_map/dynamic_slice | solution.py:286
  1.6 1.0 %dynamic-slice_bitcast_fusion = bf16[32,4,8,128]{3,2,1,0:T(8,128)(2,1)S(1)} fusion(bf16[1,32,8,8,128]{4,3,2,1,0:T(8,128)(2,1)} %param.4, s32[]{:T(128)S(6)} %select_n.29), kind=kLoop, calls=%fused_computation.1 | loop fusion | bytes 524292 | tf_op jit(solution)/shard_map/dynamic_slice | solution.py:286
  2.7 0.6 %collective-permute-start = (bf16[32,6,8,128]{3,2,1,0:T(8,128)(2,1)S(1)}, bf16[32,6,8,128]{3,2,1,0:T(8,128)(2,1)S(1)}, u32[]{:S(2)}, u32[]{:S(2)}) collective-permute-start(bf16[32,6,8,128]{3,2,1,0:T(8,128)(2,1)S(1)} %pad_maximum_fusion), channel_id=1, source_target_pairs={{0,16},{16,0},{1,17},{17,1},{2,18},{18,2},{3,19},{19,3},{4,20},{20... | collective-permute-start | bytes 1179656 | tf_op jit(solution)/shard_map/ppermute | solution.py:292
  3.2 0.0 copy-done.3
  3.2 0.0 copy-done.2
  3.2 0.0 copy-start
  3.2 0.0 copy-start.1
  3.2 1.3 %prep.1 = (bf16[3,256,768]{2,1,0:T(8,128)(2,1)S(1)}, bf16[3,256,768]{2,1,0:T(8,128)(2,1)S(1)}, bf16[3,256,768]{2,1,0:T(8,128)(2,1)S(1)}, bf16[3,256,768]{2,1,0:T(8,128)(2,1)S(1)}) custom-call(bf16[3,3,3,32,32]{4,3,2,1,0:T(8,128)(2,1)S(1)} %bitcast.13, bf16[3,3,3,32,32]{4,3,2,1,0:T(8,128)(2,1)S(1)} %bitcast.14), custom_call_target="tpu_custom_call" | custom-call | flops 2000000000 | bytes 5000000 | tf_op jit(solution)/shard_map/prep/pallas_call | solution.py:306
  4.5 0.1 collective-permute-done.refs_2_
  4.6 0.0 copy-done
  4.6 0.0 copy-done.1
  4.6 11.2 %main.1 = (bf16[768,1280]{1,0:T(8,128)(2,1)S(1)}, f32[288,96]{1,0:T(8,128)S(1)}, f32[288,96]{1,0:T(8,128)S(1)}) custom-call(bf16[32,8,8,128]{3,2,1,0:T(8,128)(2,1)S(1)} %bitcast.11, bf16[32,8,8,128]{3,2,1,0:T(8,128)(2,1)S(1)} %bitcast.12, bf16[32,6,8,128]{3,2,1,0:T(8,128)(2,1)S(1)} %collective-permute-done.refs_2_, ...), custom_call_target="tpu_custom_call" | custom-call | flops 8000000000 | bytes 8000000 | tf_op jit(solution)/shard_map/main/pallas_call | solution.py:326
  15.8 0.4 collective-permute-start.1
  16.2 1.0 %collective-permute-done.1 = f32[288,96]{1,0:T(8,128)S(1)} collective-permute-done((f32[288,96]{1,0:T(8,128)S(1)}, f32[288,96]{1,0:T(8,128)S(1)}, u32[]{:S(2)}, u32[]{:S(2)}) %collective-permute-start.1) | collective-permute-done | bytes 110624 | tf_op jit(solution)/shard_map/ppermute | solution.py:271
  17.3 2.9 %collective-permute-start.2 = (f32[288,96]{1,0:T(8,128)S(1)}, f32[288,96]{1,0:T(8,128)S(1)}, u32[]{:S(2)}, u32[]{:S(2)}) collective-permute-start(f32[288,96]{1,0:T(8,128)S(1)} %select_add_fusion), channel_id=1, source_target_pairs={{0,1},{1,0},{2,3},{3,2},{4,5},{5,4},{6,7},{7,6},{8,9},{9,8},{10,11... | collective-permute-start | bytes 331784 | tf_op jit(solution)/shard_map/ppermute | solution.py:261
  20.2 4.2 %collective-permute-done.2 = f32[288,96]{1,0:T(8,128)S(1)} collective-permute-done((f32[288,96]{1,0:T(8,128)S(1)}, f32[288,96]{1,0:T(8,128)S(1)}, u32[]{:S(2)}, u32[]{:S(2)}) %collective-permute-start.2) | collective-permute-done | bytes 110624 | tf_op jit(solution)/shard_map/ppermute | solution.py:261
  24.4 1.8 %collective-permute-start.3 = (f32[288,96]{1,0:T(8,128)S(1)}, f32[288,96]{1,0:T(8,128)S(1)}, u32[]{:S(2)}, u32[]{:S(2)}) collective-permute-start(f32[288,96]{1,0:T(8,128)S(1)} %add.18), channel_id=1, source_target_pairs={{0,2},{1,3},{2,0},{3,1},{4,6},{5,7},{6,4},{7,5},{8,10},{9,11},{10,... | collective-permute-start | bytes 331784 | tf_op jit(solution)/shard_map/ppermute | solution.py:261
  26.2 3.5 %collective-permute-done.3 = f32[288,96]{1,0:T(8,128)S(1)} collective-permute-done((f32[288,96]{1,0:T(8,128)S(1)}, f32[288,96]{1,0:T(8,128)S(1)}, u32[]{:S(2)}, u32[]{:S(2)}) %collective-permute-start.3) | collective-permute-done | bytes 110624 | tf_op jit(solution)/shard_map/ppermute | solution.py:261
  29.8 1.7 %collective-permute-start.4 = (f32[288,96]{1,0:T(8,128)S(1)}, f32[288,96]{1,0:T(8,128)S(1)}, u32[]{:S(2)}, u32[]{:S(2)}) collective-permute-start(f32[288,96]{1,0:T(8,128)S(1)} %add.19), channel_id=1, source_target_pairs={{0,4},{1,5},{2,6},{3,7},{4,0},{5,1},{6,2},{7,3},{8,12},{9,13},{10,... | collective-permute-start | bytes 331784 | tf_op jit(solution)/shard_map/ppermute | solution.py:261
  31.5 3.5 %collective-permute-done.4 = f32[288,96]{1,0:T(8,128)S(1)} collective-permute-done((f32[288,96]{1,0:T(8,128)S(1)}, f32[288,96]{1,0:T(8,128)S(1)}, u32[]{:S(2)}, u32[]{:S(2)}) %collective-permute-start.4) | collective-permute-done | bytes 110624 | tf_op jit(solution)/shard_map/ppermute | solution.py:261
  35.0 3.2 %collective-permute-start.5 = (f32[288,96]{1,0:T(8,128)S(1)}, f32[288,96]{1,0:T(8,128)S(1)}, u32[]{:S(2)}, u32[]{:S(2)}) collective-permute-start(f32[288,96]{1,0:T(8,128)S(1)} %add.20), channel_id=1, source_target_pairs={{0,8},{1,9},{2,10},{3,11},{4,12},{5,13},{6,14},{7,15},{8,0},{9,1},... | collective-permute-start | bytes 331784 | tf_op jit(solution)/shard_map/ppermute | solution.py:261
  38.2 4.7 %collective-permute-done.5 = f32[288,96]{1,0:T(8,128)S(1)} collective-permute-done((f32[288,96]{1,0:T(8,128)S(1)}, f32[288,96]{1,0:T(8,128)S(1)}, u32[]{:S(2)}, u32[]{:S(2)}) %collective-permute-start.5) | collective-permute-done | bytes 110624 | tf_op jit(solution)/shard_map/ppermute | solution.py:261
  42.9 0.1 collective-permute-start.6
  43.0 2.4 %last.1 = bf16[32,8,8,128]{3,2,1,0:T(8,128)(2,1)} custom-call(bf16[768,1280]{1,0:T(8,128)(2,1)S(1)} %get-tuple-element.15.grad_field_ref, bf16[3,256,768]{2,1,0:T(8,128)(2,1)S(1)} %get-tuple-element.16.back_one), custom_call_target="tpu_custom_call" | custom-call | flops 2000000000 | bytes 3000000 | tf_op jit(solution)/shard_map/last/pallas_call | solution.py:341
  45.3 0.0 collective-permute-done.6
  45.4 1.2 %unpack.1 = (f32[3,3,3,32,32]{4,3,2,1,0:T(8,128)}, f32[3,3,3,32,32]{4,3,2,1,0:T(8,128)}) custom-call(f32[288,96]{1,0:T(8,128)S(1)} %get-tuple-element.22.one_ref, f32[288,96]{1,0:T(8,128)S(1)} %get-tuple-element.21.two_ref), custom_call_target="tpu_custom_call" | custom-call | tf_op jit(solution)/shard_map/unpack/pallas_call | solution.py:354
  (8 shorter events, 0.2 us)
Async XLA Ops:
  0.6 2.6 %copy-start.3 = (bf16[32,32,3,3,3]{1,0,4,3,2:T(8,128)(2,1)S(1)}, bf16[32,32,3,3,3]{1,0,4,3,2:T(8,128)(2,1)}, u32[]{:S(2)}) copy-start(bf16[32,32,3,3,3]{1,0,4,3,2:T(8,128)(2,1)} %param.6) | copy-start | bytes 165892
  0.6 2.6 %copy-start.2 = (bf16[32,32,3,3,3]{1,0,4,3,2:T(8,128)(2,1)S(1)}, bf16[32,32,3,3,3]{1,0,4,3,2:T(8,128)(2,1)}, u32[]{:S(2)}) copy-start(bf16[32,32,3,3,3]{1,0,4,3,2:T(8,128)(2,1)} %param.5) | copy-start | bytes 165892
  2.7 1.9 %collective-permute-start = (bf16[32,6,8,128]{3,2,1,0:T(8,128)(2,1)S(1)}, bf16[32,6,8,128]{3,2,1,0:T(8,128)(2,1)S(1)}, u32[]{:S(2)}, u32[]{:S(2)}) collective-permute-start(bf16[32,6,8,128]{3,2,1,0:T(8,128)(2,1)S(1)} %pad_maximum_fusion), channel_id=1, source_target_pairs={{0,16},{16,0},{1,17},{17,1},{2,18},{18,2},{3,19},{19,3},{4,20},{20... | collective-permute-start | bytes 1179656 | tf_op jit(solution)/shard_map/ppermute | solution.py:292
  3.2 1.3 %copy-start = (bf16[1,32,8,8,128]{4,3,2,1,0:T(8,128)(2,1)S(1)}, bf16[1,32,8,8,128]{4,3,2,1,0:T(8,128)(2,1)}, u32[]{:S(2)}) copy-start(bf16[1,32,8,8,128]{4,3,2,1,0:T(8,128)(2,1)} %param.4) | copy-start | bytes 1572868
  3.2 1.3 %copy-start.1 = (bf16[1,32,8,8,128]{4,3,2,1,0:T(8,128)(2,1)S(1)}, bf16[1,32,8,8,128]{4,3,2,1,0:T(8,128)(2,1)}, u32[]{:S(2)}) copy-start(bf16[1,32,8,8,128]{4,3,2,1,0:T(8,128)(2,1)} %param.7) | copy-start | bytes 1572868
  15.8 1.4 %collective-permute-start.1 = (f32[288,96]{1,0:T(8,128)S(1)}, f32[288,96]{1,0:T(8,128)S(1)}, u32[]{:S(2)}, u32[]{:S(2)}) collective-permute-start(f32[288,96]{1,0:T(8,128)S(1)} %broadcast_select_fusion.2), channel_id=1, source_target_pairs={{0,16},{16,0},{1,17},{17,1},{2,18},{18,2},{3,19},{19,3},{4,20},{20... | collective-permute-start | bytes 331784 | tf_op jit(solution)/shard_map/ppermute | solution.py:271
  17.3 7.1 %collective-permute-start.2 = (f32[288,96]{1,0:T(8,128)S(1)}, f32[288,96]{1,0:T(8,128)S(1)}, u32[]{:S(2)}, u32[]{:S(2)}) collective-permute-start(f32[288,96]{1,0:T(8,128)S(1)} %select_add_fusion), channel_id=1, source_target_pairs={{0,1},{1,0},{2,3},{3,2},{4,5},{5,4},{6,7},{7,6},{8,9},{9,8},{10,11... | collective-permute-start | bytes 331784 | tf_op jit(solution)/shard_map/ppermute | solution.py:261
  24.4 5.4 %collective-permute-start.3 = (f32[288,96]{1,0:T(8,128)S(1)}, f32[288,96]{1,0:T(8,128)S(1)}, u32[]{:S(2)}, u32[]{:S(2)}) collective-permute-start(f32[288,96]{1,0:T(8,128)S(1)} %add.18), channel_id=1, source_target_pairs={{0,2},{1,3},{2,0},{3,1},{4,6},{5,7},{6,4},{7,5},{8,10},{9,11},{10,... | collective-permute-start | bytes 331784 | tf_op jit(solution)/shard_map/ppermute | solution.py:261
  29.8 5.2 %collective-permute-start.4 = (f32[288,96]{1,0:T(8,128)S(1)}, f32[288,96]{1,0:T(8,128)S(1)}, u32[]{:S(2)}, u32[]{:S(2)}) collective-permute-start(f32[288,96]{1,0:T(8,128)S(1)} %add.19), channel_id=1, source_target_pairs={{0,4},{1,5},{2,6},{3,7},{4,0},{5,1},{6,2},{7,3},{8,12},{9,13},{10,... | collective-permute-start | bytes 331784 | tf_op jit(solution)/shard_map/ppermute | solution.py:261
  35.0 7.9 %collective-permute-start.5 = (f32[288,96]{1,0:T(8,128)S(1)}, f32[288,96]{1,0:T(8,128)S(1)}, u32[]{:S(2)}, u32[]{:S(2)}) collective-permute-start(f32[288,96]{1,0:T(8,128)S(1)} %add.20), channel_id=1, source_target_pairs={{0,8},{1,9},{2,10},{3,11},{4,12},{5,13},{6,14},{7,15},{8,0},{9,1},... | collective-permute-start | bytes 331784 | tf_op jit(solution)/shard_map/ppermute | solution.py:261
  42.9 2.4 %collective-permute-start.6 = (f32[288,96]{1,0:T(8,128)S(1)}, f32[288,96]{1,0:T(8,128)S(1)}, u32[]{:S(2)}, u32[]{:S(2)}) collective-permute-start(f32[288,96]{1,0:T(8,128)S(1)} %add.21), channel_id=1, source_target_pairs={{0,16},{16,0},{1,17},{17,1},{2,18},{18,2},{3,19},{19,3},{4,20},{20... | collective-permute-start | bytes 331784 | tf_op jit(solution)/shard_map/ppermute | solution.py:273

commit v2 on v1

v2 whole, which is shorter than its diff:
```python
import functools
import math

import jax
import jax.numpy as jnp
from jax import lax
from jax.experimental import pallas as pl
from jax.experimental.pallas import tpu as pltpu
from jax.sharding import PartitionSpec as P

F32, BF16 = jnp.float32, jnp.bfloat16
NT = (((1,), (1,)), ((), ()))
REACH = 4


def params(mib):
    return pltpu.CompilerParams(vmem_limit_bytes=mib * 2**20)


def cost(flops, size):
    return pl.CostEstimate(flops=int(flops), bytes_accessed=int(size), transcendentals=0)


def pack_kernel(count, own, data_ref, cot_ref, *refs):
    outs, sems = refs[:-1], refs[-1]
    copies = []
    for side, out in enumerate(outs):
        for which, (ref, depth, at) in enumerate(
            ((data_ref, REACH, 0), (cot_ref, REACH - 2, REACH))
        ):
            start = own - depth if side == 0 else 0
            if count == 2:
                start = jnp.where(lax.axis_index("gz") == 1, 0, own - depth)
            copies.append(
                pltpu.make_async_copy(
                    ref.at[:, pl.ds(start, depth)],
                    out.at[:, pl.ds(at, depth)],
                    sems.at[side, which],
                )
            )
    for copy in copies:
        copy.start()
    for copy in copies:
        copy.wait()


def turned(turn_ref, slot, value):
    chan, height, width = value.shape
    turn_ref[slot] = value.astype(F32).reshape(chan * height, width)
    return jnp.concatenate(
        [turn_ref[slot, pl.ds(y, chan, stride=height), :] for y in range(height)], axis=0
    )


def prep_kernel(mirrored, data_ref, one_ref, two_ref, *refs):
    flip = lax.axis_index("gz") == 1 if mirrored else False
    outs, field_ref, wide, turn_ref = refs[:4], refs[4], refs[5], refs[6]
    chan = one_ref.shape[-1]
    full = outs[0].shape[1]
    height = full // chan
    own, width = data_ref.shape[1], data_ref.shape[-1]
    field = Field([(field_ref, 0, own, 0)], full, width)
    for plane in range(own):
        at = jnp.where(flip, own - 1 - plane, plane) if mirrored else plane
        field.put(plane, turned(turn_ref, plane % 2, data_ref[:, at]))
    lane = lax.broadcasted_iota(jnp.int32, (chan, full), 1)
    row = lax.broadcasted_iota(jnp.int32, (chan, full), 0)
    repeat = jnp.where(lax.rem(lane, chan) == row, 1.0, 0.0).astype(BF16)
    block = lane // chan
    for index, ref in enumerate((one_ref, two_ref)):
        forward, backward = outs[2 * index], outs[2 * index + 1]
        flat = ref[...].reshape(27 * chan, chan)
        spread = jnp.dot(flat, repeat, preferred_element_type=F32)
        wide[...] = spread.reshape(3, 9 * chan, full)
        for dz in range(3):
            source = jnp.where(flip, 2 - dz, dz) if mirrored else dz
            for dx in range(3):
                taps = [
                    wide[source, (dy * 3 + dx) * chan : (dy * 3 + dx + 1) * chan, :]
                    for dy in range(3)
                ]
                strips = []
                for y in range(height):
                    strip = jnp.zeros((chan, full), F32)
                    for dy in range(3):
                        strip = jnp.where(block == y + dy - 1, taps[dy], strip)
                    strips.append(strip.astype(BF16))
                tile = jnp.concatenate(strips, axis=0)
                forward[dz, :, dx * full : (dx + 1) * full] = tile
                backward[2 - dz, :, (2 - dx) * full : (3 - dx) * full] = tile.T


class Field:
    def __init__(self, pieces, full, width):
        self.pieces, self.full, self.width = pieces, full, width

    def run(self, plane, count):
        for ref, first, number, base in self.pieces:
            if first <= plane < first + number:
                at = plane - first
                size = min(count, number - at)
                return ref, slice((base + at) * self.width, (base + at + size) * self.width), size
        raise IndexError(plane)

    def take(self, rows, first, count):
        parts = []
        while count:
            ref, lanes, size = self.run(first, count)
            parts.append(ref[rows, lanes])
            first, count = first + size, count - size
        return parts[0] if len(parts) == 1 else jnp.concatenate(parts, axis=1)

    def put(self, plane, value):
        full, width = self.full, self.width
        ref, lanes, _ = self.run(plane, 1)
        lane = lax.broadcasted_iota(jnp.int32, (full, width), 1)
        before = jnp.where(lane == 0, 0.0, pltpu.roll(value, 1, 1))
        after = jnp.where(lane == width - 1, 0.0, pltpu.roll(value, width - 1, 1))
        for dx, item in enumerate((before, value, after)):
            ref[dx * full : (dx + 1) * full, lanes] = item.astype(BF16)

    def blank(self, plane):
        ref, lanes, _ = self.run(plane, 1)
        ref[:, lanes] = jnp.zeros((3 * self.full, self.width), BF16)

    def convolve(self, band, first, count):
        total = None
        for dz in range(3):
            window = self.take(slice(None), first + dz - 1, count)
            piece = jnp.dot(band[dz], window, preferred_element_type=F32)
            total = piece if total is None else total + piece
        return total


def spans(low, high):
    return [(at, min(2, high - at)) for at in range(low, high, 2)]


def sigmoid(value):
    return 0.5 * jnp.tanh(0.5 * value) + 0.5


def gradient(field, grads, own, chan, flip, out_ref):
    full = field.full
    height = full // chan
    sums = [[None] * 3 for _ in range(3)]
    for base in range(0, height, 2):
        right = jnp.concatenate(
            [
                grads.take(slice((2 - dx) * full + y * chan, (2 - dx) * full + (y + 1) * chan), 0, own)
                for y in (base, base + 1)
                for dx in (0, 1, 2, 2)
            ],
            axis=0,
        )
        low, high = max(base - 1, 0), min(base + 3, height)
        left = jnp.concatenate(
            [
                field.take(slice(full + low * chan, full + high * chan), dz - 1, own)
                for dz in range(3)
            ],
            axis=0,
        )
        piece = lax.dot_general(left, right, NT, preferred_element_type=F32)
        for dz in range(3):
            for step in range(2):
                for dy in range(3):
                    at = base + step + dy - 1
                    if 0 <= at < height:
                        row = (dz * (high - low) + at - low) * chan
                        part = piece[row : row + chan, step * 4 * chan : (step + 1) * 4 * chan]
                        held = sums[dz][dy]
                        sums[dz][dy] = part if held is None else held + part
    if flip is not None:
        first = [jnp.where(flip, c, a) for a, c in zip(sums[0], sums[2])]
        third = [jnp.where(flip, a, c) for a, c in zip(sums[0], sums[2])]
        sums = [first, sums[1], third]
    for dz in range(2):
        for dy in range(3):
            row = (dz * 3 + dy) * chan
            out_ref[row : row + chan, : 3 * chan] = sums[dz][dy][:, : 3 * chan]
            out_ref[row : row + chan, 3 * chan :] = sums[2][dy][:, dz * chan : (dz + 1) * chan]
    for dy in range(3):
        out_ref[6 * chan :, dy * chan : (dy + 1) * chan] = sums[2][dy][:, 2 * chan : 3 * chan]
    out_ref[6 * chan :, 3 * chan :] = jnp.zeros((chan, chan), F32)


def main_kernel(count, sizes, *refs):
    chan, own, height, width, low_side, high_side = sizes
    full = chan * height
    mirrored = count == 2
    halos = low_side + high_side
    data_ref, cot_ref = refs[:2]
    halo_refs = refs[2 : 2 + halos]
    band_one, band_two, back_two = refs[2 + halos : 5 + halos]
    grad_field_ref, term_one, term_two = refs[5 + halos : 8 + halos]
    edge_ref, h_ref, g_ref, slope_ref, turn_ref = refs[8 + halos :]
    position = lax.axis_index("gz")
    flip = position == 1 if mirrored else None

    def reach(depth):
        return (-depth * low_side, own + depth * high_side)

    def field(ref, depth):
        before = depth if low_side else 1
        item = Field([(ref, -before, slots(sizes, depth), 0)], full, width)
        return blanked(item)

    def blanked(item):
        if not low_side:
            item.blank(-1)
        if not high_side:
            item.blank(own)
        return item

    def plane_of(ref, plane, skip, depth):
        if 0 <= plane < own:
            at = jnp.where(flip, own - 1 - plane, plane) if mirrored else plane
            return ref[:, at]
        if plane < 0:
            return halo_refs[0][:, skip + depth + plane]
        at = plane - own
        if mirrored:
            at = jnp.where(flip, depth - 1 - at, at)
        return halo_refs[-1][:, skip + at]

    def kept(plane, value):
        if count == 2:
            return value
        if plane < 0:
            return jnp.where(position > 0, value, 0.0)
        if plane >= own:
            return jnp.where(position < count - 1, value, 0.0)
        return value

    before = REACH if low_side else 1
    after = REACH if high_side else 1
    data = Field(
        [(data_ref, 0, own, 0), (edge_ref, -before, before, 0), (edge_ref, own, after, before)],
        full,
        width,
    )
    blanked(data)
    for plane in range(*reach(REACH)):
        if not 0 <= plane < own:
            data.put(plane, turned(turn_ref, plane % 2, plane_of(None, plane, 0, REACH)))

    hidden = field(h_ref, REACH - 1)
    slope_low, slope_high = reach(1)
    for first, number in spans(*reach(REACH - 1)):
        pre = data.convolve(band_one, first, number)
        for step in range(number):
            plane = first + step
            value = pre[:, step * width : (step + 1) * width]
            gate = sigmoid(value)
            hidden.put(plane, kept(plane, value * gate))
            if slope_low <= plane < slope_high:
                at = (plane - slope_low) * width
                slope_ref[:, at : at + width] = gate * (1.0 + value * (1.0 - gate))

    upper = field(g_ref, REACH - 2)
    for first, number in spans(*reach(REACH - 2)):
        pre = hidden.convolve(band_two, first, number)
        for step in range(number):
            plane = first + step
            value = pre[:, step * width : (step + 1) * width]
            gate = sigmoid(value)
            seed = turned(turn_ref, plane % 2, plane_of(cot_ref, plane, REACH, REACH - 2))
            upper.put(plane, seed * (gate * (1.0 + value * (1.0 - gate))))
    gradient(hidden, upper, own, chan, flip, term_two)

    lower = field(grad_field_ref, REACH - 3)
    for first, number in spans(*reach(REACH - 3)):
        back = upper.convolve(back_two, first, number)
        for step in range(number):
            plane = first + step
            at = (plane - slope_low) * width
            grad = back[:, step * width : (step + 1) * width] * slope_ref[:, at : at + width]
            lower.put(plane, kept(plane, grad))
    gradient(data, lower, own, chan, flip, term_one)


def slots(sizes, depth):
    _, own, _, _, low_side, high_side = sizes
    return own + sum(depth if side else 1 for side in (low_side, high_side))


def last_kernel(count, sizes, grad_field_ref, back_one, out_ref, turn_ref):
    chan, own, height, width, _, _ = sizes
    full = chan * height
    mirrored = count == 2
    flip = lax.axis_index("gz") == 1 if mirrored else None
    lower = Field([(grad_field_ref, -1, own + 2, 0)], full, width)
    for first, number in spans(0, own):
        out = lower.convolve(back_one, first, number)
        for step in range(number):
            plane = first + step
            value = out[:, step * width : (step + 1) * width]
            slot = plane % 2
            for y in range(height):
                turn_ref[slot, pl.ds(y, chan, stride=height), :] = value[y * chan : (y + 1) * chan]
            at = jnp.where(flip, own - 1 - plane, plane) if mirrored else plane
            out_ref[:, at] = turn_ref[slot].reshape(chan, height, width).astype(BF16)


def unpack_kernel(factor, one_ref, two_ref, out_one, out_two):
    chan = out_one.shape[-1]
    for ref, out in ((one_ref, out_one), (two_ref, out_two)):
        value = ref[...].T * factor
        for dz in range(3):
            for dy in range(3):
                for dx in range(3):
                    row, column = (dx, 3 * dz + dy) if dz < 2 else (3, 3 * dx + dy)
                    if dz == 2 and dx == 2:
                        row, column = dy, 6
                    out[dz, dy, dx] = value[
                        row * chan : (row + 1) * chan, column * chan : (column + 1) * chan
                    ]


def doubled(value, axis, before_last=None):
    count = lax.axis_size(axis)
    if count & (count - 1):
        value = before_last(value) if before_last else value
        return lax.psum(value, axis)
    step = 1
    while step < count:
        if before_last and step * 2 == count:
            value = before_last(value)
        value = value + lax.ppermute(value, axis, [(i, i ^ step) for i in range(count)])
        step *= 2
    return value


def reduced(one, two, grad_fields, finish):
    outs = []

    def gate(value):
        value, *held = lax.optimization_barrier((value, *grad_fields))
        outs.extend(finish(held))
        return value

    if lax.axis_size("gz") == 2:
        swap = [(0, 1), (1, 0)]
        first = lax.axis_index("gz") == 0
        mine = jnp.where(first, two, one)
        mine = mine + lax.ppermute(jnp.where(first, one, two), "gz", swap)
        mine = doubled(mine, "dp", gate)
        mine, *outs = lax.optimization_barrier((mine, *(outs or finish(grad_fields))))
        other = lax.ppermute(mine, "gz", swap)
        return jnp.where(first, other, mine), jnp.where(first, mine, other), outs
    both = doubled(doubled(jnp.stack([one, two]), "gz"), "dp", gate)
    return both[0], both[1], outs or finish(grad_fields)


def halo_of(data, cot, count):
    if count == 1:
        return []
    chan, own, height, width = data.shape
    sides = 1 if count == 2 else 2
    hbm = pl.BlockSpec(memory_space=pltpu.HBM)
    messages = pl.pallas_call(
        functools.partial(pack_kernel, count, own),
        out_shape=[jax.ShapeDtypeStruct((chan, 2 * REACH - 2, height, width), BF16)] * sides,
        in_specs=[hbm, hbm],
        scratch_shapes=[pltpu.SemaphoreType.DMA((sides, 2))],
        compiler_params=params(60),
        name="pack",
    )(data, cot)
    if count == 2:
        return [lax.ppermute(messages[0], "gz", [(0, 1), (1, 0)])]
    up = [(i, i + 1) for i in range(count - 1)]
    down = [(j, i) for i, j in up]
    return [lax.ppermute(messages[0], "gz", up), lax.ppermute(messages[1], "gz", down)]


def local(inputs, kernel_one, kernel_two, cotangent):
    count = lax.axis_size("gz")
    batch, chan, own, height, width = inputs.shape
    full = chan * height
    low_side, high_side = (1, 1) if count > 2 else (0, 1 if count == 2 else 0)
    sizes = (chan, own, height, width, low_side, high_side)
    taps = [jnp.transpose(k, (2, 3, 4, 0, 1)) for k in (kernel_one, kernel_two)]
    turn = pltpu.VMEM((2, full, width), F32)

    def stack(depth):
        return (3 * full, slots(sizes, depth) * width)

    grad_fields, backs, ones, twos = [], [], [], []
    for sample in range(batch):
        data, cot = inputs[sample], cotangent[sample]
        halos = halo_of(data, cot, count)
        *bands, field = pl.pallas_call(
            functools.partial(prep_kernel, count == 2),
            out_shape=[jax.ShapeDtypeStruct((3, full, 3 * full), BF16)] * 4
            + [jax.ShapeDtypeStruct((3 * full, own * width), BF16)],
            scratch_shapes=[pltpu.VMEM((3, 9 * chan, full), F32), turn],
            compiler_params=params(16),
            cost_estimate=cost(2e9, 5e6),
            name="prep",
        )(data, *taps)
        term = jax.ShapeDtypeStruct((7 * chan, 4 * chan), F32)
        grad_field, term_one, term_two = pl.pallas_call(
            functools.partial(main_kernel, count, sizes),
            out_shape=[jax.ShapeDtypeStruct(stack(REACH - 3), BF16), term, term],
            scratch_shapes=[
                pltpu.VMEM((3 * full, (slots(sizes, REACH) - own) * width), BF16),
                pltpu.VMEM(stack(REACH - 1), BF16),
                pltpu.VMEM(stack(REACH - 2), BF16),
                pltpu.VMEM((full, (own + low_side + high_side) * width), F32),
                turn,
            ],
            compiler_params=params(32),
            cost_estimate=cost(8e9, 8e6),
            name="main",
        )(field, cot, *halos, bands[0], bands[2], bands[3])
        grad_fields.append(grad_field)
        backs.append(bands[1])
        ones.append(term_one)
        twos.append(term_two)

    def finish(fields):
        return [
            pl.pallas_call(
                functools.partial(last_kernel, count, sizes),
                out_shape=jax.ShapeDtypeStruct((chan, own, height, width), BF16),
                scratch_shapes=[turn],
                compiler_params=params(16),
                cost_estimate=cost(2e9, 3e6),
                name="last",
            )(*pair)
            for pair in zip(fields, backs)
        ]

    one, two, outs = reduced(sum(ones[1:], ones[0]), sum(twos[1:], twos[0]), grad_fields, finish)
    cells = lax.axis_size("dp") * batch * count * own * height * width
    grads = pl.pallas_call(
        functools.partial(unpack_kernel, 1.0 / math.sqrt(cells)),
        out_shape=[jax.ShapeDtypeStruct((3, 3, 3, chan, chan), F32)] * 2,
        compiler_params=params(8),
        name="unpack",
    )(one, two)
    one, two = [jnp.transpose(g, (3, 4, 0, 1, 2)) for g in grads]
    return jnp.stack(outs), one, two


def solution(mesh):
    return jax.shard_map(
        local,
        mesh=mesh,
        in_specs=(P("dp", None, "gz", None, None), P(), P(), P("dp", None, "gz", None, None)),
        out_specs=(P("dp", None, "gz", None, None), P(), P()),
        check_vma=False,
    )
```

time: 46.7 us -> 39.4 us (0.84)
  waiting for transfers between devices: 17 us -> 13.4 us
  Pallas kernels: 16 us -> 14 us
  local copies, waits for them, and re-layouts: 1.98 us -> 0.02 us
    ppermute x4, waiting for transfers between devices: 15.9 us -> 11.1 us  [doubled(): lax.ppermute(value, axis, [(i, i ^ step) for i in range(count)])]
    pallas_call x1, Pallas kernels: 11.2 us -> 7.17 us  [local(): pl.pallas_call(functools.partial(main_kernel, count, sizes), out_shape=[j...]
    dynamic_slice x2 -> x0, local copies, waits for them, and re-layouts: 1.96 us -> none  [ends(): parts.append(lax.dynamic_slice_in_dim(value, start, depth, axis=1))]
    pallas_call x1 -> x2, Pallas kernels: 2.36 us -> 4.19 us  [the longest x1 2.36 us: finish(): pl.pallas_call(functools.partial(last_kernel, count, sizes), out_shape=ja...]
    ppermute x1, waiting for transfers between devices: 0.01 us -> 1.31 us  [reduced(): other = lax.ppermute(mine, 'gz', swap)]
  transfers between devices with their start and end apart: 7 -> 7, of which waited for: 6 -> 7; matrix products, arithmetic and copies ran while one was open for 0% -> 0% of each run, Pallas kernels for 8% -> 10%
where the time goes in v2:
time: 39.4 us; the launch traced here: 39.3 us
  Pallas kernels  14 us (36%)
  waiting for transfers between devices  13.4 us (34%)
  starting transfers between devices  11 us (28%)
  between operations  0.72 us (2%)
    ppermute x4, waiting for transfers between devices, doubled(): lax.ppermute(value, axis, [(i, i ^ step) for i in range(count)])  11.1 us
    ppermute x4, starting transfers between devices, doubled(): lax.ppermute(value, axis, [(i, i ^ step) for i in range(count)])  9.96 us
    pallas_call x1, Pallas kernels, local(): pl.pallas_call(functools.partial(main_kernel, count, sizes), out_shape=[j...  7.17 us
    pallas_call x1, Pallas kernels, finish(): pl.pallas_call(functools.partial(last_kernel, count, sizes), out_shape=ja...  2.36 us
    pallas_call x1, Pallas kernels, halo_of(): pl.pallas_call(functools.partial(pack_kernel, count, own), out_shape=[jax...  1.83 us
    pallas_call x1, Pallas kernels, local(): pl.pallas_call(functools.partial(prep_kernel, count == 2), out_shape=[jax...  1.49 us
    ppermute x1, waiting for transfers between devices, reduced(): other = lax.ppermute(mine, 'gz', swap)  1.31 us
    pallas_call x1, Pallas kernels, local(): pl.pallas_call(functools.partial(unpack_kernel, 1.0 / math.sqrt(cells)),...  1.14 us
  transfers between devices with their start and end apart: 7, of which 7 were waited for; matrix products, arithmetic and copies ran while one was open for 0% of the time, Pallas kernels for 10%

profile of v2, /device:TPU:0, one launch (start us, length us, event | category | flops | bytes accessed | tf_op | source)
XLA Modules:
  0.0 39.3 jit_solution(10309837312735968301)
XLA Ops:
  0.6 0.0 copy-start
  0.6 0.0 copy-start.2
  0.7 0.0 copy-start.3
  0.7 1.8 %pack.1 = bf16[32,6,8,128]{3,2,1,0:T(8,128)(2,1)} custom-call(bf16[32,8,8,128]{3,2,1,0:T(8,128)(2,1)} %bitcast.7, bf16[32,8,8,128]{3,2,1,0:T(8,128)(2,1)} %bitcast.9), custom_call_target="tpu_custom_call" | custom-call | tf_op jit(solution)/shard_map/pack/pallas_call | solution.py:362
  2.5 0.6 %collective-permute-start = (bf16[32,6,8,128]{3,2,1,0:T(8,128)(2,1)}, bf16[32,6,8,128]{3,2,1,0:T(8,128)(2,1)S(1)}, u32[]{:S(2)}, u32[]{:S(2)}) collective-permute-start(bf16[32,6,8,128]{3,2,1,0:T(8,128)(2,1)} %pack.1), channel_id=1, source_target_pairs={{0,16},{16,0},{1,17},{17,1},{2,18},{18,2},{3,19},{19,3},{4,20},{20... | collective-permute-start | bytes 1179656 | tf_op jit(solution)/shard_map/ppermute | solution.py:371
  3.1 0.0 copy-done
  3.1 0.0 copy-done.2
  3.1 0.0 copy-done.3
  3.1 0.0 copy-start.1
  3.1 1.5 %prep.1 = (bf16[3,256,768]{2,1,0:T(8,128)(2,1)S(1)}, bf16[3,256,768]{2,1,0:T(8,128)(2,1)S(1)}, bf16[3,256,768]{2,1,0:T(8,128)(2,1)S(1)}, bf16[3,256,768]{2,1,0:T(8,128)(2,1)S(1)}, bf16[768,1024]{1,0:T(8,128)(2,1)S(1)}) custom-call(bf16[32,8,8,128]{3,2,1,0:T(8,128)(2,1)S(1)} %bitcast.8, bf16[3,3,3,32,32]{4,3,2,1,0:T(8,128)(2,1)S(1)} %bitcast.11, ...), custom_call_target="tpu_custom_call" | custom-call | flops 2000000000 | bytes 5000000 | tf_op jit(solution)/shard_map/prep/pallas_call | solution.py:393
  4.6 0.1 collective-permute-done.refs_2_
  4.6 0.0 copy-done.1
  4.6 7.2 %main.1 = (bf16[768,1280]{1,0:T(8,128)(2,1)S(1)}, f32[224,128]{1,0:T(8,128)S(1)}, f32[224,128]{1,0:T(8,128)S(1)}) custom-call(bf16[768,1024]{1,0:T(8,128)(2,1)S(1)} %get-tuple-element.17.refs_0_, bf16[32,8,8,128]{3,2,1,0:T(8,128)(2,1)S(1)} %bitcast.10, bf16[32,6,8,128]{3,2,1,0:T(8,128)(2,1)S(1)} %collective-permute-done.refs_2_, ...), custom_call_target="tpu_custom_call" | custom-call | flops 8000000000 | bytes 8000000 | tf_op jit(solution)/shard_map/main/pallas_call | solution.py:403
  11.8 0.4 %collective-permute-start.1 = (f32[224,128]{1,0:T(8,128)S(1)}, f32[224,128]{1,0:T(8,128)S(1)}, u32[]{:S(2)}, u32[]{:S(2)}) collective-permute-start(f32[224,128]{1,0:T(8,128)S(1)} %broadcast_select_fusion.2), channel_id=1, source_target_pairs={{0,16},{16,0},{1,17},{17,1},{2,18},{18,2},{3,19},{19,3},{4,20},{20... | collective-permute-start | bytes 344072 | tf_op jit(solution)/shard_map/ppermute | solution.py:347
  12.3 1.0 %collective-permute-done.1 = f32[224,128]{1,0:T(8,128)S(1)} collective-permute-done((f32[224,128]{1,0:T(8,128)S(1)}, f32[224,128]{1,0:T(8,128)S(1)}, u32[]{:S(2)}, u32[]{:S(2)}) %collective-permute-start.1) | collective-permute-done | bytes 114720 | tf_op jit(solution)/shard_map/ppermute | solution.py:347
  13.2 2.9 %collective-permute-start.2 = (f32[224,128]{1,0:T(8,128)S(1)}, f32[224,128]{1,0:T(8,128)S(1)}, u32[]{:S(2)}, u32[]{:S(2)}) collective-permute-start(f32[224,128]{1,0:T(8,128)S(1)} %select_add_fusion), channel_id=1, source_target_pairs={{0,1},{1,0},{2,3},{3,2},{4,5},{5,4},{6,7},{7,6},{8,9},{9,8},{10,11... | collective-permute-start | bytes 344072 | tf_op jit(solution)/shard_map/ppermute | solution.py:330
  16.2 3.5 %collective-permute-done.2 = f32[224,128]{1,0:T(8,128)S(1)} collective-permute-done((f32[224,128]{1,0:T(8,128)S(1)}, f32[224,128]{1,0:T(8,128)S(1)}, u32[]{:S(2)}, u32[]{:S(2)}) %collective-permute-start.2) | collective-permute-done | bytes 114720 | tf_op jit(solution)/shard_map/ppermute | solution.py:330
  19.6 1.8 %collective-permute-start.3 = (f32[224,128]{1,0:T(8,128)S(1)}, f32[224,128]{1,0:T(8,128)S(1)}, u32[]{:S(2)}, u32[]{:S(2)}) collective-permute-start(f32[224,128]{1,0:T(8,128)S(1)} %add.16), channel_id=1, source_target_pairs={{0,2},{1,3},{2,0},{3,1},{4,6},{5,7},{6,4},{7,5},{8,10},{9,11},{10,... | collective-permute-start | bytes 344072 | tf_op jit(solution)/shard_map/ppermute | solution.py:330
  21.5 3.0 %collective-permute-done.3 = f32[224,128]{1,0:T(8,128)S(1)} collective-permute-done((f32[224,128]{1,0:T(8,128)S(1)}, f32[224,128]{1,0:T(8,128)S(1)}, u32[]{:S(2)}, u32[]{:S(2)}) %collective-permute-start.3) | collective-permute-done | bytes 114720 | tf_op jit(solution)/shard_map/ppermute | solution.py:330
  24.5 1.9 %collective-permute-start.4 = (f32[224,128]{1,0:T(8,128)S(1)}, f32[224,128]{1,0:T(8,128)S(1)}, u32[]{:S(2)}, u32[]{:S(2)}) collective-permute-start(f32[224,128]{1,0:T(8,128)S(1)} %add.17), channel_id=1, source_target_pairs={{0,4},{1,5},{2,6},{3,7},{4,0},{5,1},{6,2},{7,3},{8,12},{9,13},{10,... | collective-permute-start | bytes 344072 | tf_op jit(solution)/shard_map/ppermute | solution.py:330
  26.4 3.0 %collective-permute-done.4 = f32[224,128]{1,0:T(8,128)S(1)} collective-permute-done((f32[224,128]{1,0:T(8,128)S(1)}, f32[224,128]{1,0:T(8,128)S(1)}, u32[]{:S(2)}, u32[]{:S(2)}) %collective-permute-start.4) | collective-permute-done | bytes 114720 | tf_op jit(solution)/shard_map/ppermute | solution.py:330
  29.4 3.3 %collective-permute-start.5 = (f32[224,128]{1,0:T(8,128)S(1)}, f32[224,128]{1,0:T(8,128)S(1)}, u32[]{:S(2)}, u32[]{:S(2)}) collective-permute-start(f32[224,128]{1,0:T(8,128)S(1)} %add.18), channel_id=1, source_target_pairs={{0,8},{1,9},{2,10},{3,11},{4,12},{5,13},{6,14},{7,15},{8,0},{9,1},... | collective-permute-start | bytes 344072 | tf_op jit(solution)/shard_map/ppermute | solution.py:330
  32.7 2.4 %last.1 = bf16[32,8,8,128]{3,2,1,0:T(8,128)(2,1)} custom-call(bf16[768,1280]{1,0:T(8,128)(2,1)S(1)} %get-tuple-element.25.grad_field_ref, bf16[3,256,768]{2,1,0:T(8,128)(2,1)S(1)} %get-tuple-element.26.back_one), custom_call_target="tpu_custom_call" | custom-call | flops 2000000000 | bytes 3000000 | tf_op jit(solution)/shard_map/last/pallas_call | solution.py:424
  35.1 1.6 %collective-permute-done.5 = f32[224,128]{1,0:T(8,128)S(1)} collective-permute-done((f32[224,128]{1,0:T(8,128)S(1)}, f32[224,128]{1,0:T(8,128)S(1)}, u32[]{:S(2)}, u32[]{:S(2)}) %collective-permute-start.5) | collective-permute-done | bytes 114720 | tf_op jit(solution)/shard_map/ppermute | solution.py:330
  36.7 0.1 collective-permute-start.6
  36.8 1.3 %collective-permute-done.6 = f32[224,128]{1,0:T(8,128)S(1)} collective-permute-done((f32[224,128]{1,0:T(8,128)S(1)}, f32[224,128]{1,0:T(8,128)S(1)}, u32[]{:S(2)}, u32[]{:S(2)}) %collective-permute-start.6) | collective-permute-done | bytes 114720 | tf_op jit(solution)/shard_map/ppermute | solution.py:350
  38.2 1.1 %unpack.1 = (f32[3,3,3,32,32]{4,3,2,1,0:T(8,128)}, f32[3,3,3,32,32]{4,3,2,1,0:T(8,128)}) custom-call(f32[224,128]{1,0:T(8,128)S(1)} %get-tuple-element.32.one_ref, f32[224,128]{1,0:T(8,128)S(1)} %get-tuple-element.31.two_ref), custom_call_target="tpu_custom_call" | custom-call | tf_op jit(solution)/shard_map/unpack/pallas_call | solution.py:437
  (7 shorter events, 0.1 us)
Async XLA Ops:
  0.6 2.4 %copy-start = (bf16[1,32,8,8,128]{4,3,2,1,0:T(8,128)(2,1)S(1)}, bf16[1,32,8,8,128]{4,3,2,1,0:T(8,128)(2,1)}, u32[]{:S(2)}) copy-start(bf16[1,32,8,8,128]{4,3,2,1,0:T(8,128)(2,1)} %param.4) | copy-start | bytes 1572868
  0.6 2.4 %copy-start.2 = (bf16[32,32,3,3,3]{1,0,4,3,2:T(8,128)(2,1)S(1)}, bf16[32,32,3,3,3]{1,0,4,3,2:T(8,128)(2,1)}, u32[]{:S(2)}) copy-start(bf16[32,32,3,3,3]{1,0,4,3,2:T(8,128)(2,1)} %param.5) | copy-start | bytes 165892
  0.7 2.4 %copy-start.3 = (bf16[32,32,3,3,3]{1,0,4,3,2:T(8,128)(2,1)S(1)}, bf16[32,32,3,3,3]{1,0,4,3,2:T(8,128)(2,1)}, u32[]{:S(2)}) copy-start(bf16[32,32,3,3,3]{1,0,4,3,2:T(8,128)(2,1)} %param.6) | copy-start | bytes 165892
  2.5 2.1 %collective-permute-start = (bf16[32,6,8,128]{3,2,1,0:T(8,128)(2,1)}, bf16[32,6,8,128]{3,2,1,0:T(8,128)(2,1)S(1)}, u32[]{:S(2)}, u32[]{:S(2)}) collective-permute-start(bf16[32,6,8,128]{3,2,1,0:T(8,128)(2,1)} %pack.1), channel_id=1, source_target_pairs={{0,16},{16,0},{1,17},{17,1},{2,18},{18,2},{3,19},{19,3},{4,20},{20... | collective-permute-start | bytes 1179656 | tf_op jit(solution)/shard_map/ppermute | solution.py:371
  3.1 1.6 %copy-start.1 = (bf16[1,32,8,8,128]{4,3,2,1,0:T(8,128)(2,1)S(1)}, bf16[1,32,8,8,128]{4,3,2,1,0:T(8,128)(2,1)}, u32[]{:S(2)}) copy-start(bf16[1,32,8,8,128]{4,3,2,1,0:T(8,128)(2,1)} %param.7) | copy-start | bytes 1572868
  11.8 1.4 %collective-permute-start.1 = (f32[224,128]{1,0:T(8,128)S(1)}, f32[224,128]{1,0:T(8,128)S(1)}, u32[]{:S(2)}, u32[]{:S(2)}) collective-permute-start(f32[224,128]{1,0:T(8,128)S(1)} %broadcast_select_fusion.2), channel_id=1, source_target_pairs={{0,16},{16,0},{1,17},{17,1},{2,18},{18,2},{3,19},{19,3},{4,20},{20... | collective-permute-start | bytes 344072 | tf_op jit(solution)/shard_map/ppermute | solution.py:347
  13.2 6.4 %collective-permute-start.2 = (f32[224,128]{1,0:T(8,128)S(1)}, f32[224,128]{1,0:T(8,128)S(1)}, u32[]{:S(2)}, u32[]{:S(2)}) collective-permute-start(f32[224,128]{1,0:T(8,128)S(1)} %select_add_fusion), channel_id=1, source_target_pairs={{0,1},{1,0},{2,3},{3,2},{4,5},{5,4},{6,7},{7,6},{8,9},{9,8},{10,11... | collective-permute-start | bytes 344072 | tf_op jit(solution)/shard_map/ppermute | solution.py:330
  19.6 4.9 %collective-permute-start.3 = (f32[224,128]{1,0:T(8,128)S(1)}, f32[224,128]{1,0:T(8,128)S(1)}, u32[]{:S(2)}, u32[]{:S(2)}) collective-permute-start(f32[224,128]{1,0:T(8,128)S(1)} %add.16), channel_id=1, source_target_pairs={{0,2},{1,3},{2,0},{3,1},{4,6},{5,7},{6,4},{7,5},{8,10},{9,11},{10,... | collective-permute-start | bytes 344072 | tf_op jit(solution)/shard_map/ppermute | solution.py:330
  24.5 4.9 %collective-permute-start.4 = (f32[224,128]{1,0:T(8,128)S(1)}, f32[224,128]{1,0:T(8,128)S(1)}, u32[]{:S(2)}, u32[]{:S(2)}) collective-permute-start(f32[224,128]{1,0:T(8,128)S(1)} %add.17), channel_id=1, source_target_pairs={{0,4},{1,5},{2,6},{3,7},{4,0},{5,1},{6,2},{7,3},{8,12},{9,13},{10,... | collective-permute-start | bytes 344072 | tf_op jit(solution)/shard_map/ppermute | solution.py:330
  29.4 7.3 %collective-permute-start.5 = (f32[224,128]{1,0:T(8,128)S(1)}, f32[224,128]{1,0:T(8,128)S(1)}, u32[]{:S(2)}, u32[]{:S(2)}) collective-permute-start(f32[224,128]{1,0:T(8,128)S(1)} %add.18), channel_id=1, source_target_pairs={{0,8},{1,9},{2,10},{3,11},{4,12},{5,13},{6,14},{7,15},{8,0},{9,1},... | collective-permute-start | bytes 344072 | tf_op jit(solution)/shard_map/ppermute | solution.py:330
  36.7 1.4 %collective-permute-start.6 = (f32[224,128]{1,0:T(8,128)S(1)}, f32[224,128]{1,0:T(8,128)S(1)}, u32[]{:S(2)}, u32[]{:S(2)}) collective-permute-start(f32[224,128]{1,0:T(8,128)S(1)} %add.19), channel_id=1, source_target_pairs={{0,16},{16,0},{1,17},{17,1},{2,18},{18,2},{3,19},{19,3},{4,20},{20... | collective-permute-start | bytes 344072 | tf_op jit(solution)/shard_map/ppermute | solution.py:350

commit v3 on v2

--- a/solution.py
+++ b/solution.py
@@ -19,29 +19,6 @@
 
 def cost(flops, size):
     return pl.CostEstimate(flops=int(flops), bytes_accessed=int(size), transcendentals=0)
-
-
-def pack_kernel(count, own, data_ref, cot_ref, *refs):
-    outs, sems = refs[:-1], refs[-1]
-    copies = []
-    for side, out in enumerate(outs):
-        for which, (ref, depth, at) in enumerate(
-            ((data_ref, REACH, 0), (cot_ref, REACH - 2, REACH))
-        ):
-            start = own - depth if side == 0 else 0
-            if count == 2:
-                start = jnp.where(lax.axis_index("gz") == 1, 0, own - depth)
-            copies.append(
-                pltpu.make_async_copy(
-                    ref.at[:, pl.ds(start, depth)],
-                    out.at[:, pl.ds(at, depth)],
-                    sems.at[side, which],
-                )
-            )
-    for copy in copies:
-        copy.start()
-    for copy in copies:
-        copy.wait()
 
 
 def turned(turn_ref, slot, value):
@@ -318,17 +295,41 @@
                     ]
 
 
-def doubled(value, axis, before_last=None):
+def doubled(value, axis):
     count = lax.axis_size(axis)
     if count & (count - 1):
-        value = before_last(value) if before_last else value
         return lax.psum(value, axis)
     step = 1
     while step < count:
-        if before_last and step * 2 == count:
-            value = before_last(value)
         value = value + lax.ppermute(value, axis, [(i, i ^ step) for i in range(count)])
         step *= 2
+    return value
+
+
+def crossed(value, before_last):
+    count = lax.axis_size("dp")
+    if count & (count - 1) or count == 1:
+        return lax.psum(before_last(value), "dp")
+    bits = [1 << k for k in range(count.bit_length() - 1)]
+    groups = [bits[k : k + 2] for k in range(0, len(bits), 2)]
+    partners = [group + [sum(group)] if len(group) == 2 else group for group in groups]
+    turned_order = partners[::-1] if len(partners[-1]) == 3 else partners
+    for phase, pair in enumerate(zip(partners, turned_order)):
+        if phase == len(partners) - 1:
+            value = before_last(value)
+        sent = value.astype(BF16)
+        parts = [sent]
+        for steps in zip(*pair):
+            moves = [
+                (core * count + i, core * count + (i ^ step))
+                for core, step in enumerate(steps)
+                for i in range(count)
+            ]
+            parts.append(lax.ppermute(sent, ("gz", "dp"), moves))
+        parts = [part.astype(F32) for part in parts]
+        while len(parts) > 1:
+            parts = [a + b for a, b in zip(parts[::2], parts[1::2])]
+        value = parts[0]
     return value
 
 
@@ -345,33 +346,35 @@
         first = lax.axis_index("gz") == 0
         mine = jnp.where(first, two, one)
         mine = mine + lax.ppermute(jnp.where(first, one, two), "gz", swap)
-        mine = doubled(mine, "dp", gate)
-        mine, *outs = lax.optimization_barrier((mine, *(outs or finish(grad_fields))))
+        mine = crossed(mine, gate)
+        mine, *outs = lax.optimization_barrier((mine, *outs))
         other = lax.ppermute(mine, "gz", swap)
         return jnp.where(first, other, mine), jnp.where(first, mine, other), outs
-    both = doubled(doubled(jnp.stack([one, two]), "gz"), "dp", gate)
-    return both[0], both[1], outs or finish(grad_fields)
+    both = doubled(doubled(jnp.stack([one, two]), "gz"), "dp")
+    return both[0], both[1], finish(grad_fields)
 
 
 def halo_of(data, cot, count):
     if count == 1:
         return []
-    chan, own, height, width = data.shape
-    sides = 1 if count == 2 else 2
-    hbm = pl.BlockSpec(memory_space=pltpu.HBM)
-    messages = pl.pallas_call(
-        functools.partial(pack_kernel, count, own),
-        out_shape=[jax.ShapeDtypeStruct((chan, 2 * REACH - 2, height, width), BF16)] * sides,
-        in_specs=[hbm, hbm],
-        scratch_shapes=[pltpu.SemaphoreType.DMA((sides, 2))],
-        compiler_params=params(60),
-        name="pack",
-    )(data, cot)
+    own = data.shape[1]
+
+    def ends(low, high):
+        flag = lax.axis_index("gz") == 1
+        parts = []
+        for value, depth in ((data, REACH), (cot, REACH - 2)):
+            first, last = value[:, :depth], value[:, own - depth :]
+            parts.append(jnp.where(flag, first, last) if low and high else first if low else last)
+        return jnp.concatenate(parts, axis=1)
+
     if count == 2:
-        return [lax.ppermute(messages[0], "gz", [(0, 1), (1, 0)])]
+        return [lax.ppermute(ends(True, True), "gz", [(0, 1), (1, 0)])]
     up = [(i, i + 1) for i in range(count - 1)]
     down = [(j, i) for i, j in up]
-    return [lax.ppermute(messages[0], "gz", up), lax.ppermute(messages[1], "gz", down)]
+    return [
+        lax.ppermute(ends(False, True), "gz", up),
+        lax.ppermute(ends(True, False), "gz", down),
+    ]
 
 
 def local(inputs, kernel_one, kernel_two, cotangent):

time: 39.4 us -> 34.9 us (0.89)
  waiting for transfers between devices: 13.4 us -> 9.88 us
  other arithmetic: 0.11 us -> 2.3 us
  Pallas kernels: 14 us -> 12.2 us
  starting transfers between devices: 11 us -> 9.68 us
    ppermute x5 -> x7, waiting for transfers between devices: 11.2 us -> 7.44 us  [the longest x6 7.44 us: crossed(): parts.append(lax.ppermute(sent, ('gz', 'dp'), moves))]
    select_n x0 -> x2, other arithmetic: none -> 2.14 us  [ends(): jnp.where(flag, first, last)]
    pallas_call x1 -> x0, Pallas kernels: 1.83 us -> none  [halo_of(): pl.pallas_call(functools.partial(pack_kernel, count, own), out_shape=[jax...]
    ppermute x5 -> x7, starting transfers between devices: 10.5 us -> 9.35 us  [the longest x6 8.79 us: crossed(): parts.append(lax.ppermute(sent, ('gz', 'dp'), moves))]
  transfers between devices with their start and end apart: 7 -> 9, of which waited for: 7 -> 6; matrix products, arithmetic and copies ran while one was open for 0% -> 0% of each run, Pallas kernels for 10% -> 11%
where the time goes in v3:
time: 34.9 us; the launch traced here: 34.8 us
  Pallas kernels  12.2 us (35%)
  waiting for transfers between devices  9.88 us (28%)
  starting transfers between devices  9.68 us (28%)
  other arithmetic  2.3 us (7%)
  between operations  0.74 us (2%)
    ppermute x6, starting transfers between devices, crossed(): parts.append(lax.ppermute(sent, ('gz', 'dp'), moves))  8.79 us
    ppermute x6, waiting for transfers between devices, crossed(): parts.append(lax.ppermute(sent, ('gz', 'dp'), moves))  7.44 us
    pallas_call x1, Pallas kernels, local(): pl.pallas_call(functools.partial(main_kernel, count, sizes), out_shape=[j...  7.17 us
    pallas_call x1, Pallas kernels, finish(): pl.pallas_call(functools.partial(last_kernel, count, sizes), out_shape=ja...  2.35 us
    select_n x2, other arithmetic, ends(): jnp.where(flag, first, last)  2.14 us
    pallas_call x1, Pallas kernels, local(): pl.pallas_call(functools.partial(prep_kernel, count == 2), out_shape=[jax...  1.49 us
    ppermute x1, waiting for transfers between devices, reduced(): other = lax.ppermute(mine, 'gz', swap)  1.31 us
    pallas_call x1, Pallas kernels, local(): pl.pallas_call(functools.partial(unpack_kernel, 1.0 / math.sqrt(cells)),...  1.14 us
  transfers between devices with their start and end apart: 9, of which 6 were waited for; matrix products, arithmetic and copies ran while one was open for 0% of the time, Pallas kernels for 11%

profile of v3, /device:TPU:0, one launch (start us, length us, event | category | flops | bytes accessed | tf_op | source)
XLA Modules:
  0.0 34.8 jit_solution(6615711685614798275)
XLA Ops:
  0.6 0.0 copy-start
  0.6 0.0 copy-start.3
  0.7 0.0 copy-start.2
  0.7 1.1 %slice_select_fusion.1 = bf16[32,2,8,128]{3,2,1,0:T(8,128)(2,1)S(1)} fusion(bf16[32,8,8,128]{3,2,1,0:T(8,128)(2,1)} %bitcast.9, pred[]{:T(512)S(6)} %eq.7), kind=kLoop, calls=%fused_computation.2 | loop fusion | flops 65536 | bytes 393217 | tf_op jit(solution)/shard_map/jit(_where)/select_n | solution.py:367
  1.7 1.1 %slice_select_fusion = bf16[32,4,8,128]{3,2,1,0:T(8,128)(2,1)S(1)} fusion(bf16[32,8,8,128]{3,2,1,0:T(8,128)(2,1)} %bitcast.7, pred[]{:T(512)S(6)} %eq.7), kind=kLoop, calls=%fused_computation.1 | loop fusion | flops 131072 | bytes 786433 | tf_op jit(solution)/shard_map/jit(_where)/select_n | solution.py:367
  2.9 0.6 %collective-permute-start = (bf16[32,6,8,128]{3,2,1,0:T(8,128)(2,1)S(1)}, bf16[32,6,8,128]{3,2,1,0:T(8,128)(2,1)S(1)}, u32[]{:S(2)}, u32[]{:S(2)}) collective-permute-start(bf16[32,6,8,128]{3,2,1,0:T(8,128)(2,1)S(1)} %pad_maximum_fusion), channel_id=1, source_target_pairs={{0,16},{16,0},{1,17},{17,1},{2,18},{18,2},{3,19},{19,3},{4,20},{20... | collective-permute-start | bytes 1179656 | tf_op jit(solution)/shard_map/ppermute | solution.py:371
  3.4 0.0 copy-done
  3.4 0.0 copy-done.3
  3.4 0.0 copy-done.2
  3.4 0.0 copy-start.1
  3.4 1.5 %prep.1 = (bf16[3,256,768]{2,1,0:T(8,128)(2,1)S(1)}, bf16[3,256,768]{2,1,0:T(8,128)(2,1)S(1)}, bf16[3,256,768]{2,1,0:T(8,128)(2,1)S(1)}, bf16[3,256,768]{2,1,0:T(8,128)(2,1)S(1)}, bf16[768,1024]{1,0:T(8,128)(2,1)S(1)}) custom-call(bf16[32,8,8,128]{3,2,1,0:T(8,128)(2,1)S(1)} %bitcast.8, bf16[3,3,3,32,32]{4,3,2,1,0:T(8,128)(2,1)S(1)} %bitcast.11, ...), custom_call_target="tpu_custom_call" | custom-call | flops 2000000000 | bytes 5000000 | tf_op jit(solution)/shard_map/prep/pallas_call | solution.py:396
  4.9 0.0 collective-permute-done.refs_2_
  4.9 0.0 copy-done.1
  4.9 7.2 %main.1 = (bf16[768,1280]{1,0:T(8,128)(2,1)S(1)}, f32[224,128]{1,0:T(8,128)S(1)}, f32[224,128]{1,0:T(8,128)S(1)}) custom-call(bf16[768,1024]{1,0:T(8,128)(2,1)S(1)} %get-tuple-element.17.refs_0_, bf16[32,8,8,128]{3,2,1,0:T(8,128)(2,1)S(1)} %bitcast.10, bf16[32,6,8,128]{3,2,1,0:T(8,128)(2,1)S(1)} %collective-permute-done.refs_2_, ...), custom_call_target="tpu_custom_call" | custom-call | flops 8000000000 | bytes 8000000 | tf_op jit(solution)/shard_map/main/pallas_call | solution.py:406
  12.1 0.3 collective-permute-start.1
  12.4 1.1 %collective-permute-done.1 = f32[224,128]{1,0:T(8,128)S(1)} collective-permute-done((f32[224,128]{1,0:T(8,128)S(1)}, f32[224,128]{1,0:T(8,128)S(1)}, u32[]{:S(2)}, u32[]{:S(2)}) %collective-permute-start.1) | collective-permute-done | bytes 114720 | tf_op jit(solution)/shard_map/ppermute | solution.py:348
  13.6 3.7 %collective-permute-start.4 = (bf16[224,128]{1,0:T(8,128)(2,1)S(1)}, bf16[224,128]{1,0:T(8,128)(2,1)S(1)}, u32[]{:S(2)}, u32[]{:S(2)}) collective-permute-start(bf16[224,128]{1,0:T(8,128)(2,1)S(1)} %add_convert_fusion), channel_id=1, source_target_pairs={{0,3},{1,2},{2,1},{3,0},{4,7},{5,6},{6,5},{7,4},{8,11},{9,10},{10,... | collective-permute-start | bytes 172040 | tf_op jit(solution)/shard_map/ppermute | solution.py:328
  17.3 0.5 %collective-permute-start.3 = (bf16[224,128]{1,0:T(8,128)(2,1)S(1)}, bf16[224,128]{1,0:T(8,128)(2,1)S(1)}, u32[]{:S(2)}, u32[]{:S(2)}) collective-permute-start(bf16[224,128]{1,0:T(8,128)(2,1)S(1)} %add_convert_fusion), channel_id=1, source_target_pairs={{0,2},{1,3},{2,0},{3,1},{4,6},{5,7},{6,4},{7,5},{8,10},{9,11},{10,... | collective-permute-start | bytes 172040 | tf_op jit(solution)/shard_map/ppermute | solution.py:328
  17.8 0.1 collective-permute-start.2
  17.9 1.5 %collective-permute-done.4 = bf16[224,128]{1,0:T(8,128)(2,1)S(1)} collective-permute-done((bf16[224,128]{1,0:T(8,128)(2,1)S(1)}, bf16[224,128]{1,0:T(8,128)(2,1)S(1)}, u32[]{:S(2)}, u32[]{:S(2)}) %collective-permute-start.4) | collective-permute-done | bytes 57376 | tf_op jit(solution)/shard_map/ppermute | solution.py:328
  19.4 2.0 %collective-permute-done.3 = bf16[224,128]{1,0:T(8,128)(2,1)S(1)} collective-permute-done((bf16[224,128]{1,0:T(8,128)(2,1)S(1)}, bf16[224,128]{1,0:T(8,128)(2,1)S(1)}, u32[]{:S(2)}, u32[]{:S(2)}) %collective-permute-start.3) | collective-permute-done | bytes 57376 | tf_op jit(solution)/shard_map/ppermute | solution.py:328
  21.4 0.5 %collective-permute-done.2 = bf16[224,128]{1,0:T(8,128)(2,1)S(1)} collective-permute-done((bf16[224,128]{1,0:T(8,128)(2,1)S(1)}, bf16[224,128]{1,0:T(8,128)(2,1)S(1)}, u32[]{:S(2)}, u32[]{:S(2)}) %collective-permute-start.2) | collective-permute-done | bytes 57376 | tf_op jit(solution)/shard_map/ppermute | solution.py:328
  22.0 2.7 %collective-permute-start.6 = (bf16[224,128]{1,0:T(8,128)(2,1)S(1)}, bf16[224,128]{1,0:T(8,128)(2,1)S(1)}, u32[]{:S(2)}, u32[]{:S(2)}) collective-permute-start(bf16[224,128]{1,0:T(8,128)(2,1)S(1)} %add_add_fusion.1), channel_id=1, source_target_pairs={{0,8},{1,9},{2,10},{3,11},{4,12},{5,13},{6,14},{7,15},{8,0},{9,1},... | collective-permute-start | bytes 172040 | tf_op jit(solution)/shard_map/ppermute | solution.py:328
  24.6 1.6 %collective-permute-start.5 = (bf16[224,128]{1,0:T(8,128)(2,1)S(1)}, bf16[224,128]{1,0:T(8,128)(2,1)S(1)}, u32[]{:S(2)}, u32[]{:S(2)}) collective-permute-start(bf16[224,128]{1,0:T(8,128)(2,1)S(1)} %add_add_fusion.1), channel_id=1, source_target_pairs={{0,4},{1,5},{2,6},{3,7},{4,0},{5,1},{6,2},{7,3},{8,12},{9,13},{10,... | collective-permute-start | bytes 172040 | tf_op jit(solution)/shard_map/ppermute | solution.py:328
  26.2 0.2 collective-permute-start.7
  26.4 2.4 %last.1 = bf16[32,8,8,128]{3,2,1,0:T(8,128)(2,1)} custom-call(bf16[768,1280]{1,0:T(8,128)(2,1)S(1)} %get-tuple-element.25.grad_field_ref, bf16[3,256,768]{2,1,0:T(8,128)(2,1)S(1)} %get-tuple-element.26.back_one), custom_call_target="tpu_custom_call" | custom-call | flops 2000000000 | bytes 3000000 | tf_op jit(solution)/shard_map/last/pallas_call | solution.py:427
  28.8 0.0 collective-permute-done.6
  28.8 0.0 collective-permute-done.5
  28.8 3.4 %collective-permute-done.7 = bf16[224,128]{1,0:T(8,128)(2,1)S(1)} collective-permute-done((bf16[224,128]{1,0:T(8,128)(2,1)S(1)}, bf16[224,128]{1,0:T(8,128)(2,1)S(1)}, u32[]{:S(2)}, u32[]{:S(2)}) %collective-permute-start.7) | collective-permute-done | bytes 57376 | tf_op jit(solution)/shard_map/ppermute | solution.py:328
  32.2 0.1 collective-permute-start.8
  32.3 1.3 %collective-permute-done.8 = f32[224,128]{1,0:T(8,128)S(1)} collective-permute-done((f32[224,128]{1,0:T(8,128)S(1)}, f32[224,128]{1,0:T(8,128)S(1)}, u32[]{:S(2)}, u32[]{:S(2)}) %collective-permute-start.8) | collective-permute-done | bytes 114720 | tf_op jit(solution)/shard_map/ppermute | solution.py:351
  33.6 1.1 %unpack.1 = (f32[3,3,3,32,32]{4,3,2,1,0:T(8,128)}, f32[3,3,3,32,32]{4,3,2,1,0:T(8,128)}) custom-call(f32[224,128]{1,0:T(8,128)S(1)} %get-tuple-element.32.one_ref, f32[224,128]{1,0:T(8,128)S(1)} %get-tuple-element.31.two_ref), custom_call_target="tpu_custom_call" | custom-call | tf_op jit(solution)/shard_map/unpack/pallas_call | solution.py:440
  (6 shorter events, 0.2 us)
Async XLA Ops:
  0.6 2.8 %copy-start = (bf16[1,32,8,8,128]{4,3,2,1,0:T(8,128)(2,1)S(1)}, bf16[1,32,8,8,128]{4,3,2,1,0:T(8,128)(2,1)}, u32[]{:S(2)}) copy-start(bf16[1,32,8,8,128]{4,3,2,1,0:T(8,128)(2,1)} %param.4) | copy-start | bytes 1572868
  0.6 2.8 %copy-start.3 = (bf16[32,32,3,3,3]{1,0,4,3,2:T(8,128)(2,1)S(1)}, bf16[32,32,3,3,3]{1,0,4,3,2:T(8,128)(2,1)}, u32[]{:S(2)}) copy-start(bf16[32,32,3,3,3]{1,0,4,3,2:T(8,128)(2,1)} %param.6) | copy-start | bytes 165892
  0.7 2.8 %copy-start.2 = (bf16[32,32,3,3,3]{1,0,4,3,2:T(8,128)(2,1)S(1)}, bf16[32,32,3,3,3]{1,0,4,3,2:T(8,128)(2,1)}, u32[]{:S(2)}) copy-start(bf16[32,32,3,3,3]{1,0,4,3,2:T(8,128)(2,1)} %param.5) | copy-start | bytes 165892
  2.9 2.1 %collective-permute-start = (bf16[32,6,8,128]{3,2,1,0:T(8,128)(2,1)S(1)}, bf16[32,6,8,128]{3,2,1,0:T(8,128)(2,1)S(1)}, u32[]{:S(2)}, u32[]{:S(2)}) collective-permute-start(bf16[32,6,8,128]{3,2,1,0:T(8,128)(2,1)S(1)} %pad_maximum_fusion), channel_id=1, source_target_pairs={{0,16},{16,0},{1,17},{17,1},{2,18},{18,2},{3,19},{19,3},{4,20},{20... | collective-permute-start | bytes 1179656 | tf_op jit(solution)/shard_map/ppermute | solution.py:371
  3.4 1.5 %copy-start.1 = (bf16[1,32,8,8,128]{4,3,2,1,0:T(8,128)(2,1)S(1)}, bf16[1,32,8,8,128]{4,3,2,1,0:T(8,128)(2,1)}, u32[]{:S(2)}) copy-start(bf16[1,32,8,8,128]{4,3,2,1,0:T(8,128)(2,1)} %param.7) | copy-start | bytes 1572868
  12.1 1.4 %collective-permute-start.1 = (f32[224,128]{1,0:T(8,128)S(1)}, f32[224,128]{1,0:T(8,128)S(1)}, u32[]{:S(2)}, u32[]{:S(2)}) collective-permute-start(f32[224,128]{1,0:T(8,128)S(1)} %broadcast_select_fusion.2), channel_id=1, source_target_pairs={{0,16},{16,0},{1,17},{17,1},{2,18},{18,2},{3,19},{19,3},{4,20},{20... | collective-permute-start | bytes 344072 | tf_op jit(solution)/shard_map/ppermute | solution.py:348
  13.6 5.9 %collective-permute-start.4 = (bf16[224,128]{1,0:T(8,128)(2,1)S(1)}, bf16[224,128]{1,0:T(8,128)(2,1)S(1)}, u32[]{:S(2)}, u32[]{:S(2)}) collective-permute-start(bf16[224,128]{1,0:T(8,128)(2,1)S(1)} %add_convert_fusion), channel_id=1, source_target_pairs={{0,3},{1,2},{2,1},{3,0},{4,7},{5,6},{6,5},{7,4},{8,11},{9,10},{10,... | collective-permute-start | bytes 172040 | tf_op jit(solution)/shard_map/ppermute | solution.py:328
  17.3 4.2 %collective-permute-start.3 = (bf16[224,128]{1,0:T(8,128)(2,1)S(1)}, bf16[224,128]{1,0:T(8,128)(2,1)S(1)}, u32[]{:S(2)}, u32[]{:S(2)}) collective-permute-start(bf16[224,128]{1,0:T(8,128)(2,1)S(1)} %add_convert_fusion), channel_id=1, source_target_pairs={{0,2},{1,3},{2,0},{3,1},{4,6},{5,7},{6,4},{7,5},{8,10},{9,11},{10,... | collective-permute-start | bytes 172040 | tf_op jit(solution)/shard_map/ppermute | solution.py:328
  17.8 4.2 %collective-permute-start.2 = (bf16[224,128]{1,0:T(8,128)(2,1)S(1)}, bf16[224,128]{1,0:T(8,128)(2,1)S(1)}, u32[]{:S(2)}, u32[]{:S(2)}) collective-permute-start(bf16[224,128]{1,0:T(8,128)(2,1)S(1)} %add_convert_fusion), channel_id=1, source_target_pairs={{0,1},{1,0},{2,3},{3,2},{4,5},{5,4},{6,7},{7,6},{8,9},{9,8},{10,11... | collective-permute-start | bytes 172040 | tf_op jit(solution)/shard_map/ppermute | solution.py:328
  22.0 6.8 %collective-permute-start.6 = (bf16[224,128]{1,0:T(8,128)(2,1)S(1)}, bf16[224,128]{1,0:T(8,128)(2,1)S(1)}, u32[]{:S(2)}, u32[]{:S(2)}) collective-permute-start(bf16[224,128]{1,0:T(8,128)(2,1)S(1)} %add_add_fusion.1), channel_id=1, source_target_pairs={{0,8},{1,9},{2,10},{3,11},{4,12},{5,13},{6,14},{7,15},{8,0},{9,1},... | collective-permute-start | bytes 172040 | tf_op jit(solution)/shard_map/ppermute | solution.py:328
  24.6 4.2 %collective-permute-start.5 = (bf16[224,128]{1,0:T(8,128)(2,1)S(1)}, bf16[224,128]{1,0:T(8,128)(2,1)S(1)}, u32[]{:S(2)}, u32[]{:S(2)}) collective-permute-start(bf16[224,128]{1,0:T(8,128)(2,1)S(1)} %add_add_fusion.1), channel_id=1, source_target_pairs={{0,4},{1,5},{2,6},{3,7},{4,0},{5,1},{6,2},{7,3},{8,12},{9,13},{10,... | collective-permute-start | bytes 172040 | tf_op jit(solution)/shard_map/ppermute | solution.py:328
  26.2 6.0 %collective-permute-start.7 = (bf16[224,128]{1,0:T(8,128)(2,1)S(1)}, bf16[224,128]{1,0:T(8,128)(2,1)S(1)}, u32[]{:S(2)}, u32[]{:S(2)}) collective-permute-start(bf16[224,128]{1,0:T(8,128)(2,1)S(1)} %add_add_fusion.1), channel_id=1, source_target_pairs={{0,12},{1,13},{2,14},{3,15},{4,8},{5,9},{6,10},{7,11},{8,4},{9,5},... | collective-permute-start | bytes 172040 | tf_op jit(solution)/shard_map/ppermute | solution.py:328
  32.2 1.4 %collective-permute-start.8 = (f32[224,128]{1,0:T(8,128)S(1)}, f32[224,128]{1,0:T(8,128)S(1)}, u32[]{:S(2)}, u32[]{:S(2)}) collective-permute-start(f32[224,128]{1,0:T(8,128)S(1)} %add_add_fusion), channel_id=1, source_target_pairs={{0,16},{16,0},{1,17},{17,1},{2,18},{18,2},{3,19},{19,3},{4,20},{20... | collective-permute-start | bytes 344072 | tf_op jit(solution)/shard_map/ppermute | solution.py:351

commit v4 on v3

--- a/solution.py
+++ b/solution.py
@@ -21,6 +21,23 @@
     return pl.CostEstimate(flops=int(flops), bytes_accessed=int(size), transcendentals=0)
 
 
+def pack_kernel(count, own, *refs):
+    sources, near, outs, sems = refs[:4], refs[4:8], refs[8:-1], refs[-1]
+    pairs = []
+    for side, out in enumerate(outs):
+        for ref, depth, at in ((sources[0], REACH, 0), (sources[1], REACH - 2, REACH)):
+            start = own - depth if side == 0 else 0
+            if count == 2:
+                start = jnp.where(lax.axis_index("gz") == 1, 0, own - depth)
+            pairs.append((ref.at[:, pl.ds(start, depth)], out.at[:, pl.ds(at, depth)]))
+    pairs.extend(zip(sources, near))
+    copies = [pltpu.make_async_copy(*pair, sems.at[k]) for k, pair in enumerate(pairs)]
+    for copy in copies:
+        copy.start()
+    for copy in copies:
+        copy.wait()
+
+
 def turned(turn_ref, slot, value):
     chan, height, width = value.shape
     turn_ref[slot] = value.astype(F32).reshape(chan * height, width)
@@ -29,42 +46,68 @@
     )
 
 
+def layout(height):
+    half = height // 2
+    span = half + 1
+    return half, span, (0, half - 1), -(-9 * span // 8) * 8
+
+
 def prep_kernel(mirrored, data_ref, one_ref, two_ref, *refs):
     flip = lax.axis_index("gz") == 1 if mirrored else False
-    outs, field_ref, wide, turn_ref = refs[:4], refs[4], refs[5], refs[6]
+    outs, field_ref, wide_ref, turn_ref = refs[:4], refs[4], refs[5], refs[6]
     chan = one_ref.shape[-1]
-    full = outs[0].shape[1]
-    height = full // chan
-    own, width = data_ref.shape[1], data_ref.shape[-1]
+    own, height, width = data_ref.shape[1:]
+    full = chan * height
     field = Field([(field_ref, 0, own, 0)], full, width)
     for plane in range(own):
         at = jnp.where(flip, own - 1 - plane, plane) if mirrored else plane
         field.put(plane, turned(turn_ref, plane % 2, data_ref[:, at]))
-    lane = lax.broadcasted_iota(jnp.int32, (chan, full), 1)
-    row = lax.broadcasted_iota(jnp.int32, (chan, full), 0)
-    repeat = jnp.where(lax.rem(lane, chan) == row, 1.0, 0.0).astype(BF16)
-    block = lane // chan
+
+    def iota(shape, dim):
+        return lax.broadcasted_iota(jnp.int32, shape, dim)
+
+    tile = 4 * chan
+    same = lax.rem(iota((chan, tile), 1), chan) == iota((chan, tile), 0)
+    repeat = jnp.where(same, 1.0, 0.0).astype(BF16)
+    unit = jnp.where(iota((chan, chan), 0) == iota((chan, chan), 1), 1.0, 0.0).astype(BF16)
+    row, lane = iota((tile, 4 * tile), 0), iota((tile, 4 * tile), 1)
+    chosen = (row // chan == lane // tile) & (lax.rem(row, chan) == lax.rem(lane, chan))
+    choose = jnp.where(chosen, 1.0, 0.0).astype(BF16)
+    group = iota((chan, tile), 1) // chan
+    half, span, lows, blocks = layout(height)
     for index, ref in enumerate((one_ref, two_ref)):
-        forward, backward = outs[2 * index], outs[2 * index + 1]
         flat = ref[...].reshape(27 * chan, chan)
         spread = jnp.dot(flat, repeat, preferred_element_type=F32)
-        wide[...] = spread.reshape(3, 9 * chan, full)
-        for dz in range(3):
-            source = jnp.where(flip, 2 - dz, dz) if mirrored else dz
-            for dx in range(3):
-                taps = [
-                    wide[source, (dy * 3 + dx) * chan : (dy * 3 + dx + 1) * chan, :]
-                    for dy in range(3)
-                ]
-                strips = []
-                for y in range(height):
-                    strip = jnp.zeros((chan, full), F32)
-                    for dy in range(3):
-                        strip = jnp.where(block == y + dy - 1, taps[dy], strip)
-                    strips.append(strip.astype(BF16))
-                tile = jnp.concatenate(strips, axis=0)
-                forward[dz, :, dx * full : (dx + 1) * full] = tile
-                backward[2 - dz, :, (2 - dx) * full : (3 - dx) * full] = tile.T
+        wide_ref[2 * index] = spread.reshape(3, 9 * chan, tile)
+        flat = jnp.concatenate([flat, jnp.zeros((chan, chan), BF16)], axis=0)
+        across = lax.dot_general(unit, flat, NT, preferred_element_type=F32).astype(BF16)
+        stacked = jnp.concatenate([across[:, t * tile : (t + 1) * tile] for t in range(7)], axis=0)
+        spread = jnp.dot(stacked, choose, preferred_element_type=F32)
+        for tap in range(27):
+            at, column = tap // 4 * chan, tap % 4 * tile
+            wide_ref[2 * index + 1, tap // 9, tap % 9 * chan : (tap % 9 + 1) * chan] = spread[
+                at : at + chan, column : column + tile
+            ]
+    for which, out in enumerate(outs):
+        back = which % 2
+        for part, low in enumerate(lows):
+            for y in range(half):
+                for first in range(0, blocks, 4):
+                    strip = jnp.zeros((chan, tile), F32)
+                    for block in range(first, min(first + 4, 9 * span)):
+                        dz, dx = block // (3 * span), block // span % 3
+                        dy = low + block % span - (part * half + y) + 1
+                        if not 0 <= dy < 3:
+                            continue
+                        if back:
+                            dz, dy, dx = 2 - dz, 2 - dy, 2 - dx
+                        source = jnp.where(flip, 2 - dz, dz) if mirrored else dz
+                        at = (dy * 3 + dx) * chan
+                        tap = wide_ref[which, source, at : at + chan, :]
+                        strip = jnp.where(group == block - first, tap, strip)
+                    out[part, y * chan : (y + 1) * chan, first * chan : first * chan + tile] = (
+                        strip.astype(BF16)
+                    )
 
 
 class Field:
@@ -100,13 +143,24 @@
         ref, lanes, _ = self.run(plane, 1)
         ref[:, lanes] = jnp.zeros((3 * self.full, self.width), BF16)
 
-    def convolve(self, band, first, count):
-        total = None
-        for dz in range(3):
-            window = self.take(slice(None), first + dz - 1, count)
-            piece = jnp.dot(band[dz], window, preferred_element_type=F32)
-            total = piece if total is None else total + piece
-        return total
+    def convolve(self, band, first, count, chan):
+        half, span, lows, blocks = layout(self.full // chan)
+        out = []
+        for part, low in enumerate(lows):
+            windows = [
+                self.take(
+                    slice(dx * self.full + low * chan, dx * self.full + (low + span) * chan),
+                    first + dz - 1,
+                    count,
+                )
+                for dz in range(3)
+                for dx in range(3)
+            ]
+            if blocks > 9 * span:
+                windows.append(self.take(slice(0, (blocks - 9 * span) * chan), first, count))
+            window = jnp.concatenate(windows, axis=0)
+            out.append(jnp.dot(band[part], window, preferred_element_type=F32))
+        return jnp.concatenate(out, axis=0)
 
 
 def spans(low, high):
@@ -225,7 +279,7 @@
     hidden = field(h_ref, REACH - 1)
     slope_low, slope_high = reach(1)
     for first, number in spans(*reach(REACH - 1)):
-        pre = data.convolve(band_one, first, number)
+        pre = data.convolve(band_one, first, number, chan)
         for step in range(number):
             plane = first + step
             value = pre[:, step * width : (step + 1) * width]
@@ -237,7 +291,7 @@
 
     upper = field(g_ref, REACH - 2)
     for first, number in spans(*reach(REACH - 2)):
-        pre = hidden.convolve(band_two, first, number)
+        pre = hidden.convolve(band_two, first, number, chan)
         for step in range(number):
             plane = first + step
             value = pre[:, step * width : (step + 1) * width]
@@ -248,7 +302,7 @@
 
     lower = field(grad_field_ref, REACH - 3)
     for first, number in spans(*reach(REACH - 3)):
-        back = upper.convolve(back_two, first, number)
+        back = upper.convolve(back_two, first, number, chan)
         for step in range(number):
             plane = first + step
             at = (plane - slope_low) * width
@@ -269,7 +323,7 @@
     flip = lax.axis_index("gz") == 1 if mirrored else None
     lower = Field([(grad_field_ref, -1, own + 2, 0)], full, width)
     for first, number in spans(0, own):
-        out = lower.convolve(back_one, first, number)
+        out = lower.convolve(back_one, first, number, chan)
         for step in range(number):
             plane = first + step
             value = out[:, step * width : (step + 1) * width]
@@ -310,26 +364,19 @@
     count = lax.axis_size("dp")
     if count & (count - 1) or count == 1:
         return lax.psum(before_last(value), "dp")
-    bits = [1 << k for k in range(count.bit_length() - 1)]
-    groups = [bits[k : k + 2] for k in range(0, len(bits), 2)]
-    partners = [group + [sum(group)] if len(group) == 2 else group for group in groups]
-    turned_order = partners[::-1] if len(partners[-1]) == 3 else partners
-    for phase, pair in enumerate(zip(partners, turned_order)):
-        if phase == len(partners) - 1:
+    steps = [1 << k for k in range(count.bit_length() - 1)]
+    half = len(steps) // 2
+    other = steps[half:] + steps[:half]
+    for phase, pair in enumerate(zip(other, steps)):
+        if phase == len(steps) - 1:
             value = before_last(value)
         sent = value.astype(BF16)
-        parts = [sent]
-        for steps in zip(*pair):
-            moves = [
-                (core * count + i, core * count + (i ^ step))
-                for core, step in enumerate(steps)
-                for i in range(count)
-            ]
-            parts.append(lax.ppermute(sent, ("gz", "dp"), moves))
-        parts = [part.astype(F32) for part in parts]
-        while len(parts) > 1:
-            parts = [a + b for a, b in zip(parts[::2], parts[1::2])]
-        value = parts[0]
+        moves = [
+            (core * count + i, core * count + (i ^ step))
+            for core, step in enumerate(pair)
+            for i in range(count)
+        ]
+        value = sent.astype(F32) + lax.ppermute(sent, ("gz", "dp"), moves).astype(F32)
     return value
 
 
@@ -354,27 +401,29 @@
     return both[0], both[1], finish(grad_fields)
 
 
-def halo_of(data, cot, count):
-    if count == 1:
-        return []
-    own = data.shape[1]
-
-    def ends(low, high):
-        flag = lax.axis_index("gz") == 1
-        parts = []
-        for value, depth in ((data, REACH), (cot, REACH - 2)):
-            first, last = value[:, :depth], value[:, own - depth :]
-            parts.append(jnp.where(flag, first, last) if low and high else first if low else last)
-        return jnp.concatenate(parts, axis=1)
-
+def gathered(count, data, cot, *taps):
+    chan, own, height, width = data.shape
+    sides = min(count - 1, 2)
+    arrays = (data, cot, *taps)
+    far = [pltpu.with_memory_space_constraint(value, pltpu.HBM) for value in arrays]
+    shapes = [value.shape for value in arrays]
+    shapes += [(chan, 2 * REACH - 2, height, width)] * sides
+    near = pl.pallas_call(
+        functools.partial(pack_kernel, count, own),
+        out_shape=[pltpu.VMEM(shape, BF16) for shape in shapes],
+        in_specs=[pl.BlockSpec(memory_space=pltpu.HBM)] * 4,
+        out_specs=[pl.BlockSpec(memory_space=pltpu.VMEM)] * len(shapes),
+        scratch_shapes=[pltpu.SemaphoreType.DMA((4 + 2 * sides,))],
+        compiler_params=params(4),
+        name="pack",
+    )(*far)
+    messages = near[4:]
     if count == 2:
-        return [lax.ppermute(ends(True, True), "gz", [(0, 1), (1, 0)])]
-    up = [(i, i + 1) for i in range(count - 1)]
-    down = [(j, i) for i, j in up]
-    return [
-        lax.ppermute(ends(False, True), "gz", up),
-        lax.ppermute(ends(True, False), "gz", down),
-    ]
+        moves = [[(0, 1), (1, 0)]]
+    else:
+        up = [(i, i + 1) for i in range(count - 1)]
+        moves = [up, [(j, i) for i, j in up]]
+    return near[:4], [lax.ppermute(item, "gz", move) for item, move in zip(messages, moves)]
 
 
 def local(inputs, kernel_one, kernel_two, cotangent):
@@ -385,23 +434,24 @@
     sizes = (chan, own, height, width, low_side, high_side)
     taps = [jnp.transpose(k, (2, 3, 4, 0, 1)) for k in (kernel_one, kernel_two)]
     turn = pltpu.VMEM((2, full, width), F32)
+    half, _, _, blocks = layout(height)
 
     def stack(depth):
         return (3 * full, slots(sizes, depth) * width)
 
     grad_fields, backs, ones, twos = [], [], [], []
     for sample in range(batch):
-        data, cot = inputs[sample], cotangent[sample]
-        halos = halo_of(data, cot, count)
+        near, halos = gathered(count, inputs[sample], cotangent[sample], *taps)
+        data, cot, *near_taps = near
         *bands, field = pl.pallas_call(
             functools.partial(prep_kernel, count == 2),
-            out_shape=[jax.ShapeDtypeStruct((3, full, 3 * full), BF16)] * 4
+            out_shape=[jax.ShapeDtypeStruct((2, half * chan, blocks * chan), BF16)] * 4
             + [jax.ShapeDtypeStruct((3 * full, own * width), BF16)],
-            scratch_shapes=[pltpu.VMEM((3, 9 * chan, full), F32), turn],
+            scratch_shapes=[pltpu.VMEM((4, 3, 9 * chan, 4 * chan), F32), turn],
             compiler_params=params(16),
             cost_estimate=cost(2e9, 5e6),
             name="prep",
-        )(data, *taps)
+        )(data, *near_taps)
         term = jax.ShapeDtypeStruct((7 * chan, 4 * chan), F32)
         grad_field, term_one, term_two = pl.pallas_call(
             functools.partial(main_kernel, count, sizes),

time: 34.9 us -> 33.2 us (0.951)
  other arithmetic: 2.3 us -> 0.13 us
  starting transfers between devices: 9.68 us -> 10.7 us
  waiting for transfers between devices: 9.88 us -> 9.47 us
    select_n x2 -> x0, other arithmetic: 2.14 us -> none  [ends(): jnp.where(flag, first, last)]
    pallas_call x0 -> x1, Pallas kernels: none -> 1.53 us  [gathered(): pl.pallas_call(functools.partial(pack_kernel, count, own), out_shape=[plt...]
    pallas_call x1, Pallas kernels: 7.17 us -> 6.03 us  [local(): pl.pallas_call(functools.partial(main_kernel, count, sizes), out_shape=[j...]
    ppermute x7 -> x5, starting transfers between devices: 9.35 us -> 10.3 us  [the longest x4 9.78 us: crossed(): lax.ppermute(sent, ('gz', 'dp'), moves).astype(F32)]
    pallas_call x1, Pallas kernels: 2.35 us -> 1.92 us  [finish(): pl.pallas_call(functools.partial(last_kernel, count, sizes), out_shape=ja...]
    ppermute x7 -> x5, waiting for transfers between devices: 7.44 us -> 7.06 us  [the longest x4 7.05 us: crossed(): lax.ppermute(sent, ('gz', 'dp'), moves).astype(F32)]
  transfers between devices with their start and end apart: 9 -> 7, of which waited for: 6 -> 6; matrix products, arithmetic and copies ran while one was open for 0% -> 0% of each run, Pallas kernels for 11% -> 10%
where the time goes in v4:
time: 33.2 us; the launch traced here: 33.1 us
  Pallas kernels  12.1 us (36%)
  starting transfers between devices  10.7 us (32%)
  waiting for transfers between devices  9.47 us (29%)
  between operations  0.7 us (2%)
    ppermute x4, starting transfers between devices, crossed(): lax.ppermute(sent, ('gz', 'dp'), moves).astype(F32)  9.78 us
    ppermute x4, waiting for transfers between devices, crossed(): lax.ppermute(sent, ('gz', 'dp'), moves).astype(F32)  7.05 us
    pallas_call x1, Pallas kernels, local(): pl.pallas_call(functools.partial(main_kernel, count, sizes), out_shape=[j...  6.03 us
    pallas_call x1, Pallas kernels, finish(): pl.pallas_call(functools.partial(last_kernel, count, sizes), out_shape=ja...  1.92 us
    pallas_call x1, Pallas kernels, gathered(): pl.pallas_call(functools.partial(pack_kernel, count, own), out_shape=[plt...  1.53 us
    pallas_call x1, Pallas kernels, local(): pl.pallas_call(functools.partial(prep_kernel, count == 2), out_shape=[jax...  1.47 us
    ppermute x1, waiting for transfers between devices, reduced(): other = lax.ppermute(mine, 'gz', swap)  1.31 us
    pallas_call x1, Pallas kernels, local(): pl.pallas_call(functools.partial(unpack_kernel, 1.0 / math.sqrt(cells)),...  1.14 us
  transfers between devices with their start and end apart: 7, of which 6 were waited for; matrix products, arithmetic and copies ran while one was open for 0% of the time, Pallas kernels for 10%

profile of v4, /device:TPU:0, one launch (start us, length us, event | category | flops | bytes accessed | tf_op | source)
XLA Modules:
  0.0 33.1 jit_solution(5754353569970464391)
XLA Ops:
  0.6 1.5 %pack.1 = (bf16[32,8,8,128]{3,2,1,0:T(8,128)(2,1)S(1)}, bf16[32,8,8,128]{3,2,1,0:T(8,128)(2,1)S(1)}, bf16[3,3,3,32,32]{4,3,2,1,0:T(8,128)(2,1)S(1)}, bf16[3,3,3,...) custom-call(bf16[32,8,8,128]{3,2,1,0:T(8,128)(2,1)} %bitcast.7, bf16[32,8,8,128]{3,2,1,0:T(8,128)(2,1)} %bitcast.8, ...), custom_call_target="tpu_custom_call" | custom-call | tf_op jit(solution)/shard_map/pack/pallas_call | solution.py:411
  2.2 0.6 %collective-permute-start = (bf16[32,6,8,128]{3,2,1,0:T(8,128)(2,1)S(1)}, bf16[32,6,8,128]{3,2,1,0:T(8,128)(2,1)S(1)}, u32[]{:S(2)}, u32[]{:S(2)}) collective-permute-start(bf16[32,6,8,128]{3,2,1,0:T(8,128)(2,1)S(1)} %get-tuple-element.27), channel_id=1, source_target_pairs={{0,16},{16,0},{1,17},{17,1},{2,18},{18,2},{3,19},{19,3},{4,20},{20... | collective-permute-start | bytes 1179656 | tf_op jit(solution)/shard_map/ppermute | solution.py:426
  2.7 1.5 %prep.1 = (bf16[2,128,1536]{2,1,0:T(8,128)(2,1)S(1)}, bf16[2,128,1536]{2,1,0:T(8,128)(2,1)S(1)}, bf16[2,128,1536]{2,1,0:T(8,128)(2,1)S(1)}, bf16[2,128,1536]{2,1,0:T(8,128)(2,1)S(1)}, bf16[768,1024]{1,0:T(8,128)(2,1)S(1)}) custom-call(bf16[32,8,8,128]{3,2,1,0:T(8,128)(2,1)S(1)} %get-tuple-element.22.data_ref, ...), custom_call_target="tpu_custom_call" | custom-call | flops 2000000000 | bytes 5000000 | tf_op jit(solution)/shard_map/prep/pallas_call | solution.py:446
  4.2 0.0 collective-permute-done.refs_2_
  4.2 6.0 %main.1 = (bf16[768,1280]{1,0:T(8,128)(2,1)S(1)}, f32[224,128]{1,0:T(8,128)S(1)}, f32[224,128]{1,0:T(8,128)S(1)}) custom-call(bf16[768,1024]{1,0:T(8,128)(2,1)S(1)} %get-tuple-element.25.refs_0_, bf16[32,8,8,128]{3,2,1,0:T(8,128)(2,1)S(1)} %get-tuple-element.26.refs_1_, bf16[32,6,8,128]{3,2,1,0:T(8,128)(2,1)S(1)} %collective-permute-done.refs_2_, ...), custom_call_target="tpu_custom_call" | custom-call | flops 8000000000 | bytes 8000000 | tf_op jit(solution)/shard_map/main/pallas_call | solution.py:456
  10.3 0.3 collective-permute-start.1
  10.6 1.1 %collective-permute-done.1 = f32[224,128]{1,0:T(8,128)S(1)} collective-permute-done((f32[224,128]{1,0:T(8,128)S(1)}, f32[224,128]{1,0:T(8,128)S(1)}, u32[]{:S(2)}, u32[]{:S(2)}) %collective-permute-start.1) | collective-permute-done | bytes 114720 | tf_op jit(solution)/shard_map/ppermute | solution.py:395
  11.7 2.9 %collective-permute-start.2 = (bf16[224,128]{1,0:T(8,128)(2,1)S(1)}, bf16[224,128]{1,0:T(8,128)(2,1)S(1)}, u32[]{:S(2)}, u32[]{:S(2)}) collective-permute-start(bf16[224,128]{1,0:T(8,128)(2,1)S(1)} %add_convert_fusion.2), channel_id=1, source_target_pairs={{0,4},{1,5},{2,6},{3,7},{4,0},{5,1},{6,2},{7,3},{8,12},{9,13},{10,... | collective-permute-start | bytes 172040 | tf_op jit(solution)/shard_map/ppermute | solution.py:379
  14.5 2.2 %collective-permute-done.2 = bf16[224,128]{1,0:T(8,128)(2,1)S(1)} collective-permute-done((bf16[224,128]{1,0:T(8,128)(2,1)S(1)}, bf16[224,128]{1,0:T(8,128)(2,1)S(1)}, u32[]{:S(2)}, u32[]{:S(2)}) %collective-permute-start.2) | collective-permute-done | bytes 57376 | tf_op jit(solution)/shard_map/ppermute | solution.py:379
  16.7 3.1 %collective-permute-start.3 = (bf16[224,128]{1,0:T(8,128)(2,1)S(1)}, bf16[224,128]{1,0:T(8,128)(2,1)S(1)}, u32[]{:S(2)}, u32[]{:S(2)}) collective-permute-start(bf16[224,128]{1,0:T(8,128)(2,1)S(1)} %add_convert_fusion.1), channel_id=1, source_target_pairs={{0,8},{1,9},{2,10},{3,11},{4,12},{5,13},{6,14},{7,15},{8,0},{9,1},... | collective-permute-start | bytes 172040 | tf_op jit(solution)/shard_map/ppermute | solution.py:379
  19.8 2.2 %collective-permute-done.3 = bf16[224,128]{1,0:T(8,128)(2,1)S(1)} collective-permute-done((bf16[224,128]{1,0:T(8,128)(2,1)S(1)}, bf16[224,128]{1,0:T(8,128)(2,1)S(1)}, u32[]{:S(2)}, u32[]{:S(2)}) %collective-permute-start.3) | collective-permute-done | bytes 57376 | tf_op jit(solution)/shard_map/ppermute | solution.py:379
  22.0 1.9 %collective-permute-start.4 = (bf16[224,128]{1,0:T(8,128)(2,1)S(1)}, bf16[224,128]{1,0:T(8,128)(2,1)S(1)}, u32[]{:S(2)}, u32[]{:S(2)}) collective-permute-start(bf16[224,128]{1,0:T(8,128)(2,1)S(1)} %add_convert_fusion), channel_id=1, source_target_pairs={{0,1},{1,0},{2,3},{3,2},{4,5},{5,4},{6,7},{7,6},{8,9},{9,8},{10,11... | collective-permute-start | bytes 172040 | tf_op jit(solution)/shard_map/ppermute | solution.py:379
  23.9 2.3 %collective-permute-done.4 = bf16[224,128]{1,0:T(8,128)(2,1)S(1)} collective-permute-done((bf16[224,128]{1,0:T(8,128)(2,1)S(1)}, bf16[224,128]{1,0:T(8,128)(2,1)S(1)}, u32[]{:S(2)}, u32[]{:S(2)}) %collective-permute-start.4) | collective-permute-done | bytes 57376 | tf_op jit(solution)/shard_map/ppermute | solution.py:379
  26.3 1.9 %collective-permute-start.5 = (bf16[224,128]{1,0:T(8,128)(2,1)S(1)}, bf16[224,128]{1,0:T(8,128)(2,1)S(1)}, u32[]{:S(2)}, u32[]{:S(2)}) collective-permute-start(bf16[224,128]{1,0:T(8,128)(2,1)S(1)} %convert_add_fusion.1), channel_id=1, source_target_pairs={{0,2},{1,3},{2,0},{3,1},{4,6},{5,7},{6,4},{7,5},{8,10},{9,11},{10,... | collective-permute-start | bytes 172040 | tf_op jit(solution)/shard_map/ppermute | solution.py:379
  28.2 1.9 %last.1 = bf16[32,8,8,128]{3,2,1,0:T(8,128)(2,1)} custom-call(bf16[768,1280]{1,0:T(8,128)(2,1)S(1)} %get-tuple-element.35.grad_field_ref, bf16[2,128,1536]{2,1,0:T(8,128)(2,1)S(1)} %get-tuple-element.36.back_one), custom_call_target="tpu_custom_call" | custom-call | flops 2000000000 | bytes 3000000 | tf_op jit(solution)/shard_map/last/pallas_call | solution.py:477
  30.1 0.4 %collective-permute-done.5 = bf16[224,128]{1,0:T(8,128)(2,1)S(1)} collective-permute-done((bf16[224,128]{1,0:T(8,128)(2,1)S(1)}, bf16[224,128]{1,0:T(8,128)(2,1)S(1)}, u32[]{:S(2)}, u32[]{:S(2)}) %collective-permute-start.5) | collective-permute-done | bytes 57376 | tf_op jit(solution)/shard_map/ppermute | solution.py:379
  30.5 0.1 collective-permute-start.6
  30.6 1.3 %collective-permute-done.6 = f32[224,128]{1,0:T(8,128)S(1)} collective-permute-done((f32[224,128]{1,0:T(8,128)S(1)}, f32[224,128]{1,0:T(8,128)S(1)}, u32[]{:S(2)}, u32[]{:S(2)}) %collective-permute-start.6) | collective-permute-done | bytes 114720 | tf_op jit(solution)/shard_map/ppermute | solution.py:398
  32.0 1.1 %unpack.1 = (f32[3,3,3,32,32]{4,3,2,1,0:T(8,128)}, f32[3,3,3,32,32]{4,3,2,1,0:T(8,128)}) custom-call(f32[224,128]{1,0:T(8,128)S(1)} %get-tuple-element.42.one_ref, f32[224,128]{1,0:T(8,128)S(1)} %get-tuple-element.41.two_ref), custom_call_target="tpu_custom_call" | custom-call | tf_op jit(solution)/shard_map/unpack/pallas_call | solution.py:490
  (7 shorter events, 0.1 us)
Async XLA Ops:
  2.2 2.0 %collective-permute-start = (bf16[32,6,8,128]{3,2,1,0:T(8,128)(2,1)S(1)}, bf16[32,6,8,128]{3,2,1,0:T(8,128)(2,1)S(1)}, u32[]{:S(2)}, u32[]{:S(2)}) collective-permute-start(bf16[32,6,8,128]{3,2,1,0:T(8,128)(2,1)S(1)} %get-tuple-element.27), channel_id=1, source_target_pairs={{0,16},{16,0},{1,17},{17,1},{2,18},{18,2},{3,19},{19,3},{4,20},{20... | collective-permute-start | bytes 1179656 | tf_op jit(solution)/shard_map/ppermute | solution.py:426
  10.3 1.4 %collective-permute-start.1 = (f32[224,128]{1,0:T(8,128)S(1)}, f32[224,128]{1,0:T(8,128)S(1)}, u32[]{:S(2)}, u32[]{:S(2)}) collective-permute-start(f32[224,128]{1,0:T(8,128)S(1)} %broadcast_select_fusion.2), channel_id=1, source_target_pairs={{0,16},{16,0},{1,17},{17,1},{2,18},{18,2},{3,19},{19,3},{4,20},{20... | collective-permute-start | bytes 344072 | tf_op jit(solution)/shard_map/ppermute | solution.py:395
  11.7 5.0 %collective-permute-start.2 = (bf16[224,128]{1,0:T(8,128)(2,1)S(1)}, bf16[224,128]{1,0:T(8,128)(2,1)S(1)}, u32[]{:S(2)}, u32[]{:S(2)}) collective-permute-start(bf16[224,128]{1,0:T(8,128)(2,1)S(1)} %add_convert_fusion.2), channel_id=1, source_target_pairs={{0,4},{1,5},{2,6},{3,7},{4,0},{5,1},{6,2},{7,3},{8,12},{9,13},{10,... | collective-permute-start | bytes 172040 | tf_op jit(solution)/shard_map/ppermute | solution.py:379
  16.7 5.3 %collective-permute-start.3 = (bf16[224,128]{1,0:T(8,128)(2,1)S(1)}, bf16[224,128]{1,0:T(8,128)(2,1)S(1)}, u32[]{:S(2)}, u32[]{:S(2)}) collective-permute-start(bf16[224,128]{1,0:T(8,128)(2,1)S(1)} %add_convert_fusion.1), channel_id=1, source_target_pairs={{0,8},{1,9},{2,10},{3,11},{4,12},{5,13},{6,14},{7,15},{8,0},{9,1},... | collective-permute-start | bytes 172040 | tf_op jit(solution)/shard_map/ppermute | solution.py:379
  22.0 4.2 %collective-permute-start.4 = (bf16[224,128]{1,0:T(8,128)(2,1)S(1)}, bf16[224,128]{1,0:T(8,128)(2,1)S(1)}, u32[]{:S(2)}, u32[]{:S(2)}) collective-permute-start(bf16[224,128]{1,0:T(8,128)(2,1)S(1)} %add_convert_fusion), channel_id=1, source_target_pairs={{0,1},{1,0},{2,3},{3,2},{4,5},{5,4},{6,7},{7,6},{8,9},{9,8},{10,11... | collective-permute-start | bytes 172040 | tf_op jit(solution)/shard_map/ppermute | solution.py:379
  26.3 4.2 %collective-permute-start.5 = (bf16[224,128]{1,0:T(8,128)(2,1)S(1)}, bf16[224,128]{1,0:T(8,128)(2,1)S(1)}, u32[]{:S(2)}, u32[]{:S(2)}) collective-permute-start(bf16[224,128]{1,0:T(8,128)(2,1)S(1)} %convert_add_fusion.1), channel_id=1, source_target_pairs={{0,2},{1,3},{2,0},{3,1},{4,6},{5,7},{6,4},{7,5},{8,10},{9,11},{10,... | collective-permute-start | bytes 172040 | tf_op jit(solution)/shard_map/ppermute | solution.py:379
  30.5 1.4 %collective-permute-start.6 = (f32[224,128]{1,0:T(8,128)S(1)}, f32[224,128]{1,0:T(8,128)S(1)}, u32[]{:S(2)}, u32[]{:S(2)}) collective-permute-start(f32[224,128]{1,0:T(8,128)S(1)} %convert_add_fusion), channel_id=1, source_target_pairs={{0,16},{16,0},{1,17},{17,1},{2,18},{18,2},{3,19},{19,3},{4,20},{20... | collective-permute-start | bytes 344072 | tf_op jit(solution)/shard_map/ppermute | solution.py:398

commit v5 on v4

--- a/solution.py
+++ b/solution.py
@@ -360,22 +360,24 @@
     return value
 
 
+def odd(index):
+    return bin(index).count("1") % 2
+
+
 def crossed(value, before_last):
     count = lax.axis_size("dp")
-    if count & (count - 1) or count == 1:
-        return lax.psum(before_last(value), "dp")
     steps = [1 << k for k in range(count.bit_length() - 1)]
     half = len(steps) // 2
-    other = steps[half:] + steps[:half]
-    for phase, pair in enumerate(zip(other, steps)):
+    orders = (steps[half:] + steps[:half], steps)
+    for phase in range(len(steps)):
         if phase == len(steps) - 1:
             value = before_last(value)
         sent = value.astype(BF16)
-        moves = [
-            (core * count + i, core * count + (i ^ step))
-            for core, step in enumerate(pair)
-            for i in range(count)
-        ]
+        moves = []
+        for core in range(2):
+            for chip in range(count):
+                step = orders[core ^ odd(chip)][phase]
+                moves.append((core * count + chip, (1 - core) * count + (chip ^ step)))
         value = sent.astype(F32) + lax.ppermute(sent, ("gz", "dp"), moves).astype(F32)
     return value
 
@@ -388,9 +390,11 @@
         outs.extend(finish(held))
         return value
 
-    if lax.axis_size("gz") == 2:
+    count = lax.axis_size("dp")
+    if lax.axis_size("gz") == 2 and count > 1 and count & (count - 1) == 0:
         swap = [(0, 1), (1, 0)]
-        first = lax.axis_index("gz") == 0
+        turns = lax.population_count(lax.axis_index("dp")) + lax.axis_index("gz")
+        first = turns % 2 == 0
         mine = jnp.where(first, two, one)
         mine = mine + lax.ppermute(jnp.where(first, one, two), "gz", swap)
         mine = crossed(mine, gate)

time: 33.2 us -> 31.4 us (0.946)
  waiting for transfers between devices: 9.47 us -> 7.93 us
  starting transfers between devices: 10.7 us -> 10.2 us
    ppermute x4, waiting for transfers between devices: 7.05 us -> 5.86 us  [crossed(): lax.ppermute(sent, ('gz', 'dp'), moves).astype(F32)]
    ppermute x4, starting transfers between devices: 9.78 us -> 8.82 us  [crossed(): lax.ppermute(sent, ('gz', 'dp'), moves).astype(F32)]
    ppermute x1, starting transfers between devices: 0.07 us -> 0.49 us  [reduced(): other = lax.ppermute(mine, 'gz', swap)]
    ppermute x1, waiting for transfers between devices: 1.31 us -> 0.97 us  [reduced(): other = lax.ppermute(mine, 'gz', swap)]
  transfers between devices with their start and end apart: 7 -> 7, of which waited for: 6 -> 6; matrix products, arithmetic and copies ran while one was open for 0% -> 0% of each run, Pallas kernels for 10% -> 11%
where the time goes in v5:
time: 31.4 us; the launch traced here: 31 us
  Pallas kernels  12.1 us (39%)
  starting transfers between devices  10.2 us (32%)
  waiting for transfers between devices  7.93 us (25%)
  between operations  0.7 us (2%)
    ppermute x4, starting transfers between devices, crossed(): lax.ppermute(sent, ('gz', 'dp'), moves).astype(F32)  8.82 us
    pallas_call x1, Pallas kernels, local(): pl.pallas_call(functools.partial(main_kernel, count, sizes), out_shape=[j...  6.03 us
    ppermute x4, waiting for transfers between devices, crossed(): lax.ppermute(sent, ('gz', 'dp'), moves).astype(F32)  5.86 us
    pallas_call x1, Pallas kernels, finish(): pl.pallas_call(functools.partial(last_kernel, count, sizes), out_shape=ja...  1.92 us
    pallas_call x1, Pallas kernels, gathered(): pl.pallas_call(functools.partial(pack_kernel, count, own), out_shape=[plt...  1.53 us
    pallas_call x1, Pallas kernels, local(): pl.pallas_call(functools.partial(prep_kernel, count == 2), out_shape=[jax...  1.47 us
    pallas_call x1, Pallas kernels, local(): pl.pallas_call(functools.partial(unpack_kernel, 1.0 / math.sqrt(cells)),...  1.14 us
    ppermute x1, waiting for transfers between devices, reduced(): mine = mine + lax.ppermute(jnp.where(first, one, two), 'gz', swap)  1.11 us
  transfers between devices with their start and end apart: 7, of which 6 were waited for; matrix products, arithmetic and copies ran while one was open for 0% of the time, Pallas kernels for 11%

profile of v5, /device:TPU:0, one launch (start us, length us, event | category | flops | bytes accessed | tf_op | source)
XLA Modules:
  0.0 31.0 jit_solution(10877977356499631919)
XLA Ops:
  0.6 1.5 %pack.1 = (bf16[32,8,8,128]{3,2,1,0:T(8,128)(2,1)S(1)}, bf16[32,8,8,128]{3,2,1,0:T(8,128)(2,1)S(1)}, bf16[3,3,3,32,32]{4,3,2,1,0:T(8,128)(2,1)S(1)}, bf16[3,3,3,...) custom-call(bf16[32,8,8,128]{3,2,1,0:T(8,128)(2,1)} %bitcast.7, bf16[32,8,8,128]{3,2,1,0:T(8,128)(2,1)} %bitcast.8, ...), custom_call_target="tpu_custom_call" | custom-call | tf_op jit(solution)/shard_map/pack/pallas_call | solution.py:415
  2.2 0.6 %collective-permute-start = (bf16[32,6,8,128]{3,2,1,0:T(8,128)(2,1)S(1)}, bf16[32,6,8,128]{3,2,1,0:T(8,128)(2,1)S(1)}, u32[]{:S(2)}, u32[]{:S(2)}) collective-permute-start(bf16[32,6,8,128]{3,2,1,0:T(8,128)(2,1)S(1)} %get-tuple-element.27), channel_id=1, source_target_pairs={{0,16},{16,0},{1,17},{17,1},{2,18},{18,2},{3,19},{19,3},{4,20},{20... | collective-permute-start | bytes 1179656 | tf_op jit(solution)/shard_map/ppermute | solution.py:430
  2.7 1.5 %prep.1 = (bf16[2,128,1536]{2,1,0:T(8,128)(2,1)S(1)}, bf16[2,128,1536]{2,1,0:T(8,128)(2,1)S(1)}, bf16[2,128,1536]{2,1,0:T(8,128)(2,1)S(1)}, bf16[2,128,1536]{2,1,0:T(8,128)(2,1)S(1)}, bf16[768,1024]{1,0:T(8,128)(2,1)S(1)}) custom-call(bf16[32,8,8,128]{3,2,1,0:T(8,128)(2,1)S(1)} %get-tuple-element.22.data_ref, ...), custom_call_target="tpu_custom_call" | custom-call | flops 2000000000 | bytes 5000000 | tf_op jit(solution)/shard_map/prep/pallas_call | solution.py:450
  4.2 0.0 collective-permute-done.refs_2_
  4.2 6.0 %main.1 = (bf16[768,1280]{1,0:T(8,128)(2,1)S(1)}, f32[224,128]{1,0:T(8,128)S(1)}, f32[224,128]{1,0:T(8,128)S(1)}) custom-call(bf16[768,1024]{1,0:T(8,128)(2,1)S(1)} %get-tuple-element.25.refs_0_, bf16[32,8,8,128]{3,2,1,0:T(8,128)(2,1)S(1)} %get-tuple-element.26.refs_1_, bf16[32,6,8,128]{3,2,1,0:T(8,128)(2,1)S(1)} %collective-permute-done.refs_2_, ...), custom_call_target="tpu_custom_call" | custom-call | flops 8000000000 | bytes 8000000 | tf_op jit(solution)/shard_map/main/pallas_call | solution.py:460
  10.3 0.3 collective-permute-start.1
  10.6 1.1 %collective-permute-done.1 = f32[224,128]{1,0:T(8,128)S(1)} collective-permute-done((f32[224,128]{1,0:T(8,128)S(1)}, f32[224,128]{1,0:T(8,128)S(1)}, u32[]{:S(2)}, u32[]{:S(2)}) %collective-permute-start.1) | collective-permute-done | bytes 114720 | tf_op jit(solution)/shard_map/ppermute | solution.py:399
  11.7 2.7 %collective-permute-start.2 = (bf16[224,128]{1,0:T(8,128)(2,1)S(1)}, bf16[224,128]{1,0:T(8,128)(2,1)S(1)}, u32[]{:S(2)}, u32[]{:S(2)}) collective-permute-start(bf16[224,128]{1,0:T(8,128)(2,1)S(1)} %add_convert_fusion.2), channel_id=1, source_target_pairs={{0,20},{1,16},{2,19},{3,23},{4,21},{5,17},{6,18},{7,22},{8,25},{9,... | collective-permute-start | bytes 172040 | tf_op jit(solution)/shard_map/ppermute | solution.py:381
  14.4 1.9 %collective-permute-done.2 = bf16[224,128]{1,0:T(8,128)(2,1)S(1)} collective-permute-done((bf16[224,128]{1,0:T(8,128)(2,1)S(1)}, bf16[224,128]{1,0:T(8,128)(2,1)S(1)}, u32[]{:S(2)}, u32[]{:S(2)}) %collective-permute-start.2) | collective-permute-done | bytes 57376 | tf_op jit(solution)/shard_map/ppermute | solution.py:381
  16.3 2.8 %collective-permute-start.3 = (bf16[224,128]{1,0:T(8,128)(2,1)S(1)}, bf16[224,128]{1,0:T(8,128)(2,1)S(1)}, u32[]{:S(2)}, u32[]{:S(2)}) collective-permute-start(bf16[224,128]{1,0:T(8,128)(2,1)S(1)} %add_convert_fusion.1), channel_id=1, source_target_pairs={{0,24},{1,19},{2,16},{3,27},{4,22},{5,29},{6,30},{7,21},{8,26},{9,... | collective-permute-start | bytes 172040 | tf_op jit(solution)/shard_map/ppermute | solution.py:381
  19.1 1.9 %collective-permute-done.3 = bf16[224,128]{1,0:T(8,128)(2,1)S(1)} collective-permute-done((bf16[224,128]{1,0:T(8,128)(2,1)S(1)}, bf16[224,128]{1,0:T(8,128)(2,1)S(1)}, u32[]{:S(2)}, u32[]{:S(2)}) %collective-permute-start.3) | collective-permute-done | bytes 57376 | tf_op jit(solution)/shard_map/ppermute | solution.py:381
  21.0 1.6 %collective-permute-start.4 = (bf16[224,128]{1,0:T(8,128)(2,1)S(1)}, bf16[224,128]{1,0:T(8,128)(2,1)S(1)}, u32[]{:S(2)}, u32[]{:S(2)}) collective-permute-start(bf16[224,128]{1,0:T(8,128)(2,1)S(1)} %add_convert_fusion), channel_id=1, source_target_pairs={{0,17},{1,21},{2,22},{3,18},{4,16},{5,20},{6,23},{7,19},{8,28},{9,... | collective-permute-start | bytes 172040 | tf_op jit(solution)/shard_map/ppermute | solution.py:381
  22.6 2.0 %collective-permute-done.4 = bf16[224,128]{1,0:T(8,128)(2,1)S(1)} collective-permute-done((bf16[224,128]{1,0:T(8,128)(2,1)S(1)}, bf16[224,128]{1,0:T(8,128)(2,1)S(1)}, u32[]{:S(2)}, u32[]{:S(2)}) %collective-permute-start.4) | collective-permute-done | bytes 57376 | tf_op jit(solution)/shard_map/ppermute | solution.py:381
  24.7 1.7 %collective-permute-start.5 = (bf16[224,128]{1,0:T(8,128)(2,1)S(1)}, bf16[224,128]{1,0:T(8,128)(2,1)S(1)}, u32[]{:S(2)}, u32[]{:S(2)}) collective-permute-start(bf16[224,128]{1,0:T(8,128)(2,1)S(1)} %convert_add_fusion.1), channel_id=1, source_target_pairs={{0,18},{1,25},{2,26},{3,17},{4,28},{5,23},{6,20},{7,31},{8,16},{9,... | collective-permute-start | bytes 172040 | tf_op jit(solution)/shard_map/ppermute | solution.py:381
  26.4 1.9 %last.1 = bf16[32,8,8,128]{3,2,1,0:T(8,128)(2,1)} custom-call(bf16[768,1280]{1,0:T(8,128)(2,1)S(1)} %get-tuple-element.35.grad_field_ref, bf16[2,128,1536]{2,1,0:T(8,128)(2,1)S(1)} %get-tuple-element.36.back_one), custom_call_target="tpu_custom_call" | custom-call | flops 2000000000 | bytes 3000000 | tf_op jit(solution)/shard_map/last/pallas_call | solution.py:481
  28.3 0.1 collective-permute-done.5
  28.4 0.5 %collective-permute-start.6 = (f32[224,128]{1,0:T(8,128)S(1)}, f32[224,128]{1,0:T(8,128)S(1)}, u32[]{:S(2)}, u32[]{:S(2)}) collective-permute-start(f32[224,128]{1,0:T(8,128)S(1)} %convert_add_fusion), channel_id=1, source_target_pairs={{0,16},{16,0},{1,17},{17,1},{2,18},{18,2},{3,19},{19,3},{4,20},{20... | collective-permute-start | bytes 344072 | tf_op jit(solution)/shard_map/ppermute | solution.py:402
  28.9 1.0 %collective-permute-done.6 = f32[224,128]{1,0:T(8,128)S(1)} collective-permute-done((f32[224,128]{1,0:T(8,128)S(1)}, f32[224,128]{1,0:T(8,128)S(1)}, u32[]{:S(2)}, u32[]{:S(2)}) %collective-permute-start.6) | collective-permute-done | bytes 114720 | tf_op jit(solution)/shard_map/ppermute | solution.py:402
  29.9 1.1 %unpack.1 = (f32[3,3,3,32,32]{4,3,2,1,0:T(8,128)}, f32[3,3,3,32,32]{4,3,2,1,0:T(8,128)}) custom-call(f32[224,128]{1,0:T(8,128)S(1)} %get-tuple-element.42.one_ref, f32[224,128]{1,0:T(8,128)S(1)} %get-tuple-element.41.two_ref), custom_call_target="tpu_custom_call" | custom-call | tf_op jit(solution)/shard_map/unpack/pallas_call | solution.py:494
  (7 shorter events, 0.1 us)
Async XLA Ops:
  2.2 2.0 %collective-permute-start = (bf16[32,6,8,128]{3,2,1,0:T(8,128)(2,1)S(1)}, bf16[32,6,8,128]{3,2,1,0:T(8,128)(2,1)S(1)}, u32[]{:S(2)}, u32[]{:S(2)}) collective-permute-start(bf16[32,6,8,128]{3,2,1,0:T(8,128)(2,1)S(1)} %get-tuple-element.27), channel_id=1, source_target_pairs={{0,16},{16,0},{1,17},{17,1},{2,18},{18,2},{3,19},{19,3},{4,20},{20... | collective-permute-start | bytes 1179656 | tf_op jit(solution)/shard_map/ppermute | solution.py:430
  10.3 1.4 %collective-permute-start.1 = (f32[224,128]{1,0:T(8,128)S(1)}, f32[224,128]{1,0:T(8,128)S(1)}, u32[]{:S(2)}, u32[]{:S(2)}) collective-permute-start(f32[224,128]{1,0:T(8,128)S(1)} %broadcast_select_fusion.2), channel_id=1, source_target_pairs={{0,16},{16,0},{1,17},{17,1},{2,18},{18,2},{3,19},{19,3},{4,20},{20... | collective-permute-start | bytes 344072 | tf_op jit(solution)/shard_map/ppermute | solution.py:399
  11.7 4.6 %collective-permute-start.2 = (bf16[224,128]{1,0:T(8,128)(2,1)S(1)}, bf16[224,128]{1,0:T(8,128)(2,1)S(1)}, u32[]{:S(2)}, u32[]{:S(2)}) collective-permute-start(bf16[224,128]{1,0:T(8,128)(2,1)S(1)} %add_convert_fusion.2), channel_id=1, source_target_pairs={{0,20},{1,16},{2,19},{3,23},{4,21},{5,17},{6,18},{7,22},{8,25},{9,... | collective-permute-start | bytes 172040 | tf_op jit(solution)/shard_map/ppermute | solution.py:381
  16.3 4.7 %collective-permute-start.3 = (bf16[224,128]{1,0:T(8,128)(2,1)S(1)}, bf16[224,128]{1,0:T(8,128)(2,1)S(1)}, u32[]{:S(2)}, u32[]{:S(2)}) collective-permute-start(bf16[224,128]{1,0:T(8,128)(2,1)S(1)} %add_convert_fusion.1), channel_id=1, source_target_pairs={{0,24},{1,19},{2,16},{3,27},{4,22},{5,29},{6,30},{7,21},{8,26},{9,... | collective-permute-start | bytes 172040 | tf_op jit(solution)/shard_map/ppermute | solution.py:381
  21.0 3.7 %collective-permute-start.4 = (bf16[224,128]{1,0:T(8,128)(2,1)S(1)}, bf16[224,128]{1,0:T(8,128)(2,1)S(1)}, u32[]{:S(2)}, u32[]{:S(2)}) collective-permute-start(bf16[224,128]{1,0:T(8,128)(2,1)S(1)} %add_convert_fusion), channel_id=1, source_target_pairs={{0,17},{1,21},{2,22},{3,18},{4,16},{5,20},{6,23},{7,19},{8,28},{9,... | collective-permute-start | bytes 172040 | tf_op jit(solution)/shard_map/ppermute | solution.py:381
  24.7 3.7 %collective-permute-start.5 = (bf16[224,128]{1,0:T(8,128)(2,1)S(1)}, bf16[224,128]{1,0:T(8,128)(2,1)S(1)}, u32[]{:S(2)}, u32[]{:S(2)}) collective-permute-start(bf16[224,128]{1,0:T(8,128)(2,1)S(1)} %convert_add_fusion.1), channel_id=1, source_target_pairs={{0,18},{1,25},{2,26},{3,17},{4,28},{5,23},{6,20},{7,31},{8,16},{9,... | collective-permute-start | bytes 172040 | tf_op jit(solution)/shard_map/ppermute | solution.py:381
  28.4 1.5 %collective-permute-start.6 = (f32[224,128]{1,0:T(8,128)S(1)}, f32[224,128]{1,0:T(8,128)S(1)}, u32[]{:S(2)}, u32[]{:S(2)}) collective-permute-start(f32[224,128]{1,0:T(8,128)S(1)} %convert_add_fusion), channel_id=1, source_target_pairs={{0,16},{16,0},{1,17},{17,1},{2,18},{18,2},{3,19},{19,3},{4,20},{20... | collective-permute-start | bytes 344072 | tf_op jit(solution)/shard_map/ppermute | solution.py:402

commit v6 on v5

--- a/solution.py
+++ b/solution.py
@@ -22,7 +22,7 @@
 
 
 def pack_kernel(count, own, *refs):
-    sources, near, outs, sems = refs[:4], refs[4:8], refs[8:-1], refs[-1]
+    sources, near, outs, sems = refs[:4], refs[4:7], refs[7:-1], refs[-1]
     pairs = []
     for side, out in enumerate(outs):
         for ref, depth, at in ((sources[0], REACH, 0), (sources[1], REACH - 2, REACH)):
@@ -30,7 +30,7 @@
             if count == 2:
                 start = jnp.where(lax.axis_index("gz") == 1, 0, own - depth)
             pairs.append((ref.at[:, pl.ds(start, depth)], out.at[:, pl.ds(at, depth)]))
-    pairs.extend(zip(sources, near))
+    pairs.extend(zip((sources[0], *sources[2:]), near))
     copies = [pltpu.make_async_copy(*pair, sems.at[k]) for k, pair in enumerate(pairs)]
     for copy in copies:
         copy.start()
@@ -298,7 +298,6 @@
             gate = sigmoid(value)
             seed = turned(turn_ref, plane % 2, plane_of(cot_ref, plane, REACH, REACH - 2))
             upper.put(plane, seed * (gate * (1.0 + value * (1.0 - gate))))
-    gradient(hidden, upper, own, chan, flip, term_two)
 
     lower = field(grad_field_ref, REACH - 3)
     for first, number in spans(*reach(REACH - 3)):
@@ -308,6 +307,7 @@
             at = (plane - slope_low) * width
             grad = back[:, step * width : (step + 1) * width] * slope_ref[:, at : at + width]
             lower.put(plane, kept(plane, grad))
+    gradient(hidden, upper, own, chan, flip, term_two)
     gradient(data, lower, own, chan, flip, term_one)
 
 
@@ -367,8 +367,10 @@
 def crossed(value, before_last):
     count = lax.axis_size("dp")
     steps = [1 << k for k in range(count.bit_length() - 1)]
-    half = len(steps) // 2
-    orders = (steps[half:] + steps[:half], steps)
+    near, far = steps[:-1], steps[-1:]
+    orders = (near[:1] + far + near[1:], near[-1:] + near[:1] + far + near[1:-1])
+    if len(steps) < 3:
+        orders = (steps, steps)
     for phase in range(len(steps)):
         if phase == len(steps) - 1:
             value = before_last(value)
@@ -410,24 +412,24 @@
     sides = min(count - 1, 2)
     arrays = (data, cot, *taps)
     far = [pltpu.with_memory_space_constraint(value, pltpu.HBM) for value in arrays]
-    shapes = [value.shape for value in arrays]
+    shapes = [value.shape for value in (data, *taps)]
     shapes += [(chan, 2 * REACH - 2, height, width)] * sides
     near = pl.pallas_call(
         functools.partial(pack_kernel, count, own),
         out_shape=[pltpu.VMEM(shape, BF16) for shape in shapes],
         in_specs=[pl.BlockSpec(memory_space=pltpu.HBM)] * 4,
         out_specs=[pl.BlockSpec(memory_space=pltpu.VMEM)] * len(shapes),
-        scratch_shapes=[pltpu.SemaphoreType.DMA((4 + 2 * sides,))],
+        scratch_shapes=[pltpu.SemaphoreType.DMA((3 + 2 * sides,))],
         compiler_params=params(4),
         name="pack",
     )(*far)
-    messages = near[4:]
+    messages = near[3:]
     if count == 2:
         moves = [[(0, 1), (1, 0)]]
     else:
         up = [(i, i + 1) for i in range(count - 1)]
         moves = [up, [(j, i) for i, j in up]]
-    return near[:4], [lax.ppermute(item, "gz", move) for item, move in zip(messages, moves)]
+    return [near[0], cot, *near[1:3]], [lax.ppermute(item, "gz", move) for item, move in zip(messages, moves)]
 
 
 def local(inputs, kernel_one, kernel_two, cotangent):

time: 31.4 us -> 30.9 us (0.984)
  no operation moved by 1% of the time
where the time goes in v6:
time: 30.9 us; the launch traced here: 30.7 us
  Pallas kernels  11.8 us (38%)
  starting transfers between devices  10.1 us (33%)
  waiting for transfers between devices  7.94 us (26%)
  between operations  0.7 us (2%)
    ppermute x4, starting transfers between devices, crossed(): lax.ppermute(sent, ('gz', 'dp'), moves).astype(F32)  8.92 us
    pallas_call x1, Pallas kernels, local(): pl.pallas_call(functools.partial(main_kernel, count, sizes), out_shape=[j...  5.9 us
    ppermute x4, waiting for transfers between devices, crossed(): lax.ppermute(sent, ('gz', 'dp'), moves).astype(F32)  5.8 us
    pallas_call x1, Pallas kernels, finish(): pl.pallas_call(functools.partial(last_kernel, count, sizes), out_shape=ja...  1.92 us
    pallas_call x1, Pallas kernels, local(): pl.pallas_call(functools.partial(prep_kernel, count == 2), out_shape=[jax...  1.47 us
    pallas_call x1, Pallas kernels, gathered(): pl.pallas_call(functools.partial(pack_kernel, count, own), out_shape=[plt...  1.36 us
    pallas_call x1, Pallas kernels, local(): pl.pallas_call(functools.partial(unpack_kernel, 1.0 / math.sqrt(cells)),...  1.14 us
    ppermute x1, waiting for transfers between devices, reduced(): mine = mine + lax.ppermute(jnp.where(first, one, two), 'gz', swap)  1.07 us
  transfers between devices with their start and end apart: 7, of which 6 were waited for; matrix products, arithmetic and copies ran while one was open for 0% of the time, Pallas kernels for 11%

profile of v6, /device:TPU:0, one launch (start us, length us, event | category | flops | bytes accessed | tf_op | source)
XLA Modules:
  0.0 30.7 jit_solution(6384345521724835832)
XLA Ops:
  0.6 1.4 %pack.1 = (bf16[32,8,8,128]{3,2,1,0:T(8,128)(2,1)S(1)}, bf16[3,3,3,32,32]{4,3,2,1,0:T(8,128)(2,1)S(1)}, bf16[3,3,3,32,32]{4,3,2,1,0:T(8,128)(2,1)S(1)}, bf16[32,6,8,128]{3,2,1,0:T(8,128)(2,1)S(1)}) custom-call(bf16[32,8,8,128]{3,2,1,0:T(8,128)(2,1)} %bitcast.9, bf16[32,8,8,128]{3,2,1,0:T(8,128)(2,1)} %bitcast.7, bf16[3,3,3,32,32]{4,3,2,1,0:T(8,128)(2,1)} %bitcast.10, ...), custom_call_target="tpu_custom_call" | custom-call | tf_op jit(solution)/shard_map/pack/pallas_call | solution.py:417
  2.0 0.6 %collective-permute-start = (bf16[32,6,8,128]{3,2,1,0:T(8,128)(2,1)S(1)}, bf16[32,6,8,128]{3,2,1,0:T(8,128)(2,1)S(1)}, u32[]{:S(2)}, u32[]{:S(2)}) collective-permute-start(bf16[32,6,8,128]{3,2,1,0:T(8,128)(2,1)S(1)} %get-tuple-element.25), channel_id=1, source_target_pairs={{0,16},{16,0},{1,17},{17,1},{2,18},{18,2},{3,19},{19,3},{4,20},{20... | collective-permute-start | bytes 1179656 | tf_op jit(solution)/shard_map/ppermute | solution.py:432
  2.6 0.0 copy-start
  2.6 1.5 %prep.1 = (bf16[2,128,1536]{2,1,0:T(8,128)(2,1)S(1)}, bf16[2,128,1536]{2,1,0:T(8,128)(2,1)S(1)}, bf16[2,128,1536]{2,1,0:T(8,128)(2,1)S(1)}, bf16[2,128,1536]{2,1,0:T(8,128)(2,1)S(1)}, bf16[768,1024]{1,0:T(8,128)(2,1)S(1)}) custom-call(bf16[32,8,8,128]{3,2,1,0:T(8,128)(2,1)S(1)} %get-tuple-element.21.data_ref, ...), custom_call_target="tpu_custom_call" | custom-call | flops 2000000000 | bytes 5000000 | tf_op jit(solution)/shard_map/prep/pallas_call | solution.py:452
  4.0 0.0 collective-permute-done.refs_2_
  4.0 0.0 copy-done
  4.1 5.9 %main.1 = (bf16[768,1280]{1,0:T(8,128)(2,1)S(1)}, f32[224,128]{1,0:T(8,128)S(1)}, f32[224,128]{1,0:T(8,128)S(1)}) custom-call(bf16[768,1024]{1,0:T(8,128)(2,1)S(1)} %get-tuple-element.24.refs_0_, bf16[32,8,8,128]{3,2,1,0:T(8,128)(2,1)S(1)} %bitcast.8, bf16[32,6,8,128]{3,2,1,0:T(8,128)(2,1)S(1)} %collective-permute-done.refs_2_, ...), custom_call_target="tpu_custom_call" | custom-call | flops 8000000000 | bytes 8000000 | tf_op jit(solution)/shard_map/main/pallas_call | solution.py:462
  10.0 0.3 %collective-permute-start.1 = (f32[224,128]{1,0:T(8,128)S(1)}, f32[224,128]{1,0:T(8,128)S(1)}, u32[]{:S(2)}, u32[]{:S(2)}) collective-permute-start(f32[224,128]{1,0:T(8,128)S(1)} %broadcast_select_fusion.2), channel_id=1, source_target_pairs={{0,16},{16,0},{1,17},{17,1},{2,18},{18,2},{3,19},{19,3},{4,20},{20... | collective-permute-start | bytes 344072 | tf_op jit(solution)/shard_map/ppermute | solution.py:401
  10.3 1.1 %collective-permute-done.1 = f32[224,128]{1,0:T(8,128)S(1)} collective-permute-done((f32[224,128]{1,0:T(8,128)S(1)}, f32[224,128]{1,0:T(8,128)S(1)}, u32[]{:S(2)}, u32[]{:S(2)}) %collective-permute-start.1) | collective-permute-done | bytes 114720 | tf_op jit(solution)/shard_map/ppermute | solution.py:401
  11.4 2.7 %collective-permute-start.2 = (bf16[224,128]{1,0:T(8,128)(2,1)S(1)}, bf16[224,128]{1,0:T(8,128)(2,1)S(1)}, u32[]{:S(2)}, u32[]{:S(2)}) collective-permute-start(bf16[224,128]{1,0:T(8,128)(2,1)S(1)} %add_convert_fusion.2), channel_id=1, source_target_pairs={{0,17},{1,21},{2,22},{3,18},{4,16},{5,20},{6,23},{7,19},{8,28},{9,... | collective-permute-start | bytes 172040 | tf_op jit(solution)/shard_map/ppermute | solution.py:383
  14.1 1.9 %collective-permute-done.2 = bf16[224,128]{1,0:T(8,128)(2,1)S(1)} collective-permute-done((bf16[224,128]{1,0:T(8,128)(2,1)S(1)}, bf16[224,128]{1,0:T(8,128)(2,1)S(1)}, u32[]{:S(2)}, u32[]{:S(2)}) %collective-permute-start.2) | collective-permute-done | bytes 57376 | tf_op jit(solution)/shard_map/ppermute | solution.py:383
  16.0 2.9 %collective-permute-start.3 = (bf16[224,128]{1,0:T(8,128)(2,1)S(1)}, bf16[224,128]{1,0:T(8,128)(2,1)S(1)}, u32[]{:S(2)}, u32[]{:S(2)}) collective-permute-start(bf16[224,128]{1,0:T(8,128)(2,1)S(1)} %add_convert_fusion.1), channel_id=1, source_target_pairs={{0,24},{1,16},{2,19},{3,27},{4,21},{5,29},{6,30},{7,22},{8,25},{9,... | collective-permute-start | bytes 172040 | tf_op jit(solution)/shard_map/ppermute | solution.py:383
  18.9 1.9 %collective-permute-done.3 = bf16[224,128]{1,0:T(8,128)(2,1)S(1)} collective-permute-done((bf16[224,128]{1,0:T(8,128)(2,1)S(1)}, bf16[224,128]{1,0:T(8,128)(2,1)S(1)}, u32[]{:S(2)}, u32[]{:S(2)}) %collective-permute-start.3) | collective-permute-done | bytes 57376 | tf_op jit(solution)/shard_map/ppermute | solution.py:383
  20.8 1.6 %collective-permute-start.4 = (bf16[224,128]{1,0:T(8,128)(2,1)S(1)}, bf16[224,128]{1,0:T(8,128)(2,1)S(1)}, u32[]{:S(2)}, u32[]{:S(2)}) collective-permute-start(bf16[224,128]{1,0:T(8,128)(2,1)S(1)} %add_convert_fusion), channel_id=1, source_target_pairs={{0,18},{1,25},{2,26},{3,17},{4,28},{5,23},{6,20},{7,31},{8,16},{9,... | collective-permute-start | bytes 172040 | tf_op jit(solution)/shard_map/ppermute | solution.py:383
  22.4 2.0 %collective-permute-done.4 = bf16[224,128]{1,0:T(8,128)(2,1)S(1)} collective-permute-done((bf16[224,128]{1,0:T(8,128)(2,1)S(1)}, bf16[224,128]{1,0:T(8,128)(2,1)S(1)}, u32[]{:S(2)}, u32[]{:S(2)}) %collective-permute-start.4) | collective-permute-done | bytes 57376 | tf_op jit(solution)/shard_map/ppermute | solution.py:383
  24.4 1.7 %collective-permute-start.5 = (bf16[224,128]{1,0:T(8,128)(2,1)S(1)}, bf16[224,128]{1,0:T(8,128)(2,1)S(1)}, u32[]{:S(2)}, u32[]{:S(2)}) collective-permute-start(bf16[224,128]{1,0:T(8,128)(2,1)S(1)} %convert_add_fusion.1), channel_id=1, source_target_pairs={{0,20},{1,19},{2,16},{3,23},{4,22},{5,17},{6,18},{7,21},{8,26},{9,... | collective-permute-start | bytes 172040 | tf_op jit(solution)/shard_map/ppermute | solution.py:383
  26.1 1.9 %last.1 = bf16[32,8,8,128]{3,2,1,0:T(8,128)(2,1)} custom-call(bf16[768,1280]{1,0:T(8,128)(2,1)S(1)} %get-tuple-element.33.grad_field_ref, bf16[2,128,1536]{2,1,0:T(8,128)(2,1)S(1)} %get-tuple-element.34.back_one), custom_call_target="tpu_custom_call" | custom-call | flops 2000000000 | bytes 3000000 | tf_op jit(solution)/shard_map/last/pallas_call | solution.py:483
  28.1 0.1 collective-permute-done.5
  28.1 0.3 %collective-permute-start.6 = (f32[224,128]{1,0:T(8,128)S(1)}, f32[224,128]{1,0:T(8,128)S(1)}, u32[]{:S(2)}, u32[]{:S(2)}) collective-permute-start(f32[224,128]{1,0:T(8,128)S(1)} %convert_add_fusion), channel_id=1, source_target_pairs={{0,16},{16,0},{1,17},{17,1},{2,18},{18,2},{3,19},{19,3},{4,20},{20... | collective-permute-start | bytes 344072 | tf_op jit(solution)/shard_map/ppermute | solution.py:404
  28.5 1.1 %collective-permute-done.6 = f32[224,128]{1,0:T(8,128)S(1)} collective-permute-done((f32[224,128]{1,0:T(8,128)S(1)}, f32[224,128]{1,0:T(8,128)S(1)}, u32[]{:S(2)}, u32[]{:S(2)}) %collective-permute-start.6) | collective-permute-done | bytes 114720 | tf_op jit(solution)/shard_map/ppermute | solution.py:404
  29.5 1.1 %unpack.1 = (f32[3,3,3,32,32]{4,3,2,1,0:T(8,128)}, f32[3,3,3,32,32]{4,3,2,1,0:T(8,128)}) custom-call(f32[224,128]{1,0:T(8,128)S(1)} %get-tuple-element.40.one_ref, f32[224,128]{1,0:T(8,128)S(1)} %get-tuple-element.39.two_ref), custom_call_target="tpu_custom_call" | custom-call | tf_op jit(solution)/shard_map/unpack/pallas_call | solution.py:496
  (7 shorter events, 0.1 us)
Async XLA Ops:
  2.0 2.0 %collective-permute-start = (bf16[32,6,8,128]{3,2,1,0:T(8,128)(2,1)S(1)}, bf16[32,6,8,128]{3,2,1,0:T(8,128)(2,1)S(1)}, u32[]{:S(2)}, u32[]{:S(2)}) collective-permute-start(bf16[32,6,8,128]{3,2,1,0:T(8,128)(2,1)S(1)} %get-tuple-element.25), channel_id=1, source_target_pairs={{0,16},{16,0},{1,17},{17,1},{2,18},{18,2},{3,19},{19,3},{4,20},{20... | collective-permute-start | bytes 1179656 | tf_op jit(solution)/shard_map/ppermute | solution.py:432
  2.6 1.5 %copy-start = (bf16[1,32,8,8,128]{4,3,2,1,0:T(8,128)(2,1)S(1)}, bf16[1,32,8,8,128]{4,3,2,1,0:T(8,128)(2,1)}, u32[]{:S(2)}) copy-start(bf16[1,32,8,8,128]{4,3,2,1,0:T(8,128)(2,1)} %param.7) | copy-start | bytes 1572868
  10.0 1.4 %collective-permute-start.1 = (f32[224,128]{1,0:T(8,128)S(1)}, f32[224,128]{1,0:T(8,128)S(1)}, u32[]{:S(2)}, u32[]{:S(2)}) collective-permute-start(f32[224,128]{1,0:T(8,128)S(1)} %broadcast_select_fusion.2), channel_id=1, source_target_pairs={{0,16},{16,0},{1,17},{17,1},{2,18},{18,2},{3,19},{19,3},{4,20},{20... | collective-permute-start | bytes 344072 | tf_op jit(solution)/shard_map/ppermute | solution.py:401
  11.4 4.5 %collective-permute-start.2 = (bf16[224,128]{1,0:T(8,128)(2,1)S(1)}, bf16[224,128]{1,0:T(8,128)(2,1)S(1)}, u32[]{:S(2)}, u32[]{:S(2)}) collective-permute-start(bf16[224,128]{1,0:T(8,128)(2,1)S(1)} %add_convert_fusion.2), channel_id=1, source_target_pairs={{0,17},{1,21},{2,22},{3,18},{4,16},{5,20},{6,23},{7,19},{8,28},{9,... | collective-permute-start | bytes 172040 | tf_op jit(solution)/shard_map/ppermute | solution.py:383
  16.0 4.8 %collective-permute-start.3 = (bf16[224,128]{1,0:T(8,128)(2,1)S(1)}, bf16[224,128]{1,0:T(8,128)(2,1)S(1)}, u32[]{:S(2)}, u32[]{:S(2)}) collective-permute-start(bf16[224,128]{1,0:T(8,128)(2,1)S(1)} %add_convert_fusion.1), channel_id=1, source_target_pairs={{0,24},{1,16},{2,19},{3,27},{4,21},{5,29},{6,30},{7,22},{8,25},{9,... | collective-permute-start | bytes 172040 | tf_op jit(solution)/shard_map/ppermute | solution.py:383
  20.8 3.7 %collective-permute-start.4 = (bf16[224,128]{1,0:T(8,128)(2,1)S(1)}, bf16[224,128]{1,0:T(8,128)(2,1)S(1)}, u32[]{:S(2)}, u32[]{:S(2)}) collective-permute-start(bf16[224,128]{1,0:T(8,128)(2,1)S(1)} %add_convert_fusion), channel_id=1, source_target_pairs={{0,18},{1,25},{2,26},{3,17},{4,28},{5,23},{6,20},{7,31},{8,16},{9,... | collective-permute-start | bytes 172040 | tf_op jit(solution)/shard_map/ppermute | solution.py:383
  24.4 3.7 %collective-permute-start.5 = (bf16[224,128]{1,0:T(8,128)(2,1)S(1)}, bf16[224,128]{1,0:T(8,128)(2,1)S(1)}, u32[]{:S(2)}, u32[]{:S(2)}) collective-permute-start(bf16[224,128]{1,0:T(8,128)(2,1)S(1)} %convert_add_fusion.1), channel_id=1, source_target_pairs={{0,20},{1,19},{2,16},{3,23},{4,22},{5,17},{6,18},{7,21},{8,26},{9,... | collective-permute-start | bytes 172040 | tf_op jit(solution)/shard_map/ppermute | solution.py:383
  28.1 1.4 %collective-permute-start.6 = (f32[224,128]{1,0:T(8,128)S(1)}, f32[224,128]{1,0:T(8,128)S(1)}, u32[]{:S(2)}, u32[]{:S(2)}) collective-permute-start(f32[224,128]{1,0:T(8,128)S(1)} %convert_add_fusion), channel_id=1, source_target_pairs={{0,16},{16,0},{1,17},{17,1},{2,18},{18,2},{3,19},{19,3},{4,20},{20... | collective-permute-start | bytes 344072 | tf_op jit(solution)/shard_map/ppermute | solution.py:404

commit v7 on v6

--- a/solution.py
+++ b/solution.py
@@ -334,19 +334,54 @@
             out_ref[:, at] = turn_ref[slot].reshape(chan, height, width).astype(BF16)
 
 
-def unpack_kernel(factor, one_ref, two_ref, out_one, out_two):
-    chan = out_one.shape[-1]
-    for ref, out in ((one_ref, out_one), (two_ref, out_two)):
-        value = ref[...].T * factor
-        for dz in range(3):
-            for dy in range(3):
-                for dx in range(3):
-                    row, column = (dx, 3 * dz + dy) if dz < 2 else (3, 3 * dx + dy)
-                    if dz == 2 and dx == 2:
-                        row, column = dy, 6
-                    out[dz, dy, dx] = value[
-                        row * chan : (row + 1) * chan, column * chan : (column + 1) * chan
-                    ]
+def holds_second():
+    count, place, core = lax.axis_size("dp"), lax.axis_index("dp"), lax.axis_index("gz")
+    for bit in range(count.bit_length() - 1):
+        core = core + lax.shift_right_logical(place, bit)
+    return core % 2 == 0
+
+
+def unpack_kernel(factor, which, packed_ref, *refs):
+    out_one, out_two, grad_ref, sem = refs[-4:]
+    chan = grad_ref.shape[-1]
+    value = packed_ref[...].T * factor
+    for dz in range(3):
+        for dy in range(3):
+            for dx in range(3):
+                row, column = (dx, 3 * dz + dy) if dz < 2 else (3, 3 * dx + dy)
+                if dz == 2 and dx == 2:
+                    row, column = dy, 6
+                grad_ref[dz, dy, dx] = value[
+                    row * chan : (row + 1) * chan, column * chan : (column + 1) * chan
+                ]
+
+    def send(out):
+        copy = pltpu.make_async_copy(grad_ref, out, sem)
+        copy.start()
+        copy.wait()
+
+    if which in (0, 1):
+        send(out_two if which else out_one)
+    else:
+        second = holds_second() == (which == "held")
+        pl.when(second)(lambda: send(out_two))
+        pl.when(jnp.logical_not(second))(lambda: send(out_one))
+
+
+def unpacked(packed, which, factor, chan, outs=()):
+    shape = (3, 3, 3, chan, chan)
+    hbm = pl.BlockSpec(memory_space=pltpu.HBM)
+    return pl.pallas_call(
+        functools.partial(unpack_kernel, factor, which),
+        out_shape=[pltpu.HBM(shape, F32)] * 2,
+        in_specs=[pl.BlockSpec(memory_space=pltpu.VMEM)] + [hbm] * len(outs),
+        out_specs=[hbm] * 2,
+        scratch_shapes=[pltpu.VMEM(shape, F32), pltpu.SemaphoreType.DMA],
+        input_output_aliases={1 + k: k for k in range(len(outs))},
+        compiler_params=params(8),
+        cost_estimate=cost(1e9, 1e6),
+        name="unpack",
+    )(packed, *outs)
 
 
 def doubled(value, axis):
@@ -384,7 +419,7 @@
     return value
 
 
-def reduced(one, two, grad_fields, finish):
+def reduced(one, two, grad_fields, finish, unpack):
     outs = []
 
     def gate(value):
@@ -395,16 +430,15 @@
     count = lax.axis_size("dp")
     if lax.axis_size("gz") == 2 and count > 1 and count & (count - 1) == 0:
         swap = [(0, 1), (1, 0)]
-        turns = lax.population_count(lax.axis_index("dp")) + lax.axis_index("gz")
-        first = turns % 2 == 0
-        mine = jnp.where(first, two, one)
-        mine = mine + lax.ppermute(jnp.where(first, one, two), "gz", swap)
+        second = holds_second()
+        mine = jnp.where(second, two, one)
+        mine = mine + lax.ppermute(jnp.where(second, one, two), "gz", swap)
         mine = crossed(mine, gate)
         mine, *outs = lax.optimization_barrier((mine, *outs))
         other = lax.ppermute(mine, "gz", swap)
-        return jnp.where(first, other, mine), jnp.where(first, mine, other), outs
+        return unpack(other, "other", unpack(mine, "held")), outs
     both = doubled(doubled(jnp.stack([one, two]), "gz"), "dp")
-    return both[0], both[1], finish(grad_fields)
+    return unpack(both[1], 1, unpack(both[0], 0)), finish(grad_fields)
 
 
 def gathered(count, data, cot, *taps):
@@ -491,14 +525,13 @@
             for pair in zip(fields, backs)
         ]
 
-    one, two, outs = reduced(sum(ones[1:], ones[0]), sum(twos[1:], twos[0]), grad_fields, finish)
     cells = lax.axis_size("dp") * batch * count * own * height * width
-    grads = pl.pallas_call(
-        functools.partial(unpack_kernel, 1.0 / math.sqrt(cells)),
-        out_shape=[jax.ShapeDtypeStruct((3, 3, 3, chan, chan), F32)] * 2,
-        compiler_params=params(8),
-        name="unpack",
-    )(one, two)
+
+    def unpack(packed, which, outs=()):
+        return unpacked(packed, which, 1.0 / math.sqrt(cells), chan, outs)
+
+    one, two = sum(ones[1:], ones[0]), sum(twos[1:], twos[0])
+    grads, outs = reduced(one, two, grad_fields, finish, unpack)
     one, two = [jnp.transpose(g, (3, 4, 0, 1, 2)) for g in grads]
     return jnp.stack(outs), one, two
 

time: 30.9 us -> 30.7 us (level)
  waiting for transfers between devices: 7.94 us -> 6.95 us
  Pallas kernels: 11.8 us -> 12.6 us
    ppermute x1, waiting for transfers between devices: 1.07 us -> 0.07 us  [reduced(): other = lax.ppermute(mine, 'gz', swap)]
    pallas_call x1 -> x2, Pallas kernels: 1.14 us -> 1.98 us  [unpacked(): pl.pallas_call(functools.partial(unpack_kernel, factor, which), out_shape...]
  transfers between devices with their start and end apart: 7 -> 7, of which waited for: 6 -> 6; matrix products, arithmetic and copies ran while one was open for 0% -> 0% of each run, Pallas kernels for 11% -> 14%
where the time goes in v7:
time: 30.7 us; the launch traced here: 30.5 us
  Pallas kernels  12.6 us (41%)
  starting transfers between devices  10.1 us (33%)
  waiting for transfers between devices  6.95 us (23%)
  between operations  0.71 us (2%)
    ppermute x4, starting transfers between devices, crossed(): lax.ppermute(sent, ('gz', 'dp'), moves).astype(F32)  8.92 us
    pallas_call x1, Pallas kernels, local(): pl.pallas_call(functools.partial(main_kernel, count, sizes), out_shape=[j...  5.9 us
    ppermute x4, waiting for transfers between devices, crossed(): lax.ppermute(sent, ('gz', 'dp'), moves).astype(F32)  5.8 us
    pallas_call x2, Pallas kernels, unpacked(): pl.pallas_call(functools.partial(unpack_kernel, factor, which), out_shape...  1.98 us
    pallas_call x1, Pallas kernels, finish(): pl.pallas_call(functools.partial(last_kernel, count, sizes), out_shape=ja...  1.92 us
    pallas_call x1, Pallas kernels, local(): pl.pallas_call(functools.partial(prep_kernel, count == 2), out_shape=[jax...  1.47 us
    pallas_call x1, Pallas kernels, gathered(): pl.pallas_call(functools.partial(pack_kernel, count, own), out_shape=[plt...  1.36 us
    ppermute x1, waiting for transfers between devices, reduced(): mine = mine + lax.ppermute(jnp.where(second, one, two), 'gz', swap)  1.07 us
  transfers between devices with their start and end apart: 7, of which 6 were waited for; matrix products, arithmetic and copies ran while one was open for 0% of the time, Pallas kernels for 14%

profile of v7, /device:TPU:0, one launch (start us, length us, event | category | flops | bytes accessed | tf_op | source)
XLA Modules:
  0.0 30.5 jit_solution(2656354507589225818)
XLA Ops:
  0.6 1.4 %pack.1 = (bf16[32,8,8,128]{3,2,1,0:T(8,128)(2,1)S(1)}, bf16[3,3,3,32,32]{4,3,2,1,0:T(8,128)(2,1)S(1)}, bf16[3,3,3,32,32]{4,3,2,1,0:T(8,128)(2,1)S(1)}, bf16[32,6,8,128]{3,2,1,0:T(8,128)(2,1)S(1)}) custom-call(bf16[32,8,8,128]{3,2,1,0:T(8,128)(2,1)} %bitcast.9, bf16[32,8,8,128]{3,2,1,0:T(8,128)(2,1)} %bitcast.7, bf16[3,3,3,32,32]{4,3,2,1,0:T(8,128)(2,1)} %bitcast.10, ...), custom_call_target="tpu_custom_call" | custom-call | tf_op jit(solution)/shard_map/pack/pallas_call | solution.py:451
  2.0 0.6 %collective-permute-start = (bf16[32,6,8,128]{3,2,1,0:T(8,128)(2,1)S(1)}, bf16[32,6,8,128]{3,2,1,0:T(8,128)(2,1)S(1)}, u32[]{:S(2)}, u32[]{:S(2)}) collective-permute-start(bf16[32,6,8,128]{3,2,1,0:T(8,128)(2,1)S(1)} %get-tuple-element.27), channel_id=1, source_target_pairs={{0,16},{16,0},{1,17},{17,1},{2,18},{18,2},{3,19},{19,3},{4,20},{20... | collective-permute-start | bytes 1179656 | tf_op jit(solution)/shard_map/ppermute | solution.py:466
  2.6 0.0 copy-start
  2.6 1.5 %prep.1 = (bf16[2,128,1536]{2,1,0:T(8,128)(2,1)S(1)}, bf16[2,128,1536]{2,1,0:T(8,128)(2,1)S(1)}, bf16[2,128,1536]{2,1,0:T(8,128)(2,1)S(1)}, bf16[2,128,1536]{2,1,0:T(8,128)(2,1)S(1)}, bf16[768,1024]{1,0:T(8,128)(2,1)S(1)}) custom-call(bf16[32,8,8,128]{3,2,1,0:T(8,128)(2,1)S(1)} %get-tuple-element.23.data_ref, ...), custom_call_target="tpu_custom_call" | custom-call | flops 2000000000 | bytes 5000000 | tf_op jit(solution)/shard_map/prep/pallas_call | solution.py:486
  4.0 0.0 collective-permute-done.refs_2_
  4.0 0.0 copy-done
  4.1 5.9 %main.1 = (bf16[768,1280]{1,0:T(8,128)(2,1)S(1)}, f32[224,128]{1,0:T(8,128)S(1)}, f32[224,128]{1,0:T(8,128)S(1)}) custom-call(bf16[768,1024]{1,0:T(8,128)(2,1)S(1)} %get-tuple-element.26.refs_0_, bf16[32,8,8,128]{3,2,1,0:T(8,128)(2,1)S(1)} %bitcast.8, bf16[32,6,8,128]{3,2,1,0:T(8,128)(2,1)S(1)} %collective-permute-done.refs_2_, ...), custom_call_target="tpu_custom_call" | custom-call | flops 8000000000 | bytes 8000000 | tf_op jit(solution)/shard_map/main/pallas_call | solution.py:496
  10.0 0.3 %collective-permute-start.1 = (f32[224,128]{1,0:T(8,128)S(1)}, f32[224,128]{1,0:T(8,128)S(1)}, u32[]{:S(2)}, u32[]{:S(2)}) collective-permute-start(f32[224,128]{1,0:T(8,128)S(1)} %broadcast_select_fusion), channel_id=1, source_target_pairs={{0,16},{16,0},{1,17},{17,1},{2,18},{18,2},{3,19},{19,3},{4,20},{20... | collective-permute-start | bytes 344072 | tf_op jit(solution)/shard_map/ppermute | solution.py:435
  10.3 1.1 %collective-permute-done.1 = f32[224,128]{1,0:T(8,128)S(1)} collective-permute-done((f32[224,128]{1,0:T(8,128)S(1)}, f32[224,128]{1,0:T(8,128)S(1)}, u32[]{:S(2)}, u32[]{:S(2)}) %collective-permute-start.1) | collective-permute-done | bytes 114720 | tf_op jit(solution)/shard_map/ppermute | solution.py:435
  11.4 2.7 %collective-permute-start.2 = (bf16[224,128]{1,0:T(8,128)(2,1)S(1)}, bf16[224,128]{1,0:T(8,128)(2,1)S(1)}, u32[]{:S(2)}, u32[]{:S(2)}) collective-permute-start(bf16[224,128]{1,0:T(8,128)(2,1)S(1)} %add_convert_fusion.2), channel_id=1, source_target_pairs={{0,17},{1,21},{2,22},{3,18},{4,16},{5,20},{6,23},{7,19},{8,28},{9,... | collective-permute-start | bytes 172040 | tf_op jit(solution)/shard_map/ppermute | solution.py:418
  14.1 1.9 %collective-permute-done.2 = bf16[224,128]{1,0:T(8,128)(2,1)S(1)} collective-permute-done((bf16[224,128]{1,0:T(8,128)(2,1)S(1)}, bf16[224,128]{1,0:T(8,128)(2,1)S(1)}, u32[]{:S(2)}, u32[]{:S(2)}) %collective-permute-start.2) | collective-permute-done | bytes 57376 | tf_op jit(solution)/shard_map/ppermute | solution.py:418
  16.0 2.9 %collective-permute-start.3 = (bf16[224,128]{1,0:T(8,128)(2,1)S(1)}, bf16[224,128]{1,0:T(8,128)(2,1)S(1)}, u32[]{:S(2)}, u32[]{:S(2)}) collective-permute-start(bf16[224,128]{1,0:T(8,128)(2,1)S(1)} %add_convert_fusion.1), channel_id=1, source_target_pairs={{0,24},{1,16},{2,19},{3,27},{4,21},{5,29},{6,30},{7,22},{8,25},{9,... | collective-permute-start | bytes 172040 | tf_op jit(solution)/shard_map/ppermute | solution.py:418
  18.9 1.9 %collective-permute-done.3 = bf16[224,128]{1,0:T(8,128)(2,1)S(1)} collective-permute-done((bf16[224,128]{1,0:T(8,128)(2,1)S(1)}, bf16[224,128]{1,0:T(8,128)(2,1)S(1)}, u32[]{:S(2)}, u32[]{:S(2)}) %collective-permute-start.3) | collective-permute-done | bytes 57376 | tf_op jit(solution)/shard_map/ppermute | solution.py:418
  20.8 1.6 %collective-permute-start.4 = (bf16[224,128]{1,0:T(8,128)(2,1)S(1)}, bf16[224,128]{1,0:T(8,128)(2,1)S(1)}, u32[]{:S(2)}, u32[]{:S(2)}) collective-permute-start(bf16[224,128]{1,0:T(8,128)(2,1)S(1)} %add_convert_fusion), channel_id=1, source_target_pairs={{0,18},{1,25},{2,26},{3,17},{4,28},{5,23},{6,20},{7,31},{8,16},{9,... | collective-permute-start | bytes 172040 | tf_op jit(solution)/shard_map/ppermute | solution.py:418
  22.4 2.0 %collective-permute-done.4 = bf16[224,128]{1,0:T(8,128)(2,1)S(1)} collective-permute-done((bf16[224,128]{1,0:T(8,128)(2,1)S(1)}, bf16[224,128]{1,0:T(8,128)(2,1)S(1)}, u32[]{:S(2)}, u32[]{:S(2)}) %collective-permute-start.4) | collective-permute-done | bytes 57376 | tf_op jit(solution)/shard_map/ppermute | solution.py:418
  24.4 1.7 %collective-permute-start.5 = (bf16[224,128]{1,0:T(8,128)(2,1)S(1)}, bf16[224,128]{1,0:T(8,128)(2,1)S(1)}, u32[]{:S(2)}, u32[]{:S(2)}) collective-permute-start(bf16[224,128]{1,0:T(8,128)(2,1)S(1)} %convert_add_fusion.1), channel_id=1, source_target_pairs={{0,20},{1,19},{2,16},{3,23},{4,22},{5,17},{6,18},{7,21},{8,26},{9,... | collective-permute-start | bytes 172040 | tf_op jit(solution)/shard_map/ppermute | solution.py:418
  26.1 1.9 %last.1 = bf16[32,8,8,128]{3,2,1,0:T(8,128)(2,1)} custom-call(bf16[768,1280]{1,0:T(8,128)(2,1)S(1)} %get-tuple-element.35.grad_field_ref, bf16[2,128,1536]{2,1,0:T(8,128)(2,1)S(1)} %get-tuple-element.36.back_one), custom_call_target="tpu_custom_call" | custom-call | flops 2000000000 | bytes 3000000 | tf_op jit(solution)/shard_map/last/pallas_call | solution.py:517
  28.1 0.1 collective-permute-done.5
  28.1 0.3 %collective-permute-start.6 = (f32[224,128]{1,0:T(8,128)S(1)}, f32[224,128]{1,0:T(8,128)S(1)}, u32[]{:S(2)}, u32[]{:S(2)}) collective-permute-start(f32[224,128]{1,0:T(8,128)S(1)} %convert_add_fusion.packed_ref), channel_id=1, source_target_pairs={{0,16},{16,0},{1,17},{17,1},{2,18},{18,2},{3,19},{19,3},{4,20},{20... | collective-permute-start | bytes 344072 | tf_op jit(solution)/shard_map/ppermute | solution.py:438
  28.5 1.0 %unpack.2 = (f32[3,3,3,32,32]{4,3,2,1,0:T(8,128)}, f32[3,3,3,32,32]{4,3,2,1,0:T(8,128)}) custom-call(f32[224,128]{1,0:T(8,128)S(1)} %convert_add_fusion.packed_ref), custom_call_target="tpu_custom_call" | custom-call | flops 1000000000 | bytes 1000000 | tf_op jit(solution)/shard_map/unpack/pallas_call | solution.py:374
  29.5 0.1 collective-permute-done.6.packed_ref
  29.5 1.0 %unpack.3 = (f32[3,3,3,32,32]{4,3,2,1,0:T(8,128)}, f32[3,3,3,32,32]{4,3,2,1,0:T(8,128)}) custom-call(f32[224,128]{1,0:T(8,128)S(1)} %collective-permute-done.6.packed_ref, f32[3,3,3,32,32]{4,3,2,1,0:T(8,128)} %get-tuple-element.39.refs_0_, f32[3,3,3,32,32]{4,3,2,1,0:T(8,128)} %get-tuple-element.40.refs_1_), custom_call_target="tpu_custom_call", output_to_operand_aliasing={{0}: (1, {}), {1}: (2, {})} | custom-call | flops 1000000000 | bytes 1000000 | tf_op jit(solution)/shard_map/unpack/pallas_call | solution.py:374
  (6 shorter events, 0.1 us)
Async XLA Ops:
  2.0 2.0 %collective-permute-start = (bf16[32,6,8,128]{3,2,1,0:T(8,128)(2,1)S(1)}, bf16[32,6,8,128]{3,2,1,0:T(8,128)(2,1)S(1)}, u32[]{:S(2)}, u32[]{:S(2)}) collective-permute-start(bf16[32,6,8,128]{3,2,1,0:T(8,128)(2,1)S(1)} %get-tuple-element.27), channel_id=1, source_target_pairs={{0,16},{16,0},{1,17},{17,1},{2,18},{18,2},{3,19},{19,3},{4,20},{20... | collective-permute-start | bytes 1179656 | tf_op jit(solution)/shard_map/ppermute | solution.py:466
  2.6 1.5 %copy-start = (bf16[1,32,8,8,128]{4,3,2,1,0:T(8,128)(2,1)S(1)}, bf16[1,32,8,8,128]{4,3,2,1,0:T(8,128)(2,1)}, u32[]{:S(2)}) copy-start(bf16[1,32,8,8,128]{4,3,2,1,0:T(8,128)(2,1)} %param.7) | copy-start | bytes 1572868
  10.0 1.4 %collective-permute-start.1 = (f32[224,128]{1,0:T(8,128)S(1)}, f32[224,128]{1,0:T(8,128)S(1)}, u32[]{:S(2)}, u32[]{:S(2)}) collective-permute-start(f32[224,128]{1,0:T(8,128)S(1)} %broadcast_select_fusion), channel_id=1, source_target_pairs={{0,16},{16,0},{1,17},{17,1},{2,18},{18,2},{3,19},{19,3},{4,20},{20... | collective-permute-start | bytes 344072 | tf_op jit(solution)/shard_map/ppermute | solution.py:435
  11.4 4.5 %collective-permute-start.2 = (bf16[224,128]{1,0:T(8,128)(2,1)S(1)}, bf16[224,128]{1,0:T(8,128)(2,1)S(1)}, u32[]{:S(2)}, u32[]{:S(2)}) collective-permute-start(bf16[224,128]{1,0:T(8,128)(2,1)S(1)} %add_convert_fusion.2), channel_id=1, source_target_pairs={{0,17},{1,21},{2,22},{3,18},{4,16},{5,20},{6,23},{7,19},{8,28},{9,... | collective-permute-start | bytes 172040 | tf_op jit(solution)/shard_map/ppermute | solution.py:418
  16.0 4.8 %collective-permute-start.3 = (bf16[224,128]{1,0:T(8,128)(2,1)S(1)}, bf16[224,128]{1,0:T(8,128)(2,1)S(1)}, u32[]{:S(2)}, u32[]{:S(2)}) collective-permute-start(bf16[224,128]{1,0:T(8,128)(2,1)S(1)} %add_convert_fusion.1), channel_id=1, source_target_pairs={{0,24},{1,16},{2,19},{3,27},{4,21},{5,29},{6,30},{7,22},{8,25},{9,... | collective-permute-start | bytes 172040 | tf_op jit(solution)/shard_map/ppermute | solution.py:418
  20.8 3.7 %collective-permute-start.4 = (bf16[224,128]{1,0:T(8,128)(2,1)S(1)}, bf16[224,128]{1,0:T(8,128)(2,1)S(1)}, u32[]{:S(2)}, u32[]{:S(2)}) collective-permute-start(bf16[224,128]{1,0:T(8,128)(2,1)S(1)} %add_convert_fusion), channel_id=1, source_target_pairs={{0,18},{1,25},{2,26},{3,17},{4,28},{5,23},{6,20},{7,31},{8,16},{9,... | collective-permute-start | bytes 172040 | tf_op jit(solution)/shard_map/ppermute | solution.py:418
  24.4 3.7 %collective-permute-start.5 = (bf16[224,128]{1,0:T(8,128)(2,1)S(1)}, bf16[224,128]{1,0:T(8,128)(2,1)S(1)}, u32[]{:S(2)}, u32[]{:S(2)}) collective-permute-start(bf16[224,128]{1,0:T(8,128)(2,1)S(1)} %convert_add_fusion.1), channel_id=1, source_target_pairs={{0,20},{1,19},{2,16},{3,23},{4,22},{5,17},{6,18},{7,21},{8,26},{9,... | collective-permute-start | bytes 172040 | tf_op jit(solution)/shard_map/ppermute | solution.py:418
  28.1 1.4 %collective-permute-start.6 = (f32[224,128]{1,0:T(8,128)S(1)}, f32[224,128]{1,0:T(8,128)S(1)}, u32[]{:S(2)}, u32[]{:S(2)}) collective-permute-start(f32[224,128]{1,0:T(8,128)S(1)} %convert_add_fusion.packed_ref), channel_id=1, source_target_pairs={{0,16},{16,0},{1,17},{17,1},{2,18},{18,2},{3,19},{19,3},{4,20},{20... | collective-permute-start | bytes 344072 | tf_op jit(solution)/shard_map/ppermute | solution.py:438

commit v8 on v7

--- a/solution.py
+++ b/solution.py
@@ -345,6 +345,18 @@
     out_one, out_two, grad_ref, sem = refs[-4:]
     chan = grad_ref.shape[-1]
     value = packed_ref[...].T * factor
+
+    def each(dz, act):
+        def on(out):
+            act(pltpu.make_async_copy(grad_ref.at[dz], out.at[dz], sem.at[dz]))
+
+        if which in (0, 1):
+            on(out_two if which else out_one)
+        else:
+            second = holds_second() == (which == "held")
+            pl.when(second)(lambda: on(out_two))
+            pl.when(jnp.logical_not(second))(lambda: on(out_one))
+
     for dz in range(3):
         for dy in range(3):
             for dx in range(3):
@@ -354,18 +366,9 @@
                 grad_ref[dz, dy, dx] = value[
                     row * chan : (row + 1) * chan, column * chan : (column + 1) * chan
                 ]
-
-    def send(out):
-        copy = pltpu.make_async_copy(grad_ref, out, sem)
-        copy.start()
-        copy.wait()
-
-    if which in (0, 1):
-        send(out_two if which else out_one)
-    else:
-        second = holds_second() == (which == "held")
-        pl.when(second)(lambda: send(out_two))
-        pl.when(jnp.logical_not(second))(lambda: send(out_one))
+        each(dz, lambda copy: copy.start())
+    for dz in range(3):
+        each(dz, lambda copy: copy.wait())
 
 
 def unpacked(packed, which, factor, chan, outs=()):
@@ -376,7 +379,7 @@
         out_shape=[pltpu.HBM(shape, F32)] * 2,
         in_specs=[pl.BlockSpec(memory_space=pltpu.VMEM)] + [hbm] * len(outs),
         out_specs=[hbm] * 2,
-        scratch_shapes=[pltpu.VMEM(shape, F32), pltpu.SemaphoreType.DMA],
+        scratch_shapes=[pltpu.VMEM(shape, F32), pltpu.SemaphoreType.DMA((3,))],
         input_output_aliases={1 + k: k for k in range(len(outs))},
         compiler_params=params(8),
         cost_estimate=cost(1e9, 1e6),

time: 30.7 us -> 30.7 us (level)
  no operation moved by 1% of the time
where the time goes in v8:
time: 30.7 us; the launch traced here: 30.5 us
  Pallas kernels  12.6 us (41%)
  starting transfers between devices  10.1 us (33%)
  waiting for transfers between devices  6.97 us (23%)
  between operations  0.71 us (2%)
    ppermute x4, starting transfers between devices, crossed(): lax.ppermute(sent, ('gz', 'dp'), moves).astype(F32)  8.92 us
    pallas_call x1, Pallas kernels, local(): pl.pallas_call(functools.partial(main_kernel, count, sizes), out_shape=[j...  5.9 us
    ppermute x4, waiting for transfers between devices, crossed(): lax.ppermute(sent, ('gz', 'dp'), moves).astype(F32)  5.8 us
    pallas_call x2, Pallas kernels, unpacked(): pl.pallas_call(functools.partial(unpack_kernel, factor, which), out_shape...  1.92 us
    pallas_call x1, Pallas kernels, finish(): pl.pallas_call(functools.partial(last_kernel, count, sizes), out_shape=ja...  1.92 us
    pallas_call x1, Pallas kernels, local(): pl.pallas_call(functools.partial(prep_kernel, count == 2), out_shape=[jax...  1.47 us
    pallas_call x1, Pallas kernels, gathered(): pl.pallas_call(functools.partial(pack_kernel, count, own), out_shape=[plt...  1.36 us
    ppermute x1, waiting for transfers between devices, reduced(): mine = mine + lax.ppermute(jnp.where(second, one, two), 'gz', swap)  1.07 us
  transfers between devices with their start and end apart: 7, of which 6 were waited for; matrix products, arithmetic and copies ran while one was open for 0% of the time, Pallas kernels for 14%

profile of v8, /device:TPU:0, one launch (start us, length us, event | category | flops | bytes accessed | tf_op | source)
XLA Modules:
  0.0 30.5 jit_solution(14111875155294411172)
XLA Ops:
  0.6 1.4 %pack.1 = (bf16[32,8,8,128]{3,2,1,0:T(8,128)(2,1)S(1)}, bf16[3,3,3,32,32]{4,3,2,1,0:T(8,128)(2,1)S(1)}, bf16[3,3,3,32,32]{4,3,2,1,0:T(8,128)(2,1)S(1)}, bf16[32,6,8,128]{3,2,1,0:T(8,128)(2,1)S(1)}) custom-call(bf16[32,8,8,128]{3,2,1,0:T(8,128)(2,1)} %bitcast.9, bf16[32,8,8,128]{3,2,1,0:T(8,128)(2,1)} %bitcast.7, bf16[3,3,3,32,32]{4,3,2,1,0:T(8,128)(2,1)} %bitcast.10, ...), custom_call_target="tpu_custom_call" | custom-call | tf_op jit(solution)/shard_map/pack/pallas_call | solution.py:454
  2.0 0.6 %collective-permute-start = (bf16[32,6,8,128]{3,2,1,0:T(8,128)(2,1)S(1)}, bf16[32,6,8,128]{3,2,1,0:T(8,128)(2,1)S(1)}, u32[]{:S(2)}, u32[]{:S(2)}) collective-permute-start(bf16[32,6,8,128]{3,2,1,0:T(8,128)(2,1)S(1)} %get-tuple-element.27), channel_id=1, source_target_pairs={{0,16},{16,0},{1,17},{17,1},{2,18},{18,2},{3,19},{19,3},{4,20},{20... | collective-permute-start | bytes 1179656 | tf_op jit(solution)/shard_map/ppermute | solution.py:469
  2.6 0.0 copy-start
  2.6 1.5 %prep.1 = (bf16[2,128,1536]{2,1,0:T(8,128)(2,1)S(1)}, bf16[2,128,1536]{2,1,0:T(8,128)(2,1)S(1)}, bf16[2,128,1536]{2,1,0:T(8,128)(2,1)S(1)}, bf16[2,128,1536]{2,1,0:T(8,128)(2,1)S(1)}, bf16[768,1024]{1,0:T(8,128)(2,1)S(1)}) custom-call(bf16[32,8,8,128]{3,2,1,0:T(8,128)(2,1)S(1)} %get-tuple-element.23.data_ref, ...), custom_call_target="tpu_custom_call" | custom-call | flops 2000000000 | bytes 5000000 | tf_op jit(solution)/shard_map/prep/pallas_call | solution.py:489
  4.0 0.0 collective-permute-done.refs_2_
  4.0 0.0 copy-done
  4.1 5.9 %main.1 = (bf16[768,1280]{1,0:T(8,128)(2,1)S(1)}, f32[224,128]{1,0:T(8,128)S(1)}, f32[224,128]{1,0:T(8,128)S(1)}) custom-call(bf16[768,1024]{1,0:T(8,128)(2,1)S(1)} %get-tuple-element.26.refs_0_, bf16[32,8,8,128]{3,2,1,0:T(8,128)(2,1)S(1)} %bitcast.8, bf16[32,6,8,128]{3,2,1,0:T(8,128)(2,1)S(1)} %collective-permute-done.refs_2_, ...), custom_call_target="tpu_custom_call" | custom-call | flops 8000000000 | bytes 8000000 | tf_op jit(solution)/shard_map/main/pallas_call | solution.py:499
  10.0 0.3 %collective-permute-start.1 = (f32[224,128]{1,0:T(8,128)S(1)}, f32[224,128]{1,0:T(8,128)S(1)}, u32[]{:S(2)}, u32[]{:S(2)}) collective-permute-start(f32[224,128]{1,0:T(8,128)S(1)} %broadcast_select_fusion), channel_id=1, source_target_pairs={{0,16},{16,0},{1,17},{17,1},{2,18},{18,2},{3,19},{19,3},{4,20},{20... | collective-permute-start | bytes 344072 | tf_op jit(solution)/shard_map/ppermute | solution.py:438
  10.3 1.1 %collective-permute-done.1 = f32[224,128]{1,0:T(8,128)S(1)} collective-permute-done((f32[224,128]{1,0:T(8,128)S(1)}, f32[224,128]{1,0:T(8,128)S(1)}, u32[]{:S(2)}, u32[]{:S(2)}) %collective-permute-start.1) | collective-permute-done | bytes 114720 | tf_op jit(solution)/shard_map/ppermute | solution.py:438
  11.4 2.7 %collective-permute-start.2 = (bf16[224,128]{1,0:T(8,128)(2,1)S(1)}, bf16[224,128]{1,0:T(8,128)(2,1)S(1)}, u32[]{:S(2)}, u32[]{:S(2)}) collective-permute-start(bf16[224,128]{1,0:T(8,128)(2,1)S(1)} %add_convert_fusion.2), channel_id=1, source_target_pairs={{0,17},{1,21},{2,22},{3,18},{4,16},{5,20},{6,23},{7,19},{8,28},{9,... | collective-permute-start | bytes 172040 | tf_op jit(solution)/shard_map/ppermute | solution.py:421
  14.1 1.9 %collective-permute-done.2 = bf16[224,128]{1,0:T(8,128)(2,1)S(1)} collective-permute-done((bf16[224,128]{1,0:T(8,128)(2,1)S(1)}, bf16[224,128]{1,0:T(8,128)(2,1)S(1)}, u32[]{:S(2)}, u32[]{:S(2)}) %collective-permute-start.2) | collective-permute-done | bytes 57376 | tf_op jit(solution)/shard_map/ppermute | solution.py:421
  16.0 2.9 %collective-permute-start.3 = (bf16[224,128]{1,0:T(8,128)(2,1)S(1)}, bf16[224,128]{1,0:T(8,128)(2,1)S(1)}, u32[]{:S(2)}, u32[]{:S(2)}) collective-permute-start(bf16[224,128]{1,0:T(8,128)(2,1)S(1)} %add_convert_fusion.1), channel_id=1, source_target_pairs={{0,24},{1,16},{2,19},{3,27},{4,21},{5,29},{6,30},{7,22},{8,25},{9,... | collective-permute-start | bytes 172040 | tf_op jit(solution)/shard_map/ppermute | solution.py:421
  18.9 1.9 %collective-permute-done.3 = bf16[224,128]{1,0:T(8,128)(2,1)S(1)} collective-permute-done((bf16[224,128]{1,0:T(8,128)(2,1)S(1)}, bf16[224,128]{1,0:T(8,128)(2,1)S(1)}, u32[]{:S(2)}, u32[]{:S(2)}) %collective-permute-start.3) | collective-permute-done | bytes 57376 | tf_op jit(solution)/shard_map/ppermute | solution.py:421
  20.8 1.6 %collective-permute-start.4 = (bf16[224,128]{1,0:T(8,128)(2,1)S(1)}, bf16[224,128]{1,0:T(8,128)(2,1)S(1)}, u32[]{:S(2)}, u32[]{:S(2)}) collective-permute-start(bf16[224,128]{1,0:T(8,128)(2,1)S(1)} %add_convert_fusion), channel_id=1, source_target_pairs={{0,18},{1,25},{2,26},{3,17},{4,28},{5,23},{6,20},{7,31},{8,16},{9,... | collective-permute-start | bytes 172040 | tf_op jit(solution)/shard_map/ppermute | solution.py:421
  22.4 2.0 %collective-permute-done.4 = bf16[224,128]{1,0:T(8,128)(2,1)S(1)} collective-permute-done((bf16[224,128]{1,0:T(8,128)(2,1)S(1)}, bf16[224,128]{1,0:T(8,128)(2,1)S(1)}, u32[]{:S(2)}, u32[]{:S(2)}) %collective-permute-start.4) | collective-permute-done | bytes 57376 | tf_op jit(solution)/shard_map/ppermute | solution.py:421
  24.4 1.7 %collective-permute-start.5 = (bf16[224,128]{1,0:T(8,128)(2,1)S(1)}, bf16[224,128]{1,0:T(8,128)(2,1)S(1)}, u32[]{:S(2)}, u32[]{:S(2)}) collective-permute-start(bf16[224,128]{1,0:T(8,128)(2,1)S(1)} %convert_add_fusion.1), channel_id=1, source_target_pairs={{0,20},{1,19},{2,16},{3,23},{4,22},{5,17},{6,18},{7,21},{8,26},{9,... | collective-permute-start | bytes 172040 | tf_op jit(solution)/shard_map/ppermute | solution.py:421
  26.1 1.9 %last.1 = bf16[32,8,8,128]{3,2,1,0:T(8,128)(2,1)} custom-call(bf16[768,1280]{1,0:T(8,128)(2,1)S(1)} %get-tuple-element.35.grad_field_ref, bf16[2,128,1536]{2,1,0:T(8,128)(2,1)S(1)} %get-tuple-element.36.back_one), custom_call_target="tpu_custom_call" | custom-call | flops 2000000000 | bytes 3000000 | tf_op jit(solution)/shard_map/last/pallas_call | solution.py:520
  28.1 0.1 collective-permute-done.5
  28.1 0.3 %collective-permute-start.6 = (f32[224,128]{1,0:T(8,128)S(1)}, f32[224,128]{1,0:T(8,128)S(1)}, u32[]{:S(2)}, u32[]{:S(2)}) collective-permute-start(f32[224,128]{1,0:T(8,128)S(1)} %convert_add_fusion.packed_ref), channel_id=1, source_target_pairs={{0,16},{16,0},{1,17},{17,1},{2,18},{18,2},{3,19},{19,3},{4,20},{20... | collective-permute-start | bytes 344072 | tf_op jit(solution)/shard_map/ppermute | solution.py:441
  28.5 1.0 %unpack.2 = (f32[3,3,3,32,32]{4,3,2,1,0:T(8,128)}, f32[3,3,3,32,32]{4,3,2,1,0:T(8,128)}) custom-call(f32[224,128]{1,0:T(8,128)S(1)} %convert_add_fusion.packed_ref), custom_call_target="tpu_custom_call" | custom-call | flops 1000000000 | bytes 1000000 | tf_op jit(solution)/shard_map/unpack/pallas_call | solution.py:377
  29.4 0.1 collective-permute-done.6.packed_ref
  29.5 1.0 %unpack.3 = (f32[3,3,3,32,32]{4,3,2,1,0:T(8,128)}, f32[3,3,3,32,32]{4,3,2,1,0:T(8,128)}) custom-call(f32[224,128]{1,0:T(8,128)S(1)} %collective-permute-done.6.packed_ref, f32[3,3,3,32,32]{4,3,2,1,0:T(8,128)} %get-tuple-element.39.refs_0_, f32[3,3,3,32,32]{4,3,2,1,0:T(8,128)} %get-tuple-element.40.refs_1_), custom_call_target="tpu_custom_call", output_to_operand_aliasing={{0}: (1, {}), {1}: (2, {})} | custom-call | flops 1000000000 | bytes 1000000 | tf_op jit(solution)/shard_map/unpack/pallas_call | solution.py:377
  (6 shorter events, 0.1 us)
Async XLA Ops:
  2.0 2.0 %collective-permute-start = (bf16[32,6,8,128]{3,2,1,0:T(8,128)(2,1)S(1)}, bf16[32,6,8,128]{3,2,1,0:T(8,128)(2,1)S(1)}, u32[]{:S(2)}, u32[]{:S(2)}) collective-permute-start(bf16[32,6,8,128]{3,2,1,0:T(8,128)(2,1)S(1)} %get-tuple-element.27), channel_id=1, source_target_pairs={{0,16},{16,0},{1,17},{17,1},{2,18},{18,2},{3,19},{19,3},{4,20},{20... | collective-permute-start | bytes 1179656 | tf_op jit(solution)/shard_map/ppermute | solution.py:469
  2.6 1.5 %copy-start = (bf16[1,32,8,8,128]{4,3,2,1,0:T(8,128)(2,1)S(1)}, bf16[1,32,8,8,128]{4,3,2,1,0:T(8,128)(2,1)}, u32[]{:S(2)}) copy-start(bf16[1,32,8,8,128]{4,3,2,1,0:T(8,128)(2,1)} %param.7) | copy-start | bytes 1572868
  10.0 1.4 %collective-permute-start.1 = (f32[224,128]{1,0:T(8,128)S(1)}, f32[224,128]{1,0:T(8,128)S(1)}, u32[]{:S(2)}, u32[]{:S(2)}) collective-permute-start(f32[224,128]{1,0:T(8,128)S(1)} %broadcast_select_fusion), channel_id=1, source_target_pairs={{0,16},{16,0},{1,17},{17,1},{2,18},{18,2},{3,19},{19,3},{4,20},{20... | collective-permute-start | bytes 344072 | tf_op jit(solution)/shard_map/ppermute | solution.py:438
  11.4 4.5 %collective-permute-start.2 = (bf16[224,128]{1,0:T(8,128)(2,1)S(1)}, bf16[224,128]{1,0:T(8,128)(2,1)S(1)}, u32[]{:S(2)}, u32[]{:S(2)}) collective-permute-start(bf16[224,128]{1,0:T(8,128)(2,1)S(1)} %add_convert_fusion.2), channel_id=1, source_target_pairs={{0,17},{1,21},{2,22},{3,18},{4,16},{5,20},{6,23},{7,19},{8,28},{9,... | collective-permute-start | bytes 172040 | tf_op jit(solution)/shard_map/ppermute | solution.py:421
  16.0 4.8 %collective-permute-start.3 = (bf16[224,128]{1,0:T(8,128)(2,1)S(1)}, bf16[224,128]{1,0:T(8,128)(2,1)S(1)}, u32[]{:S(2)}, u32[]{:S(2)}) collective-permute-start(bf16[224,128]{1,0:T(8,128)(2,1)S(1)} %add_convert_fusion.1), channel_id=1, source_target_pairs={{0,24},{1,16},{2,19},{3,27},{4,21},{5,29},{6,30},{7,22},{8,25},{9,... | collective-permute-start | bytes 172040 | tf_op jit(solution)/shard_map/ppermute | solution.py:421
  20.8 3.7 %collective-permute-start.4 = (bf16[224,128]{1,0:T(8,128)(2,1)S(1)}, bf16[224,128]{1,0:T(8,128)(2,1)S(1)}, u32[]{:S(2)}, u32[]{:S(2)}) collective-permute-start(bf16[224,128]{1,0:T(8,128)(2,1)S(1)} %add_convert_fusion), channel_id=1, source_target_pairs={{0,18},{1,25},{2,26},{3,17},{4,28},{5,23},{6,20},{7,31},{8,16},{9,... | collective-permute-start | bytes 172040 | tf_op jit(solution)/shard_map/ppermute | solution.py:421
  24.4 3.7 %collective-permute-start.5 = (bf16[224,128]{1,0:T(8,128)(2,1)S(1)}, bf16[224,128]{1,0:T(8,128)(2,1)S(1)}, u32[]{:S(2)}, u32[]{:S(2)}) collective-permute-start(bf16[224,128]{1,0:T(8,128)(2,1)S(1)} %convert_add_fusion.1), channel_id=1, source_target_pairs={{0,20},{1,19},{2,16},{3,23},{4,22},{5,17},{6,18},{7,21},{8,26},{9,... | collective-permute-start | bytes 172040 | tf_op jit(solution)/shard_map/ppermute | solution.py:421
  28.1 1.4 %collective-permute-start.6 = (f32[224,128]{1,0:T(8,128)S(1)}, f32[224,128]{1,0:T(8,128)S(1)}, u32[]{:S(2)}, u32[]{:S(2)}) collective-permute-start(f32[224,128]{1,0:T(8,128)S(1)} %convert_add_fusion.packed_ref), channel_id=1, source_target_pairs={{0,16},{16,0},{1,17},{17,1},{2,18},{18,2},{3,19},{19,3},{4,20},{20... | collective-permute-start | bytes 344072 | tf_op jit(solution)/shard_map/ppermute | solution.py:441
